TPU v7x, 256 devices: a whole 4x4x8 slice. The times are simulated.
256 devices in a mesh: seq: 64 (over x, y, z_hi), chan: 4 (over z_lo, core).
Axes of the slice: x: 4, y: 4, z: 8 (z_hi: 4, z_lo: 2; z = z_hi * 2 + z_lo), core: 2. Of those that a mesh axis runs over, the one named last changes fastest.
Arguments:
- tokens: bfloat16 [768, 131072], P('chan', 'seq'), may hold values from -7.5 to 7.5
- filter_spectrum: float32 [2, 768, 131072], P(None, 'chan', 'seq'), may hold values from -6 to 6
- skip_weight: float32 [768], P('chan'), may hold values from -1 to 1
- norm_gain: float32 [768], P('chan'), may hold values from 0.5 to 1.5
- mlp_gain: float32 [768], P('chan'), may hold values from 0.5 to 1.5
- mix_in: bfloat16 [4, 36864], P('chan'), may hold values from -0.4375 to 0.4375
- up_weight: bfloat16 [4, 147456], P('chan'), may hold values from -0.4375 to 0.4375
- down_weight: bfloat16 [4, 147456], P('chan'), may hold values from -0.21875 to 0.21875
- mix_out: bfloat16 [4, 36864], P('chan'), may hold values from -0.4375 to 0.4375
Outputs:
- mixed: bfloat16 [768, 131072], P('chan', 'seq')
All inputs are finite; a program needn't handle non-finite values.
Results may differ from a plain program's by a relative error of at most 0.013.
Values may be sent and summed in bfloat16 or wider, within the bound.
No kernel may reach another device: no remote copies, remote signals or barrier semaphores. Data moves between devices by JAX's collectives and lax.ppermute only.
A program may use at most 64 MiB of HBM per device.

v0:
```python
import functools
import math

import jax
import jax.numpy as jnp
from jax import lax
from jax.experimental import pallas as pl
from jax.experimental.pallas import tpu as pltpu
from jax.sharding import PartitionSpec as P

D = 768
CH = 192
HALF = 96
QUART = 24
TOK = 2048
NSEQ = 64
SHARE = 32
LENGTH = TOK * NSEQ
HID = 768
PIECE = 48
CHUNKS = 2
TC = TOK // CHUNKS
F32 = jnp.float32
BF16 = jnp.bfloat16
ROOT_HALF = math.sqrt(0.5)
VMEM_LIMIT = 48 * 1024 * 1024


def vm():
    return pl.BlockSpec(memory_space=pltpu.VMEM)


def sm():
    return pl.BlockSpec(memory_space=pltpu.SMEM)


def call(body, out_shape, n_smem, n_vmem, scratch=(), name=None):
    many = isinstance(out_shape, (tuple, list))
    return pl.pallas_call(
        body,
        out_shape=out_shape,
        in_specs=[sm()] * n_smem + [vm()] * n_vmem,
        out_specs=[vm() for _ in out_shape] if many else vm(),
        scratch_shapes=scratch,
        compiler_params=pltpu.CompilerParams(vmem_limit_bytes=VMEM_LIMIT),
        name=name,
    )


def shape(dims, dtype):
    return jax.ShapeDtypeStruct(dims, dtype)


def lane_group(rows):
    return lax.broadcasted_iota(jnp.int32, (rows, 128), 1)


def regroup(parts):
    rows = parts[0].shape[0]
    lane = lane_group(rows)
    low = lane < 64
    even = (lane // 32) % 2 == 0
    step = list(parts)
    for a, b in ((0, 2), (1, 3)):
        x, y = step[a], step[b]
        step[a] = jnp.where(low, x, pltpu.roll(y, 64, 1))
        step[b] = jnp.where(low, pltpu.roll(x, 64, 1), y)
    for a, b in ((0, 1), (2, 3)):
        x, y = step[a], step[b]
        step[a] = jnp.where(even, x, pltpu.roll(y, 32, 1))
        step[b] = jnp.where(even, pltpu.roll(x, 96, 1), y)
    return step


def sums_kernel(x_ref, out_ref):
    x = x_ref[...].astype(F32)
    out_ref[0:1, :] = jnp.sum(x, axis=0, keepdims=True)
    out_ref[1:2, :] = jnp.sum(x * x, axis=0, keepdims=True)


def table_kernel(alpha_ref, beta_ref, w_ref):
    def rows(b, carry):
        ac = jnp.broadcast_to(alpha_ref[0, pl.ds(b, 1), :], (SHARE, 128))
        as_ = jnp.broadcast_to(alpha_ref[1, pl.ds(b, 1), :], (SHARE, 128))
        start = pl.multiple_of(b * SHARE, SHARE)
        for u in range(8):
            bc = beta_ref[0, :, 128 * u : 128 * (u + 1)]
            bs = beta_ref[1, :, 128 * u : 128 * (u + 1)]
            w_ref[pl.ds(start, SHARE), 256 * u : 256 * u + 128] = (ac * bc - as_ * bs).astype(BF16)
            w_ref[pl.ds(start, SHARE), 256 * u + 128 : 256 * (u + 1)] = (
                -(as_ * bc + ac * bs)
            ).astype(BF16)
        return carry

    lax.fori_loop(0, NSEQ, rows, 0)


def forward_kernel(x_ref, s0, s1, s2, s3, gain_ref, w_ref, send_ref, normed_ref):
    total = s0[...] + s1[...] + s2[...] + s3[...]
    mean = total[0:1, :] / D
    square = total[1:2, :] / D
    scale = lax.rsqrt(square - mean * mean + 1e-05)
    xn = ((x_ref[...].astype(F32) - mean) * scale * gain_ref[...]).astype(BF16)
    normed_ref[...] = xn
    for u in range(8):
        y = jnp.dot(normed_ref[...], w_ref[:, 256 * u : 256 * (u + 1)], preferred_element_type=F32)
        for half in range(2):
            both = []
            for part in range(2):
                both.append(
                    regroup(
                        [
                            y[
                                half * HALF + w * QUART : half * HALF + (w + 1) * QUART,
                                128 * part : 128 * (part + 1),
                            ]
                            for w in range(4)
                        ]
                    )
                )
            for v in range(4):
                q = 4 * u + v
                dest = 63 - q if half else q
                send_ref[dest] = jnp.concatenate([both[0][v], both[1][v]], axis=0).astype(BF16)


def filter_kernel(flags, own_ref, got_ref, ca_ref, cb_ref, g_ref, g1_ref):
    high = flags[0] == 1
    first = flags[1] == 1
    row = lax.broadcasted_iota(jnp.int32, (128, 128), 0)
    lane = lax.broadcasted_iota(jnp.int32, (128, 128), 1)
    mirror = jnp.where((row + lane == 128) & (lane % SHARE != 0), 1.0, 0.0).astype(BF16)
    crow = lax.broadcasted_iota(jnp.int32, (NSEQ, 128), 0)
    clane = lax.broadcasted_iota(jnp.int32, (NSEQ, 128), 1)
    keep = jnp.where(first, 0.0, 1.0)

    def spread(target):
        return jnp.where((clane % SHARE == 0) & (crow == target + clane // SHARE), 1.0, 0.0)

    for part in range(2):
        column = (ca_ref[part].astype(F32) + cb_ref[part].astype(F32)).astype(BF16)
        for t in range(16):
            here = slice(128 * t, 128 * (t + 1))
            there = slice(128 * (15 - t), 128 * (16 - t))
            direct = jnp.where(high, got_ref[part, :, here].astype(F32), own_ref[part, :, here])
            other = jnp.where(
                high, own_ref[part, :, there], got_ref[part, :, there].astype(F32)
            ).astype(BF16)
            crossed = jnp.where(
                (clane % SHARE == 0) & (crow == 63 - 4 * t - clane // SHARE), 1.0, 0.0
            ).astype(BF16)
            mirrored = jnp.dot(other, mirror, preferred_element_type=F32) + keep * jnp.dot(
                column, crossed, preferred_element_type=F32
            )
            both = direct + mirrored if part == 0 else direct - mirrored
            out = regroup([both[w * QUART : (w + 1) * QUART] for w in range(4)])
            for v in range(4):
                g_ref[part, 4 * t + v] = out[v]

    @pl.when(first)
    def _():
        for part in range(2):
            column = (ca_ref[part].astype(F32) + cb_ref[part].astype(F32)).astype(BF16)
            for t in range(16):
                plain = spread(4 * t).astype(BF16)
                both = jnp.dot(column, plain, preferred_element_type=F32)
                out = regroup([both[w * QUART : (w + 1) * QUART] for w in range(4)])
                for v in range(4):
                    g1_ref[part, 4 * t + v] = out[v]


def turn_i(re, im, s):
    return (-im, re) if s > 0 else (im, -re)


def dft4(xr, xi, s):
    ar, ai = xr[0] + xr[2], xi[0] + xi[2]
    br, bi = xr[0] - xr[2], xi[0] - xi[2]
    cr, ci = xr[1] + xr[3], xi[1] + xi[3]
    dr, di = turn_i(xr[1] - xr[3], xi[1] - xi[3], s)
    return [ar + cr, br + dr, ar - cr, br - dr], [ai + ci, bi + di, ai - ci, bi - di]


def dft8(xr, xi, s):
    er, ei = dft4(xr[0::2], xi[0::2], s)
    dr, di = dft4(xr[1::2], xi[1::2], s)
    c = ROOT_HALF
    if s > 0:
        dr1, di1 = c * (dr[1] - di[1]), c * (di[1] + dr[1])
        dr3, di3 = -c * (dr[3] + di[3]), c * (dr[3] - di[3])
    else:
        dr1, di1 = c * (dr[1] + di[1]), c * (di[1] - dr[1])
        dr3, di3 = c * (di[3] - dr[3]), -c * (di[3] + dr[3])
    dr2, di2 = turn_i(dr[2], di[2], s)
    qr = [dr[0], dr1, dr2, dr3]
    qi = [di[0], di1, di2, di3]
    return (
        [er[k] + qr[k] for k in range(4)] + [er[k] - qr[k] for k in range(4)],
        [ei[k] + qi[k] for k in range(4)] + [ei[k] - qi[k] for k in range(4)],
    )


def twiddle(re, im, index, s):
    index %= 64
    if index == 0:
        return re, im
    c = math.cos(2.0 * math.pi * index / 64.0)
    d = s * math.sin(2.0 * math.pi * index / 64.0)
    return re * c - im * d, im * c + re * d


def across(load, store, gains, a_ref, b_ref):
    for p0 in range(8):
        xr, xi = zip(*[load(p0 + 8 * p1) for p1 in range(8)])
        yr, yi = dft8(list(xr), list(xi), -1)
        for g1 in range(8):
            a_ref[0, g1 * 8 + p0], a_ref[1, g1 * 8 + p0] = twiddle(yr[g1], yi[g1], p0 * g1, -1)
    for g1 in range(8):
        yr, yi = dft8(
            [a_ref[0, g1 * 8 + p0] for p0 in range(8)],
            [a_ref[1, g1 * 8 + p0] for p0 in range(8)],
            -1,
        )
        for g2 in range(8):
            hr, hi = gains(g1 + 8 * g2)
            yr[g2], yi[g2] = hr * yr[g2] - hi * yi[g2], hr * yi[g2] + hi * yr[g2]
        zr, zi = dft8(yr, yi, 1)
        for p0 in range(8):
            b_ref[0, p0 * 8 + g1], b_ref[1, p0 * 8 + g1] = twiddle(zr[p0], zi[p0], g1 * p0, 1)
    for p0 in range(8):
        zr, zi = dft8(
            [b_ref[0, p0 * 8 + g1] for g1 in range(8)],
            [b_ref[1, p0 * 8 + g1] for g1 in range(8)],
            1,
        )
        for p1 in range(8):
            store(p0 + 8 * p1, zr[p1], zi[p1])


def middle_kernel(flags, got_ref, g_ref, g1_ref, out_ref, xs, a_ref, b_ref, t1):
    first = flags[1] == 1
    special = (lane_group(8) % SHARE == 0) & first

    def widen(p, carry):
        xs[p] = got_ref[p].astype(F32)
        return carry

    lax.fori_loop(0, NSEQ, widen, 0)

    def half_turn(p):
        return math.cos(2.0 * math.pi * p / 128.0), math.sin(2.0 * math.pi * p / 128.0)

    @pl.when(first)
    def _():
        def alone(i, carry):
            top = pl.ds(pl.multiple_of(i * 8, 8), 8)
            bottom = pl.ds(pl.multiple_of(i * 8 + QUART, 8), 8)

            def load(p):
                c, s = half_turn(p)
                im = jnp.where(special, xs[p, bottom, :], 0.0)
                return im * c, im * (-s)

            def store(p, re, im):
                c, s = half_turn(p)
                t1[p, top, :] = re * c - im * s

            across(load, store, lambda g: (g1_ref[0, g, top, :], g1_ref[1, g, top, :]), a_ref, b_ref)
            return carry

        lax.fori_loop(0, 3, alone, 0)

    def every(i, carry):
        top = pl.ds(pl.multiple_of(i * 8, 8), 8)
        bottom = pl.ds(pl.multiple_of(i * 8 + QUART, 8), 8)

        def load(p):
            return xs[p, top, :], jnp.where(special, 0.0, xs[p, bottom, :])

        def store(p, re, im):
            xs[p, top, :] = re
            xs[p, bottom, :] = jnp.where(special, t1[p, top, :], im)

        across(load, store, lambda g: (g_ref[0, g, top, :], g_ref[1, g, top, :]), a_ref, b_ref)
        return carry

    lax.fori_loop(0, 3, every, 0)

    def narrow(p, carry):
        out_ref[p] = xs[p].astype(BF16)
        return carry

    lax.fori_loop(0, NSEQ, narrow, 0)


def back_kernel(
    flags, got_ref, w_ref, x_ref, normed_ref, skip_ref, gain_ref, gain_row, mix_ref, mix_t_ref,
    res_ref, st_ref, u0, u1, u2, u3, tm,
):
    for half in range(2):
        for u in range(8):
            parts = []
            for v in range(4):
                q = 4 * u + v
                parts.append(got_ref[63 - q if half else q].astype(F32))
            out = regroup(parts)
            for w in range(4):
                low = half * HALF + w * QUART
                tm[low : low + QUART, 256 * u : 256 * u + 128] = out[w][:QUART]
                tm[low : low + QUART, 256 * u + 128 : 256 * (u + 1)] = out[w][QUART:]
    values = tm[...].astype(BF16)
    outs = (u0, u1, u2, u3)
    me = flags[2]
    st_ref[2:3, :] = jnp.zeros((1, TOK), F32)
    st_ref[3:4, :] = jnp.zeros((1, TOK), F32)
    st_ref[2:3, 0:CH] = jnp.dot(
        gain_row[...], mix_ref[...].astype(F32), preferred_element_type=F32,
        precision=lax.Precision.HIGHEST,
    )
    for n in range(8):
        cols = slice(256 * n, 256 * (n + 1))
        conv = lax.dot_general(
            values, w_ref[cols, :], (((1,), (1,)), ((), ())), preferred_element_type=F32
        )
        res = (
            x_ref[:, cols].astype(F32)
            + conv * (1.0 / LENGTH)
            + skip_ref[...] * normed_ref[:, cols].astype(F32)
        ).astype(BF16)
        res_ref[:, cols] = res
        r = res.astype(F32)
        mean = jnp.sum(r, axis=0, keepdims=True) * (1.0 / CH)
        centred = r - mean
        st_ref[0:1, cols] = mean
        st_ref[1:2, cols] = jnp.sum(centred * centred, axis=0, keepdims=True)
        z = (centred * gain_ref[...]).astype(BF16)
        tm[:, cols] = jnp.dot(mix_t_ref[...], z, preferred_element_type=F32)
    for k in range(4):
        rows = pl.ds(pl.multiple_of((me ^ k) * PIECE, PIECE), PIECE)
        outs[k][...] = tm[rows, :].astype(BF16)


def mlp_kernel(
    flags, p0, p1, p2, p3, s0, s1, s2, s3, up_t, down_t, o0, o1, o2, o3, f_ref, low_ref, *, chunk
):
    me = flags[2]
    here = slice(chunk * TC, (chunk + 1) * TC)
    stats = [s[...] for s in (s0, s1, s2, s3)]
    means = [s[0:1, here] for s in stats]
    mean = (means[0] + means[1] + means[2] + means[3]) * 0.25
    spread = sum(s[1:2, here] for s in stats) + CH * sum((m - mean) * (m - mean) for m in means)
    scale = lax.rsqrt(spread * (1.0 / D) + 1e-05)
    row = lax.broadcasted_iota(jnp.int32, (PIECE, CH), 0)
    lane = lax.broadcasted_iota(jnp.int32, (PIECE, CH), 1)
    pick = lane == row + me * PIECE
    for k, p in enumerate((p0, p1, p2, p3)):
        weight = jnp.sum(jnp.where(pick, stats[k][2:3, 0:CH], 0.0), axis=1, keepdims=True)
        value = scale * (p[...].astype(F32) - (mean - means[k]) * weight)
        f_ref[pl.ds(pl.multiple_of((me ^ k) * PIECE, PIECE), PIECE), :] = value
    for n in range(TC // 256):
        cols = slice(256 * n, 256 * (n + 1))
        f = f_ref[:, cols].astype(BF16)
        total = None
        for h in range(3):
            rows = slice(256 * h, 256 * (h + 1))
            wide = jnp.dot(up_t[rows, :], f, preferred_element_type=F32)
            act = (0.5 * wide * (1.0 + lax.erf(wide * ROOT_HALF))).astype(BF16)
            part = jnp.dot(down_t[:, rows], act, preferred_element_type=F32)
            total = part if total is None else total + part
        low_ref[:, cols] = total
    for k, o in enumerate((o0, o1, o2, o3)):
        o[...] = low_ref[pl.ds(pl.multiple_of((me ^ k) * PIECE, PIECE), PIECE), :].astype(BF16)


def final_kernel(flags, *refs):
    pieces = (refs[0:4], refs[4:8])
    res_ref, mix_t_ref, out_ref, f_ref = refs[8:]
    me = flags[2]
    for c in range(CHUNKS):
        here = slice(c * TC, (c + 1) * TC)
        for k in range(4):
            rows = pl.ds(pl.multiple_of((me ^ k) * PIECE, PIECE), PIECE)
            f_ref[rows, here] = pieces[c][k][...].astype(F32)
        for n in range(TC // 256):
            cols = slice(c * TC + 256 * n, c * TC + 256 * (n + 1))
            add = jnp.dot(mix_t_ref[...], f_ref[:, cols].astype(BF16), preferred_element_type=F32)
            out_ref[:, cols] = (res_ref[:, cols].astype(F32) + add).astype(BF16)


def swap(x, k):
    return lax.ppermute(x, "chan", [(i, i ^ k) for i in range(4)])


def shards(
    tokens, filter_spectrum, skip_weight, norm_gain, mlp_gain, mix_in, up_weight, down_weight, mix_out
):
    place = lax.axis_index("seq")
    lane_of = lax.axis_index("chan")
    high = place >= 32
    first = (place == 0) | (place == 63)
    flags = jnp.stack([high, first, lane_of, place]).astype(jnp.int32)
    mine = jnp.where(high, HALF, 0)
    theirs = jnp.where(high, 0, HALF)
    give = lax.dynamic_slice_in_dim(filter_spectrum, theirs, HALF, 1).astype(BF16)
    got = lax.ppermute(give, "seq", [(i, 63 - i) for i in range(64)])
    sums = call(sums_kernel, shape((2, TOK), F32), 0, 1, name="sums")(tokens)
    others = [swap(sums, k) for k in (1, 2, 3)]
    own = lax.dynamic_slice_in_dim(filter_spectrum, mine, HALF, 1)
    pick_row = jnp.arange(TOK, dtype=jnp.int32)[:, None]
    pick_col = jnp.arange(NSEQ, dtype=jnp.int32)[None, :]
    pick = (pick_row == SHARE * pick_col).astype(BF16)
    column = jnp.einsum(
        "pcj,jg->pcg", filter_spectrum.astype(BF16), pick, preferred_element_type=F32
    ).astype(BF16)
    ca = lax.ppermute(column[:, :HALF], "seq", [(32, 0)] + [(64 - i, i) for i in range(1, 32)])
    cb = lax.ppermute(column[:, HALF:], "seq", [(32, 63)] + [(i + 1, i) for i in range(32, 63)])
    freq = jnp.arange(TOK // 2, dtype=jnp.int32)
    step = jnp.arange(SHARE, dtype=jnp.int32)
    angle = (freq[None, :] * (64 * step[:, None] + place) % LENGTH).astype(F32) * (
        2.0 * math.pi / LENGTH
    )
    parity = 1.0 - 2.0 * (step % 2).astype(F32)
    beta = jnp.stack(
        [jnp.cos(angle), jnp.where(freq[None, :] == 0, -parity[:, None], jnp.sin(angle))]
    )
    turn = (
        (jnp.arange(NSEQ, dtype=jnp.int32)[:, None] * (jnp.arange(128, dtype=jnp.int32)[None, :])) % 64
    ).astype(F32) * (2.0 * math.pi / 64)
    alpha = jnp.stack([jnp.cos(turn), jnp.sin(turn)])
    table = call(table_kernel, shape((TOK, TOK), BF16), 0, 2, name="table")(alpha, beta)
    send, normed = call(
        forward_kernel,
        (shape((NSEQ, 2 * QUART, 128), BF16), shape((CH, TOK), BF16)),
        0,
        7,
        name="forward",
    )(tokens, sums, *others, norm_gain[:, None], table)
    moved = lax.all_to_all(send, "seq", split_axis=0, concat_axis=0, tiled=True)
    gains, gains_first = call(
        filter_kernel,
        (shape((2, NSEQ, QUART, 128), F32), shape((2, NSEQ, QUART, 128), F32)),
        1,
        4,
        name="gains",
    )(flags, own, got, ca, cb)
    mix_in_full = mix_in.reshape(CH, CH)
    mix_in_t = mix_in_full.T
    mix_out_t = mix_out.reshape(CH, CH).T
    up_t = up_weight.reshape(CH, HID).T
    down_t = down_weight.reshape(HID, CH).T
    moved, gains, gains_first, mix_in_full, mix_in_t, mix_out_t, up_t, down_t = (
        lax.optimization_barrier(
            (moved, gains, gains_first, mix_in_full, mix_in_t, mix_out_t, up_t, down_t)
        )
    )
    back = call(
        middle_kernel,
        shape((NSEQ, 2 * QUART, 128), BF16),
        1,
        3,
        scratch=[
            pltpu.VMEM((NSEQ, 2 * QUART, 128), F32),
            pltpu.VMEM((2, NSEQ, 8, 128), F32),
            pltpu.VMEM((2, NSEQ, 8, 128), F32),
            pltpu.VMEM((NSEQ, QUART, 128), F32),
        ],
        name="middle",
    )(flags, moved, gains, gains_first)
    home = lax.all_to_all(back, "seq", split_axis=0, concat_axis=0, tiled=True)
    residual, stats, *firsts = call(
        back_kernel,
        (shape((CH, TOK), BF16), shape((4, TOK), F32)) + (shape((PIECE, TOK), BF16),) * 4,
        1,
        9,
        scratch=[pltpu.VMEM((CH, TOK), F32)],
        name="back",
    )(
        flags, home, table, tokens, normed, skip_weight[:, None], mlp_gain[:, None],
        mlp_gain[None, :], mix_in_full, mix_in_t,
    )
    all_stats = [stats] + [swap(stats, k) for k in (1, 2, 3)]
    arrived = []
    for c in range(CHUNKS):
        pieces = [f[:, c * TC : (c + 1) * TC] for f in firsts]
        arrived.append([pieces[0]] + [swap(pieces[k], k) for k in (1, 2, 3)])
    returned = []
    for c in range(CHUNKS):
        lows = call(
            functools.partial(mlp_kernel, chunk=c),
            (shape((PIECE, TC), BF16),) * 4,
            1,
            10,
            scratch=[pltpu.VMEM((CH, TC), F32), pltpu.VMEM((CH, TC), F32)],
            name="mlp",
        )(flags, *arrived[c], *all_stats, up_t, down_t)
        returned.append([lows[0]] + [swap(lows[k], k) for k in (1, 2, 3)])
    return call(
        final_kernel,
        shape((CH, TOK), BF16),
        1,
        10,
        scratch=[pltpu.VMEM((CH, TOK), F32)],
        name="final",
    )(flags, *returned[0], *returned[1], residual, mix_out_t)


def solution(mesh):
    in_specs = (
        P("chan", "seq"),
        P(None, "chan", "seq"),
        P("chan"),
        P("chan"),
        P("chan"),
        P("chan", None),
        P("chan", None),
        P("chan", None),
        P("chan", None),
    )
    out_specs = P("chan", "seq")
    return jax.shard_map(shards, mesh=mesh, in_specs=in_specs, out_specs=out_specs, check_vma=False)
```

profile of v0, /device:TPU:1, one launch (start us, length us, event | category | flops | bytes accessed | tf_op | source)
XLA Modules:
  0.0 179.0 jit_solution(1962239902491449794)
XLA Ops:
  1.3 3.3 %collective-permute-start = (f32[2,2048]{1,0:T(2,128)S(1)}, f32[2,2048]{1,0:T(2,128)S(1)}, u32[]{:S(2)}, u32[]{:S(2)}) collective-permute-start(f32[2,2048]{1,0:T(2,128)S(1)} %sums.1.s0), channel_id=1, source_target_pairs={{0,1},{1,0},{2,3},{3,2},{4,5},{5,4},{6,7},{7,6},{8,9},{9,8},{10,11... | collective-permute-start | bytes 49160 | tf_op jit(solution)/shard_map/ppermute | solution.py:391
  4.6 1.7 collective-permute-start.2
  8.0 6.3 %table.1.w_ref = bf16[2048,2048]{1,0:T(8,128)(2,1)} custom-call(f32[2,64,128]{2,1,0:T(8,128)S(1)} %pad_maximum_fusion.1.alpha_ref, f32[2,32,1024]{2,1,0:T(8,128)S(1)} %pad_maximum_fusion.beta_ref), custom_call_target="tpu_custom_call" | custom-call | tf_op jit(solution)/shard_map/table/pallas_call | solution.py:430
  14.3 6.4 %forward.1 = (bf16[64,48,128]{2,1,0:T(8,128)(2,1)}, bf16[192,2048]{1,0:T(8,128)(2,1)S(1)}) custom-call(bf16[192,2048]{1,0:T(8,128)(2,1)S(1)} %copy-done.1, f32[2,2048]{1,0:T(2,128)S(1)} %sums.1.s0, f32[2,2048]{1,0:T(2,128)S(1)} %collective-permute-done.s1, f32[2,2048]{1,0:T(2,128)S(1)} %collective-permute-done.1.s2, ...), custom_call_target="tpu_custom_call" | custom-call | tf_op jit(solution)/shard_map/forward/pallas_call | solution.py:431
  21.6 12.6 %all-to-all-start = ((bf16[64,48,128]{2,1,0:T(8,128)(2,1)}), bf16[64,48,128]{2,1,0:T(8,128)(2,1)S(1)}, u32[]{:S(2)}, u32[]{:S(2)}) async-start(bf16[64,48,128]{2,1,0:T(8,128)(2,1)} %get-tuple-element.31), calls=%async_computation | async-start | bytes 1572864 | tf_op jit(solution)/shard_map/all_to_all | solution.py:438
  34.2 2.5 %dynamic-slice_convert_fusion = bf16[2,96,2048]{2,1,0:T(8,128)(2,1)} fusion(f32[2,192,2048]{2,1,0:T(8,128)} %param.10, s32[]{:T(128)S(6)} %select_n.72), kind=kLoop, calls=%fused_computation.2 | loop fusion | bytes 1572868 | tf_op jit(solution)/shard_map/convert_element_type | solution.py:404
  36.7 7.7 %collective-permute-start.3 = (bf16[2,96,2048]{2,1,0:T(8,128)(2,1)}, bf16[2,96,2048]{2,1,0:T(8,128)(2,1)}, u32[]{:S(2)}, u32[]{:S(2)}) collective-permute-start(bf16[2,96,2048]{2,1,0:T(8,128)(2,1)} %dynamic-slice_convert_fusion), channel_id=1, source_target_pairs={{0,252},{4,248},{8,244},{12,240},{16,236},{20,232},{24,228},{28,22... | collective-permute-start | bytes 2359304 | tf_op jit(solution)/shard_map/ppermute | solution.py:405
  44.3 2.6 %fusion.2 = bf16[64,2,192]{2,0,1:T(8,128)(2,1)S(1)} fusion(f32[2,192,2048]{2,1,0:T(8,128)} %param.10, s32[64]{0:T(128)S(1)} %iota_multiply_fusion), kind=kOutput, calls=%fused_computation.3 | convolution fusion | flops 101605376 | bytes 3195136 | tf_op jit(solution)/shard_map/pcj,jg->pcg/dot_general | solution.py:412
  50.2 1.5 constant_dynamic-slice_fusion.own_ref
  53.1 7.1 %reduce.3 = bf16[147456]{0:T(1024)(128)(2,1)S(1)} reduce(bf16[1,147456]{1,0:T(2,128)(2,1)} %param.16, bf16[]{:T(256)} %constant.77), dimensions={0}, to_apply=%param.16.reduce_sub_computation | reduce | bytes 589826 | tf_op args[7]
  61.2 1.9 %copy.25 = bf16[768,192]{0,1:T(8,128)(2,1)} copy(bf16[768,192]{1,0:T(8,128)(2,1)} %reshape.254) | data formatting | bytes 589824 | tf_op jit(solution)/shard_map/reshape | solution.py:450
  63.1 7.1 %reduce.2 = bf16[147456]{0:T(1024)(128)(2,1)S(1)} reduce(bf16[1,147456]{1,0:T(2,128)(2,1)} %param.15, bf16[]{:T(256)} %constant.77), dimensions={0}, to_apply=%param.15.reduce_sub_computation | reduce | bytes 589826 | tf_op args[6]
  72.3 1.9 %reduce.1 = bf16[36864]{0:T(1024)(128)(2,1)} reduce(bf16[1,36864]{1,0:T(2,128)(2,1)} %param.17, bf16[]{:T(256)} %constant.77), dimensions={0}, to_apply=%param.17.reduce_sub_computation | reduce | bytes 147458 | tf_op args[8]
  74.3 1.6 reshape.252
  75.9 1.6 copy.23
  77.6 7.0 %collective-permute-done.3.got_ref = bf16[2,96,2048]{2,1,0:T(8,128)(2,1)} collective-permute-done((bf16[2,96,2048]{2,1,0:T(8,128)(2,1)}, bf16[2,96,2048]{2,1,0:T(8,128)(2,1)}, u32[]{:S(2)}, u32[]{:S(2)}) %collective-permute-start.3) | collective-permute-done | bytes 786464 | tf_op jit(solution)/shard_map/ppermute | solution.py:405
  84.5 5.3 %gains.1 = (f32[2,64,24,128]{3,2,1,0:T(8,128)S(1)}, f32[2,64,24,128]{3,2,1,0:T(8,128)S(1)}) custom-call(s32[4]{0:T(128)S(1)} %pad_add_fusion.flags, f32[2,96,2048]{2,1,0:T(8,128)S(1)} %constant_dynamic-slice_fusion.own_ref, bf16[2,96,2048]{2,1,0:T(8,128)(2,1)} %collective-permute-done.3.got_ref, bf16[2,96,64]{2,1,0:T(8,128)(2,1)} %collective-permute-done.4.ca_ref, ...), custom_call_target="tpu_custom_call" | custom-call | tf_op jit(solution)/shard_map/gains/pallas_call | solution.py:439
  94.9 4.8 %middle.1 = bf16[64,48,128]{2,1,0:T(8,128)(2,1)} custom-call(s32[4]{0:T(128)S(1)} %pad_add_fusion.flags, bf16[64,48,128]{2,1,0:T(8,128)(2,1)S(1)} %all-to-all-done.got_ref, f32[2,64,24,128]{3,2,1,0:T(8,128)S(1)} %copy-done.4, f32[2,64,24,128]{3,2,1,0:T(8,128)S(1)} %copy-done.6), custom_call_target="tpu_custom_call" | custom-call | tf_op jit(solution)/shard_map/middle/pallas_call | solution.py:456
  99.8 14.3 %all-to-all-start.1 = ((bf16[64,48,128]{2,1,0:T(8,128)(2,1)}), bf16[64,48,128]{2,1,0:T(8,128)(2,1)S(1)}, u32[]{:S(2)}, u32[]{:S(2)}) async-start(bf16[64,48,128]{2,1,0:T(8,128)(2,1)} %middle.1), calls=%async_computation.1 | async-start | bytes 1572864 | tf_op jit(solution)/shard_map/all_to_all | solution.py:469
  114.3 21.2 %all-to-all-done.1.got_ref = bf16[64,48,128]{2,1,0:T(8,128)(2,1)S(1)} async-done(((bf16[64,48,128]{2,1,0:T(8,128)(2,1)}), bf16[64,48,128]{2,1,0:T(8,128)(2,1)S(1)}, u32[]{:S(2)}, u32[]{:S(2)}) %all-to-all-start.1) | async-done | bytes 786464 | tf_op jit(solution)/shard_map/all_to_all | solution.py:469
  138.5 10.4 %back.1 = (bf16[192,2048]{1,0:T(8,128)(2,1)S(1)}, f32[4,2048]{1,0:T(4,128)S(1)}, bf16[48,2048]{1,0:T(8,128)(2,1)S(1)}, bf16[48,2048]{1,0:T(8,128)(2,1)S(1)}, bf1...) custom-call(s32[4]{0:T(128)S(1)} %pad_add_fusion.flags, bf16[64,48,128]{2,1,0:T(8,128)(2,1)S(1)} %all-to-all-done.1.got_ref, ...), custom_call_target="tpu_custom_call" | custom-call | tf_op jit(solution)/shard_map/back/pallas_call | solution.py:470
  148.9 4.3 %collective-permute-start.10 = (f32[4,2048]{1,0:T(4,128)S(1)}, f32[4,2048]{1,0:T(4,128)S(1)}, u32[]{:S(2)}, u32[]{:S(2)}) collective-permute-start(f32[4,2048]{1,0:T(4,128)S(1)} %get-tuple-element.44.s0), channel_id=1, source_target_pairs={{0,2},{1,3},{2,0},{3,1},{4,6},{5,7},{6,4},{7,5},{8,10},{9,11},{10,... | collective-permute-start | bytes 98312 | tf_op jit(solution)/shard_map/ppermute | solution.py:391
  153.2 2.3 %collective-permute-start.11 = (f32[4,2048]{1,0:T(4,128)S(1)}, f32[4,2048]{1,0:T(4,128)S(1)}, u32[]{:S(2)}, u32[]{:S(2)}) collective-permute-start(f32[4,2048]{1,0:T(4,128)S(1)} %get-tuple-element.44.s0), channel_id=1, source_target_pairs={{0,3},{1,2},{2,1},{3,0},{4,7},{5,6},{6,5},{7,4},{8,11},{9,10},{10,... | collective-permute-start | bytes 98312 | tf_op jit(solution)/shard_map/ppermute | solution.py:391
  156.1 1.7 collective-permute-start.16
  159.9 1.6 collective-permute-start.8
  161.5 1.8 %collective-permute-done.17.p3 = bf16[48,1024]{1,0:T(8,128)(2,1)S(1)} collective-permute-done((bf16[48,1024]{1,0:T(8,128)(2,1)S(1)}, bf16[48,1024]{1,0:T(8,128)(2,1)S(1)}, u32[]{:S(2)}, u32[]{:S(2)}) %collective-permute-start.17) | collective-permute-done | bytes 98336 | tf_op jit(solution)/shard_map/ppermute | solution.py:391
  163.3 2.2 %mlp.3 = (bf16[48,1024]{1,0:T(8,128)(2,1)S(1)}, bf16[48,1024]{1,0:T(8,128)(2,1)S(1)}, bf16[48,1024]{1,0:T(8,128)(2,1)S(1)}, bf16[48,1024]{1,0:T(8,128)(2,1)S(1)}) custom-call(s32[4]{0:T(128)S(1)} %pad_add_fusion.flags, bf16[48,1024]{1,0:T(8,128)(2,1)S(1)} %get-tuple-element.63.p0, bf16[48,1024]{1,0:T(8,128)(2,1)S(1)} %collective-permute-done.15.p1, ...), custom_call_target="tpu_custom_call" | custom-call | tf_op jit(solution)/shard_map/mlp/pallas_call | solution.py:488
  165.7 1.6 collective-permute-start.19
  167.7 2.2 %mlp.2 = (bf16[48,1024]{1,0:T(8,128)(2,1)S(1)}, bf16[48,1024]{1,0:T(8,128)(2,1)S(1)}, bf16[48,1024]{1,0:T(8,128)(2,1)S(1)}, bf16[48,1024]{1,0:T(8,128)(2,1)S(1)}) custom-call(s32[4]{0:T(128)S(1)} %pad_add_fusion.flags, bf16[48,1024]{1,0:T(8,128)(2,1)S(1)} %get-tuple-element.64.p0, bf16[48,1024]{1,0:T(8,128)(2,1)S(1)} %collective-permute-done.6.p1, ...), custom_call_target="tpu_custom_call" | custom-call | tf_op jit(solution)/shard_map/mlp/pallas_call | solution.py:488
  172.7 1.8 %collective-permute-done.13.refs_2_ = bf16[48,1024]{1,0:T(8,128)(2,1)S(1)} collective-permute-done((bf16[48,1024]{1,0:T(8,128)(2,1)S(1)}, bf16[48,1024]{1,0:T(8,128)(2,1)S(1)}, u32[]{:S(2)}, u32[]{:S(2)}) %collective-permute-start.13) | collective-permute-done | bytes 98336 | tf_op jit(solution)/shard_map/ppermute | solution.py:391
  174.5 2.6 %collective-permute-done.14.refs_3_ = bf16[48,1024]{1,0:T(8,128)(2,1)S(1)} collective-permute-done((bf16[48,1024]{1,0:T(8,128)(2,1)S(1)}, bf16[48,1024]{1,0:T(8,128)(2,1)S(1)}, u32[]{:S(2)}, u32[]{:S(2)}) %collective-permute-start.14) | collective-permute-done | bytes 98336 | tf_op jit(solution)/shard_map/ppermute | solution.py:391
  177.1 1.9 %final.1 = bf16[192,2048]{1,0:T(8,128)(2,1)} custom-call(s32[4]{0:T(128)S(1)} %pad_add_fusion.flags, bf16[48,1024]{1,0:T(8,128)(2,1)S(1)} %get-tuple-element.47.refs_0_, bf16[48,1024]{1,0:T(8,128)(2,1)S(1)} %collective-permute-done.12.refs_1_, bf16[48,1024]{1,0:T(8,128)(2,1)S(1)} %collective-permute-done.13.refs_2_, ...), custom_call_target="tpu_custom_call" | custom-call | tf_op jit(solution)/shard_map/final/pallas_call | solution.py:497
  (88 shorter events, 26.0 us)
Async XLA Ops:
  1.3 13.0 %collective-permute-start = (f32[2,2048]{1,0:T(2,128)S(1)}, f32[2,2048]{1,0:T(2,128)S(1)}, u32[]{:S(2)}, u32[]{:S(2)}) collective-permute-start(f32[2,2048]{1,0:T(2,128)S(1)} %sums.1.s0), channel_id=1, source_target_pairs={{0,1},{1,0},{2,3},{3,2},{4,5},{5,4},{6,7},{7,6},{8,9},{9,8},{10,11... | collective-permute-start | bytes 49160 | tf_op jit(solution)/shard_map/ppermute | solution.py:391
  4.6 9.7 %collective-permute-start.1 = (f32[2,2048]{1,0:T(2,128)S(1)}, f32[2,2048]{1,0:T(2,128)S(1)}, u32[]{:S(2)}, u32[]{:S(2)}) collective-permute-start(f32[2,2048]{1,0:T(2,128)S(1)} %sums.1.s0), channel_id=1, source_target_pairs={{0,2},{1,3},{2,0},{3,1},{4,6},{5,7},{6,4},{7,5},{8,10},{9,11},{10,... | collective-permute-start | bytes 49160 | tf_op jit(solution)/shard_map/ppermute | solution.py:391
  4.6 9.7 %collective-permute-start.2 = (f32[2,2048]{1,0:T(2,128)S(1)}, f32[2,2048]{1,0:T(2,128)S(1)}, u32[]{:S(2)}, u32[]{:S(2)}) collective-permute-start(f32[2,2048]{1,0:T(2,128)S(1)} %sums.1.s0), channel_id=1, source_target_pairs={{0,3},{1,2},{2,1},{3,0},{4,7},{5,6},{6,5},{7,4},{8,11},{9,10},{10,... | collective-permute-start | bytes 49160 | tf_op jit(solution)/shard_map/ppermute | solution.py:391
  8.0 6.3 %copy-start.1 = (bf16[192,2048]{1,0:T(8,128)(2,1)S(1)}, bf16[192,2048]{1,0:T(8,128)(2,1)}, u32[]{:S(2)}) copy-start(bf16[192,2048]{1,0:T(8,128)(2,1)} %x_ref.5) | copy-start | bytes 2359300
  21.6 70.5 %all-to-all-start = ((bf16[64,48,128]{2,1,0:T(8,128)(2,1)}), bf16[64,48,128]{2,1,0:T(8,128)(2,1)S(1)}, u32[]{:S(2)}, u32[]{:S(2)}) async-start(bf16[64,48,128]{2,1,0:T(8,128)(2,1)} %get-tuple-element.31), calls=%async_computation | async-start | bytes 1572864 | tf_op jit(solution)/shard_map/all_to_all | solution.py:438
  36.7 47.9 %collective-permute-start.3 = (bf16[2,96,2048]{2,1,0:T(8,128)(2,1)}, bf16[2,96,2048]{2,1,0:T(8,128)(2,1)}, u32[]{:S(2)}, u32[]{:S(2)}) collective-permute-start(bf16[2,96,2048]{2,1,0:T(8,128)(2,1)} %dynamic-slice_convert_fusion), channel_id=1, source_target_pairs={{0,252},{4,248},{8,244},{12,240},{16,236},{20,232},{24,228},{28,22... | collective-permute-start | bytes 2359304 | tf_op jit(solution)/shard_map/ppermute | solution.py:405
  44.3 7.5 %copy-start.14 = (bf16[1,36864]{1,0:T(2,128)(2,1)S(1)}, bf16[1,36864]{1,0:T(2,128)(2,1)}, u32[]{:S(2)}) copy-start(bf16[1,36864]{1,0:T(2,128)(2,1)} %param.14) | copy-start | bytes 221188
  47.7 29.9 %collective-permute-start.4 = (bf16[2,96,64]{2,1,0:T(8,128)(2,1)}, bf16[2,96,64]{2,1,0:T(8,128)(2,1)}, u32[]{:S(2)}, u32[]{:S(2)}) collective-permute-start(bf16[2,96,64]{2,1,0:T(8,128)(2,1)} %get-tuple-element.66), channel_id=1, source_target_pairs={{128,0},{252,4},{248,8},{244,12},{240,16},{236,20},{232,24},{228,2... | collective-permute-start | bytes 73736 | tf_op jit(solution)/shard_map/ppermute | solution.py:415
  48.9 28.6 %collective-permute-start.5 = (bf16[2,96,64]{2,1,0:T(8,128)(2,1)}, bf16[2,96,64]{2,1,0:T(8,128)(2,1)}, u32[]{:S(2)}, u32[]{:S(2)}) collective-permute-start(bf16[2,96,64]{2,1,0:T(8,128)(2,1)} %get-tuple-element.65), channel_id=1, source_target_pairs={{128,252},{132,128},{136,132},{140,136},{144,140},{148,144},{152,1... | collective-permute-start | bytes 73736 | tf_op jit(solution)/shard_map/ppermute | solution.py:416
  52.4 17.8 %copy-start.7 = (bf16[192,192]{1,0:T(8,128)(2,1)}, bf16[192,192]{1,0:T(8,128)(2,1)S(1)}, u32[]{:S(2)}) copy-start(bf16[192,192]{1,0:T(8,128)(2,1)S(1)} %reshape.251.mix_ref) | copy-start | bytes 221188
  92.1 1.4 copy-start.4
  93.5 1.4 copy-start.6
  94.9 19.1 %copy-start.15 = (f32[192]{0:T(256)S(1)}, f32[192]{0:T(256)}, u32[]{:S(2)}) copy-start(f32[192]{0:T(256)} %param.11) | copy-start | bytes 2308
  94.9 19.2 %copy-start.13 = (f32[192]{0:T(256)S(1)}, f32[192]{0:T(256)}, u32[]{:S(2)}) copy-start(f32[192]{0:T(256)} %param.13) | copy-start | bytes 2308
  99.8 35.8 %all-to-all-start.1 = ((bf16[64,48,128]{2,1,0:T(8,128)(2,1)}), bf16[64,48,128]{2,1,0:T(8,128)(2,1)S(1)}, u32[]{:S(2)}, u32[]{:S(2)}) async-start(bf16[64,48,128]{2,1,0:T(8,128)(2,1)} %middle.1), calls=%async_computation.1 | async-start | bytes 1572864 | tf_op jit(solution)/shard_map/all_to_all | solution.py:469
  138.5 24.8 %copy-start.2 = (bf16[768,192]{0,1:T(8,128)(2,1)S(1)}, bf16[768,192]{0,1:T(8,128)(2,1)}, u32[]{:S(2)}) copy-start(bf16[768,192]{0,1:T(8,128)(2,1)} %copy.25) | copy-start | bytes 884740
  148.9 28.2 %copy-start.12 = (bf16[192,192]{0,1:T(8,128)(2,1)S(1)}, bf16[192,192]{0,1:T(8,128)(2,1)}, u32[]{:S(2)}) copy-start(bf16[192,192]{0,1:T(8,128)(2,1)} %copy.23) | copy-start | bytes 221188
  148.9 8.9 %collective-permute-start.10 = (f32[4,2048]{1,0:T(4,128)S(1)}, f32[4,2048]{1,0:T(4,128)S(1)}, u32[]{:S(2)}, u32[]{:S(2)}) collective-permute-start(f32[4,2048]{1,0:T(4,128)S(1)} %get-tuple-element.44.s0), channel_id=1, source_target_pairs={{0,2},{1,3},{2,0},{3,1},{4,6},{5,7},{6,4},{7,5},{8,10},{9,11},{10,... | collective-permute-start | bytes 98312 | tf_op jit(solution)/shard_map/ppermute | solution.py:391
  153.2 6.1 %collective-permute-start.11 = (f32[4,2048]{1,0:T(4,128)S(1)}, f32[4,2048]{1,0:T(4,128)S(1)}, u32[]{:S(2)}, u32[]{:S(2)}) collective-permute-start(f32[4,2048]{1,0:T(4,128)S(1)} %get-tuple-element.44.s0), channel_id=1, source_target_pairs={{0,3},{1,2},{2,1},{3,0},{4,7},{5,6},{6,5},{7,4},{8,11},{9,10},{10,... | collective-permute-start | bytes 98312 | tf_op jit(solution)/shard_map/ppermute | solution.py:391
  155.5 3.9 %collective-permute-start.9 = (f32[4,2048]{1,0:T(4,128)S(1)}, f32[4,2048]{1,0:T(4,128)S(1)}, u32[]{:S(2)}, u32[]{:S(2)}) collective-permute-start(f32[4,2048]{1,0:T(4,128)S(1)} %get-tuple-element.44.s0), channel_id=1, source_target_pairs={{0,1},{1,0},{2,3},{3,2},{4,5},{5,4},{6,7},{7,6},{8,9},{9,8},{10,11... | collective-permute-start | bytes 98312 | tf_op jit(solution)/shard_map/ppermute | solution.py:391
  155.8 4.1 %collective-permute-start.15 = (bf16[48,1024]{1,0:T(8,128)(2,1)S(1)}, bf16[48,1024]{1,0:T(8,128)(2,1)S(1)}, u32[]{:S(2)}, u32[]{:S(2)}) collective-permute-start(bf16[48,1024]{1,0:T(8,128)(2,1)S(1)} %get-tuple-element.61), channel_id=1, source_target_pairs={{0,1},{1,0},{2,3},{3,2},{4,5},{5,4},{6,7},{7,6},{8,9},{9,8},{10,11... | collective-permute-start | bytes 294920 | tf_op jit(solution)/shard_map/ppermute | solution.py:391
  156.1 5.4 %collective-permute-start.16 = (bf16[48,1024]{1,0:T(8,128)(2,1)S(1)}, bf16[48,1024]{1,0:T(8,128)(2,1)S(1)}, u32[]{:S(2)}, u32[]{:S(2)}) collective-permute-start(bf16[48,1024]{1,0:T(8,128)(2,1)S(1)} %get-tuple-element.59), channel_id=1, source_target_pairs={{0,2},{1,3},{2,0},{3,1},{4,6},{5,7},{6,4},{7,5},{8,10},{9,11},{10,... | collective-permute-start | bytes 294920 | tf_op jit(solution)/shard_map/ppermute | solution.py:391
  157.8 5.5 %collective-permute-start.17 = (bf16[48,1024]{1,0:T(8,128)(2,1)S(1)}, bf16[48,1024]{1,0:T(8,128)(2,1)S(1)}, u32[]{:S(2)}, u32[]{:S(2)}) collective-permute-start(bf16[48,1024]{1,0:T(8,128)(2,1)S(1)} %get-tuple-element.57), channel_id=1, source_target_pairs={{0,3},{1,2},{2,1},{3,0},{4,7},{5,6},{6,5},{7,4},{8,11},{9,10},{10,... | collective-permute-start | bytes 294920 | tf_op jit(solution)/shard_map/ppermute | solution.py:391
  159.3 8.0 %collective-permute-start.6 = (bf16[48,1024]{1,0:T(8,128)(2,1)S(1)}, bf16[48,1024]{1,0:T(8,128)(2,1)S(1)}, u32[]{:S(2)}, u32[]{:S(2)}) collective-permute-start(bf16[48,1024]{1,0:T(8,128)(2,1)S(1)} %get-tuple-element.62), channel_id=1, source_target_pairs={{0,1},{1,0},{2,3},{3,2},{4,5},{5,4},{6,7},{7,6},{8,9},{9,8},{10,11... | collective-permute-start | bytes 294920 | tf_op jit(solution)/shard_map/ppermute | solution.py:391
  159.4 8.4 %collective-permute-start.7 = (bf16[48,1024]{1,0:T(8,128)(2,1)S(1)}, bf16[48,1024]{1,0:T(8,128)(2,1)S(1)}, u32[]{:S(2)}, u32[]{:S(2)}) collective-permute-start(bf16[48,1024]{1,0:T(8,128)(2,1)S(1)} %get-tuple-element.60), channel_id=1, source_target_pairs={{0,2},{1,3},{2,0},{3,1},{4,6},{5,7},{6,4},{7,5},{8,10},{9,11},{10,... | collective-permute-start | bytes 294920 | tf_op jit(solution)/shard_map/ppermute | solution.py:391
  159.9 7.8 %collective-permute-start.8 = (bf16[48,1024]{1,0:T(8,128)(2,1)S(1)}, bf16[48,1024]{1,0:T(8,128)(2,1)S(1)}, u32[]{:S(2)}, u32[]{:S(2)}) collective-permute-start(bf16[48,1024]{1,0:T(8,128)(2,1)S(1)} %get-tuple-element.58), channel_id=1, source_target_pairs={{0,3},{1,2},{2,1},{3,0},{4,7},{5,6},{6,5},{7,4},{8,11},{9,10},{10,... | collective-permute-start | bytes 294920 | tf_op jit(solution)/shard_map/ppermute | solution.py:391
  165.5 6.2 %collective-permute-start.18 = (bf16[48,1024]{1,0:T(8,128)(2,1)S(1)}, bf16[48,1024]{1,0:T(8,128)(2,1)S(1)}, u32[]{:S(2)}, u32[]{:S(2)}) collective-permute-start(bf16[48,1024]{1,0:T(8,128)(2,1)S(1)} %get-tuple-element.52), channel_id=1, source_target_pairs={{0,1},{1,0},{2,3},{3,2},{4,5},{5,4},{6,7},{7,6},{8,9},{9,8},{10,11... | collective-permute-start | bytes 294920 | tf_op jit(solution)/shard_map/ppermute | solution.py:391
  165.7 6.5 %collective-permute-start.19 = (bf16[48,1024]{1,0:T(8,128)(2,1)S(1)}, bf16[48,1024]{1,0:T(8,128)(2,1)S(1)}, u32[]{:S(2)}, u32[]{:S(2)}) collective-permute-start(bf16[48,1024]{1,0:T(8,128)(2,1)S(1)} %get-tuple-element.53), channel_id=1, source_target_pairs={{0,2},{1,3},{2,0},{3,1},{4,6},{5,7},{6,4},{7,5},{8,10},{9,11},{10,... | collective-permute-start | bytes 294920 | tf_op jit(solution)/shard_map/ppermute | solution.py:391
  167.3 5.4 %collective-permute-start.20 = (bf16[48,1024]{1,0:T(8,128)(2,1)S(1)}, bf16[48,1024]{1,0:T(8,128)(2,1)S(1)}, u32[]{:S(2)}, u32[]{:S(2)}) collective-permute-start(bf16[48,1024]{1,0:T(8,128)(2,1)S(1)} %get-tuple-element.54), channel_id=1, source_target_pairs={{0,3},{1,2},{2,1},{3,0},{4,7},{5,6},{6,5},{7,4},{8,11},{9,10},{10,... | collective-permute-start | bytes 294920 | tf_op jit(solution)/shard_map/ppermute | solution.py:391
  169.9 2.7 %collective-permute-start.12 = (bf16[48,1024]{1,0:T(8,128)(2,1)S(1)}, bf16[48,1024]{1,0:T(8,128)(2,1)S(1)}, u32[]{:S(2)}, u32[]{:S(2)}) collective-permute-start(bf16[48,1024]{1,0:T(8,128)(2,1)S(1)} %get-tuple-element.48), channel_id=1, source_target_pairs={{0,1},{1,0},{2,3},{3,2},{4,5},{5,4},{6,7},{7,6},{8,9},{9,8},{10,11... | collective-permute-start | bytes 294920 | tf_op jit(solution)/shard_map/ppermute | solution.py:391
  170.3 4.2 %collective-permute-start.13 = (bf16[48,1024]{1,0:T(8,128)(2,1)S(1)}, bf16[48,1024]{1,0:T(8,128)(2,1)S(1)}, u32[]{:S(2)}, u32[]{:S(2)}) collective-permute-start(bf16[48,1024]{1,0:T(8,128)(2,1)S(1)} %get-tuple-element.49), channel_id=1, source_target_pairs={{0,2},{1,3},{2,0},{3,1},{4,6},{5,7},{6,4},{7,5},{8,10},{9,11},{10,... | collective-permute-start | bytes 294920 | tf_op jit(solution)/shard_map/ppermute | solution.py:391
  171.7 5.4 %collective-permute-start.14 = (bf16[48,1024]{1,0:T(8,128)(2,1)S(1)}, bf16[48,1024]{1,0:T(8,128)(2,1)S(1)}, u32[]{:S(2)}, u32[]{:S(2)}) collective-permute-start(bf16[48,1024]{1,0:T(8,128)(2,1)S(1)} %get-tuple-element.50), channel_id=1, source_target_pairs={{0,3},{1,2},{2,1},{3,0},{4,7},{5,6},{6,5},{7,4},{8,11},{9,10},{10,... | collective-permute-start | bytes 294920 | tf_op jit(solution)/shard_map/ppermute | solution.py:391
  (7 other events, 7.3 us)
where the time goes:
time: 180 us; the launch traced here: 179 us
  starting transfers between devices  59 us (33%)
  Pallas kernels  39.6 us (22%)
  waiting for transfers between devices  35 us (19%)
  local copies, waits for them, and re-layouts  25.1 us (14%)
  other arithmetic  17.4 us (10%)
  matrix products  2.57 us (1%)
    ppermute x18, starting transfers between devices, swap(): return lax.ppermute(x, 'chan', [(i, i ^ k) for i in range(4)])  22 us
    all_to_all x1, waiting for transfers between devices, shards(): home = lax.all_to_all(back, 'seq', split_axis=0, concat_axis=0, tiled=True)  21.2 us
    unnamed x4, other arithmetic  16.5 us
    all_to_all x1, starting transfers between devices, shards(): home = lax.all_to_all(back, 'seq', split_axis=0, concat_axis=0, tiled=True)  14.3 us
    all_to_all x1, starting transfers between devices, shards(): moved = lax.all_to_all(send, 'seq', split_axis=0, concat_axis=0, tiled=True)  12.6 us
    pallas_call x1, Pallas kernels, shards(): call(back_kernel, (shape((CH, TOK), BF16), shape((4, TOK), F32)) + (shape...  10.4 us
    unnamed x32, local copies, waits for them, and re-layouts  10.1 us
    ppermute x1, starting transfers between devices, shards(): got = lax.ppermute(give, 'seq', [(i, 63 - i) for i in range(64)])  7.65 us
  transfers between devices with their start and end apart: 23, of which 6 were waited for; matrix products, arithmetic and copies ran while one was open for 20% of the time, Pallas kernels for 9%

commit v1 on v0

--- a/solution.py
+++ b/solution.py
@@ -1,4 +1,3 @@
-import functools
 import math
 
 import jax
@@ -7,6 +6,7 @@
 from jax.experimental import pallas as pl
 from jax.experimental.pallas import tpu as pltpu
 from jax.sharding import PartitionSpec as P
+
 
 D = 768
 CH = 192
@@ -23,7 +23,8 @@
 F32 = jnp.float32
 BF16 = jnp.bfloat16
 ROOT_HALF = math.sqrt(0.5)
-VMEM_LIMIT = 48 * 1024 * 1024
+MIB = 1024 * 1024
+ROWS = 56
 
 
 def vm():
@@ -34,17 +35,26 @@
     return pl.BlockSpec(memory_space=pltpu.SMEM)
 
 
-def call(body, out_shape, n_smem, n_vmem, scratch=(), name=None):
+def hb():
+    return pl.BlockSpec(memory_space=pltpu.HBM)
+
+
+def call(body, out_shape, kinds, scratch=(), mib=14, outs=None):
+    spec = {"s": sm, "v": vm, "h": hb}
     many = isinstance(out_shape, (tuple, list))
+    outs = outs or "v" * (len(out_shape) if many else 1)
     return pl.pallas_call(
         body,
         out_shape=out_shape,
-        in_specs=[sm()] * n_smem + [vm()] * n_vmem,
-        out_specs=[vm() for _ in out_shape] if many else vm(),
+        in_specs=[spec[k]() for k in kinds],
+        out_specs=[spec[k]() for k in outs] if many else spec[outs](),
         scratch_shapes=scratch,
-        compiler_params=pltpu.CompilerParams(vmem_limit_bytes=VMEM_LIMIT),
-        name=name,
-    )
+        compiler_params=pltpu.CompilerParams(vmem_limit_bytes=mib * MIB),
+    )
+
+
+def in_hbm(x):
+    return pltpu.with_memory_space_constraint(x, pltpu.HBM)
 
 
 def shape(dims, dtype):
@@ -72,13 +82,23 @@
     return step
 
 
+def column_of(row_ref):
+    n = row_ref.shape[1]
+    eye = lax.broadcasted_iota(jnp.int32, (n, n), 0) == lax.broadcasted_iota(jnp.int32, (n, n), 1)
+    return jnp.sum(jnp.where(eye, row_ref[...], 0.0), axis=1, keepdims=True)
+
+
 def sums_kernel(x_ref, out_ref):
     x = x_ref[...].astype(F32)
     out_ref[0:1, :] = jnp.sum(x, axis=0, keepdims=True)
     out_ref[1:2, :] = jnp.sum(x * x, axis=0, keepdims=True)
 
 
-def table_kernel(alpha_ref, beta_ref, w_ref):
+def table_kernel(flags, alpha_ref, beta_ref, filter_ref, w_ref, give_ref, held, sem):
+    theirs = pl.multiple_of((1 - flags[0]) * HALF, HALF)
+    fetch = pltpu.make_async_copy(filter_ref.at[:, pl.ds(theirs, HALF), :], held, sem)
+    fetch.start()
+
     def rows(b, carry):
         ac = jnp.broadcast_to(alpha_ref[0, pl.ds(b, 1), :], (SHARE, 128))
         as_ = jnp.broadcast_to(alpha_ref[1, pl.ds(b, 1), :], (SHARE, 128))
@@ -93,6 +113,8 @@
         return carry
 
     lax.fori_loop(0, NSEQ, rows, 0)
+    fetch.wait()
+    give_ref[...] = held[...].astype(BF16)
 
 
 def forward_kernel(x_ref, s0, s1, s2, s3, gain_ref, w_ref, send_ref, normed_ref):
@@ -100,7 +122,7 @@
     mean = total[0:1, :] / D
     square = total[1:2, :] / D
     scale = lax.rsqrt(square - mean * mean + 1e-05)
-    xn = ((x_ref[...].astype(F32) - mean) * scale * gain_ref[...]).astype(BF16)
+    xn = ((x_ref[...].astype(F32) - mean) * scale * column_of(gain_ref)).astype(BF16)
     normed_ref[...] = xn
     for u in range(8):
         y = jnp.dot(normed_ref[...], w_ref[:, 256 * u : 256 * (u + 1)], preferred_element_type=F32)
@@ -124,7 +146,9 @@
                 send_ref[dest] = jnp.concatenate([both[0][v], both[1][v]], axis=0).astype(BF16)
 
 
-def filter_kernel(flags, own_ref, got_ref, ca_ref, cb_ref, g_ref, g1_ref):
+def filter_kernel(
+    flags, own_ref, got_ref, ca_ref, cb_ref, g_out, g1_out, g_ref, g1_ref, sems
+):
     high = flags[0] == 1
     first = flags[1] == 1
     row = lax.broadcasted_iota(jnp.int32, (128, 128), 0)
@@ -156,6 +180,7 @@
             out = regroup([both[w * QUART : (w + 1) * QUART] for w in range(4)])
             for v in range(4):
                 g_ref[part, 4 * t + v] = out[v]
+        pltpu.make_async_copy(g_ref.at[part], g_out.at[part], sems.at[part]).start()
 
     @pl.when(first)
     def _():
@@ -167,6 +192,12 @@
                 out = regroup([both[w * QUART : (w + 1) * QUART] for w in range(4)])
                 for v in range(4):
                     g1_ref[part, 4 * t + v] = out[v]
+        last = pltpu.make_async_copy(g1_ref, g1_out, sems.at[2])
+        last.start()
+        last.wait()
+
+    for part in range(2):
+        pltpu.make_async_copy(g_ref.at[part], g_out.at[part], sems.at[part]).wait()
 
 
 def turn_i(re, im, s):
@@ -237,8 +268,12 @@
             store(p0 + 8 * p1, zr[p1], zi[p1])
 
 
-def middle_kernel(flags, got_ref, g_ref, g1_ref, out_ref, xs, a_ref, b_ref, t1):
+def middle_kernel(
+    flags, got_ref, g_in, g1_in, out_ref, xs, a_ref, b_ref, t1, g_ref, g1_ref, sems
+):
     first = flags[1] == 1
+    gains = pltpu.make_async_copy(g_in, g_ref, sems.at[0])
+    gains.start()
     special = (lane_group(8) % SHARE == 0) & first
 
     def widen(p, carry):
@@ -252,6 +287,10 @@
 
     @pl.when(first)
     def _():
+        fetch = pltpu.make_async_copy(g1_in, g1_ref, sems.at[1])
+        fetch.start()
+        fetch.wait()
+
         def alone(i, carry):
             top = pl.ds(pl.multiple_of(i * 8, 8), 8)
             bottom = pl.ds(pl.multiple_of(i * 8 + QUART, 8), 8)
@@ -270,6 +309,8 @@
 
         lax.fori_loop(0, 3, alone, 0)
 
+    gains.wait()
+
     def every(i, carry):
         top = pl.ds(pl.multiple_of(i * 8, 8), 8)
         bottom = pl.ds(pl.multiple_of(i * 8 + QUART, 8), 8)
@@ -293,10 +334,70 @@
     lax.fori_loop(0, NSEQ, narrow, 0)
 
 
-def back_kernel(
-    flags, got_ref, w_ref, x_ref, normed_ref, skip_ref, gain_ref, gain_row, mix_ref, mix_t_ref,
-    res_ref, st_ref, u0, u1, u2, u3, tm,
-):
+def in_three(x):
+    a = x.astype(BF16)
+    rest = x - a.astype(F32)
+    b = rest.astype(BF16)
+    return [a, b, (rest - b.astype(F32)).astype(BF16)]
+
+
+def tokens_back(
+    flags, values, w_ref, x_ref, normed_ref, skip_row, gain_row, mix_ref, mix_t_ref, res_ref, outs, tm, st,
+    fetches,
+    chunk,
+):
+    me = flags[2]
+    skip = column_of(skip_row)
+    gain = column_of(gain_row)
+    st[...] = jnp.zeros((8, TC), F32)
+    weight = jnp.dot(
+        gain_row[...], mix_ref[...].astype(F32), preferred_element_type=F32,
+        precision=lax.Precision.HIGHEST,
+    )
+    for k, part in enumerate(in_three(weight)[:2]):
+        st[5 + k : 6 + k, 0:CH] = part.astype(F32)
+    for n in range(TC // 256):
+        here = slice(256 * n, 256 * (n + 1))
+        cols = slice(chunk * TC + 256 * n, chunk * TC + 256 * (n + 1))
+        fetches[n].wait()
+        conv = lax.dot_general(
+            values, w_ref[here, :], (((1,), (1,)), ((), ())), preferred_element_type=F32
+        )
+        res = (
+            x_ref[:, cols].astype(F32)
+            + conv * (1.0 / LENGTH)
+            + skip * normed_ref[:, cols].astype(F32)
+        ).astype(BF16)
+        res_ref[:, here] = res
+        r = res.astype(F32)
+        mean = jnp.sum(r, axis=0, keepdims=True) * (1.0 / CH)
+        centred = r - mean
+        for k, part in enumerate(in_three(mean)):
+            st[k : k + 1, here] = part.astype(F32)
+        for k, part in enumerate(in_three(jnp.sum(centred * centred, axis=0, keepdims=True))[:2]):
+            st[3 + k : 4 + k, here] = part.astype(F32)
+        z = (centred * gain).astype(BF16)
+        tm[:, here] = jnp.dot(mix_t_ref[...], z, preferred_element_type=F32)
+    for k in range(4):
+        rows = pl.ds(pl.multiple_of((me ^ k) * PIECE, PIECE), PIECE)
+        outs[k][...] = jnp.concatenate([tm[rows, :], st[...]], axis=0).astype(BF16)
+
+
+def fetch_table(w_hbm, w_ref, sems, chunk):
+    fetches = []
+    for n in range(TC // 256):
+        here = slice(256 * n, 256 * (n + 1))
+        there = slice(chunk * TC + 256 * n, chunk * TC + 256 * (n + 1))
+        fetches.append(pltpu.make_async_copy(w_hbm.at[there, :], w_ref.at[here, :], sems.at[n]))
+        fetches[-1].start()
+    return fetches
+
+
+def back_first_kernel(
+    flags, got_ref, w_hbm, x_ref, normed_ref, skip_row, gain_row, mix_ref, mix_t_ref,
+    values_ref, res_ref, u0, u1, u2, u3, tall, tm, st, w_ref, sems,
+):
+    fetches = fetch_table(w_hbm, w_ref, sems, 0)
     for half in range(2):
         for u in range(8):
             parts = []
@@ -306,57 +407,44 @@
             out = regroup(parts)
             for w in range(4):
                 low = half * HALF + w * QUART
-                tm[low : low + QUART, 256 * u : 256 * u + 128] = out[w][:QUART]
-                tm[low : low + QUART, 256 * u + 128 : 256 * (u + 1)] = out[w][QUART:]
-    values = tm[...].astype(BF16)
-    outs = (u0, u1, u2, u3)
+                tall[low : low + QUART, 256 * u : 256 * u + 128] = out[w][:QUART]
+                tall[low : low + QUART, 256 * u + 128 : 256 * (u + 1)] = out[w][QUART:]
+    values = tall[...].astype(BF16)
+    values_ref[...] = values
+    tokens_back(
+        flags, values_ref[...], w_ref, x_ref, normed_ref, skip_row, gain_row, mix_ref, mix_t_ref, res_ref,
+        (u0, u1, u2, u3), tm, st, fetches, 0,
+    )
+
+
+def back_second_kernel(
+    flags, values_ref, w_hbm, x_ref, normed_ref, skip_row, gain_row, mix_ref, mix_t_ref,
+    res_ref, u0, u1, u2, u3, tm, st, w_ref, sems,
+):
+    fetches = fetch_table(w_hbm, w_ref, sems, 1)
+    tokens_back(
+        flags, values_ref[...], w_ref, x_ref, normed_ref, skip_row, gain_row, mix_ref, mix_t_ref, res_ref,
+        (u0, u1, u2, u3), tm, st, fetches, 1,
+    )
+
+
+def mlp_kernel(flags, p0, p1, p2, p3, up_t, down_t, o0, o1, o2, o3, f_ref, low_ref):
     me = flags[2]
-    st_ref[2:3, :] = jnp.zeros((1, TOK), F32)
-    st_ref[3:4, :] = jnp.zeros((1, TOK), F32)
-    st_ref[2:3, 0:CH] = jnp.dot(
-        gain_row[...], mix_ref[...].astype(F32), preferred_element_type=F32,
-        precision=lax.Precision.HIGHEST,
-    )
-    for n in range(8):
-        cols = slice(256 * n, 256 * (n + 1))
-        conv = lax.dot_general(
-            values, w_ref[cols, :], (((1,), (1,)), ((), ())), preferred_element_type=F32
-        )
-        res = (
-            x_ref[:, cols].astype(F32)
-            + conv * (1.0 / LENGTH)
-            + skip_ref[...] * normed_ref[:, cols].astype(F32)
-        ).astype(BF16)
-        res_ref[:, cols] = res
-        r = res.astype(F32)
-        mean = jnp.sum(r, axis=0, keepdims=True) * (1.0 / CH)
-        centred = r - mean
-        st_ref[0:1, cols] = mean
-        st_ref[1:2, cols] = jnp.sum(centred * centred, axis=0, keepdims=True)
-        z = (centred * gain_ref[...]).astype(BF16)
-        tm[:, cols] = jnp.dot(mix_t_ref[...], z, preferred_element_type=F32)
-    for k in range(4):
-        rows = pl.ds(pl.multiple_of((me ^ k) * PIECE, PIECE), PIECE)
-        outs[k][...] = tm[rows, :].astype(BF16)
-
-
-def mlp_kernel(
-    flags, p0, p1, p2, p3, s0, s1, s2, s3, up_t, down_t, o0, o1, o2, o3, f_ref, low_ref, *, chunk
-):
-    me = flags[2]
-    here = slice(chunk * TC, (chunk + 1) * TC)
-    stats = [s[...] for s in (s0, s1, s2, s3)]
-    means = [s[0:1, here] for s in stats]
+    values = [p[...].astype(F32) for p in (p0, p1, p2, p3)]
+    tails = [x[PIECE:ROWS] for x in values]
+    means = [t[0:1] + t[1:2] + t[2:3] for t in tails]
     mean = (means[0] + means[1] + means[2] + means[3]) * 0.25
-    spread = sum(s[1:2, here] for s in stats) + CH * sum((m - mean) * (m - mean) for m in means)
+    spread = sum(t[3:4] + t[4:5] for t in tails) + CH * sum((m - mean) * (m - mean) for m in means)
     scale = lax.rsqrt(spread * (1.0 / D) + 1e-05)
     row = lax.broadcasted_iota(jnp.int32, (PIECE, CH), 0)
     lane = lax.broadcasted_iota(jnp.int32, (PIECE, CH), 1)
     pick = lane == row + me * PIECE
-    for k, p in enumerate((p0, p1, p2, p3)):
-        weight = jnp.sum(jnp.where(pick, stats[k][2:3, 0:CH], 0.0), axis=1, keepdims=True)
-        value = scale * (p[...].astype(F32) - (mean - means[k]) * weight)
-        f_ref[pl.ds(pl.multiple_of((me ^ k) * PIECE, PIECE), PIECE), :] = value
+    for k in range(4):
+        line = tails[k][5:6, 0:CH] + tails[k][6:7, 0:CH]
+        weight = jnp.sum(jnp.where(pick, line, 0.0), axis=1, keepdims=True)
+        f_ref[pl.ds(pl.multiple_of((me ^ k) * PIECE, PIECE), PIECE), :] = scale * (
+            values[k][:PIECE] - (mean - means[k]) * weight
+        )
     for n in range(TC // 256):
         cols = slice(256 * n, 256 * (n + 1))
         f = f_ref[:, cols].astype(BF16)
@@ -372,19 +460,68 @@
         o[...] = low_ref[pl.ds(pl.multiple_of((me ^ k) * PIECE, PIECE), PIECE), :].astype(BF16)
 
 
-def final_kernel(flags, *refs):
-    pieces = (refs[0:4], refs[4:8])
-    res_ref, mix_t_ref, out_ref, f_ref = refs[8:]
+def weights_kernel(
+    mix_in_ref, up_ref, down_ref, mix_out_ref, in_ref, in_t, up_t, down_t, out_t, square, wide, tall
+):
+    def unroll(src, dst, rows, cols):
+        def step(i, carry):
+            for k in range(8):
+                row = i * 8 + k
+                start = pl.multiple_of(row * cols, 128)
+                dst[pl.ds(row, 1), :] = src[:, pl.ds(start, cols)].astype(F32)
+            return carry
+
+        lax.fori_loop(0, rows // 8, step, 0)
+
+    unroll(up_ref, wide, CH, HID)
+    up_t[...] = wide[...].T.astype(BF16)
+    for src, dst in ((mix_in_ref, in_t), (mix_out_ref, out_t)):
+        paired(src, square, CH)
+        if dst is in_t:
+            in_ref[...] = square[...].astype(BF16)
+        dst[...] = square[...].T.astype(BF16)
+    paired(down_ref, tall, HID)
+    down_t[...] = tall[...].T.astype(BF16)
+
+
+def paired(src, dst, rows):
+    def step(i, carry):
+        for k in range(4):
+            row = i * 8 + 2 * k
+            start = pl.multiple_of(row * CH, 128)
+            both = src[:, pl.ds(start, 2 * CH)].astype(F32)
+            dst[pl.ds(row, 1), :] = both[:, :CH]
+            dst[pl.ds(row + 1, 1), :] = both[:, CH:]
+        return carry
+
+    lax.fori_loop(0, rows // 8, step, 0)
+
+
+def tokens_out(flags, pieces, res_ref, mix_t_ref, f_ref, store):
     me = flags[2]
-    for c in range(CHUNKS):
-        here = slice(c * TC, (c + 1) * TC)
-        for k in range(4):
-            rows = pl.ds(pl.multiple_of((me ^ k) * PIECE, PIECE), PIECE)
-            f_ref[rows, here] = pieces[c][k][...].astype(F32)
-        for n in range(TC // 256):
-            cols = slice(c * TC + 256 * n, c * TC + 256 * (n + 1))
-            add = jnp.dot(mix_t_ref[...], f_ref[:, cols].astype(BF16), preferred_element_type=F32)
-            out_ref[:, cols] = (res_ref[:, cols].astype(F32) + add).astype(BF16)
+    for k in range(4):
+        rows = pl.ds(pl.multiple_of((me ^ k) * PIECE, PIECE), PIECE)
+        f_ref[rows, :] = pieces[k][...].astype(F32)
+    for n in range(TC // 256):
+        cols = slice(256 * n, 256 * (n + 1))
+        add = jnp.dot(mix_t_ref[...], f_ref[:, cols].astype(BF16), preferred_element_type=F32)
+        store(cols, (res_ref[:, cols].astype(F32) + add).astype(BF16))
+
+
+def final_first_kernel(flags, p0, p1, p2, p3, res_ref, mix_t_ref, out_ref, f_ref):
+    def store(cols, x):
+        out_ref[:, cols] = x
+
+    tokens_out(flags, (p0, p1, p2, p3), res_ref, mix_t_ref, f_ref, store)
+
+
+def final_second_kernel(flags, p0, p1, p2, p3, res_ref, mix_t_ref, early_ref, out_ref, f_ref):
+    out_ref[:, 0:TC] = early_ref[...]
+
+    def store(cols, x):
+        out_ref[:, cols.start + TC : cols.stop + TC] = x
+
+    tokens_out(flags, (p0, p1, p2, p3), res_ref, mix_t_ref, f_ref, store)
 
 
 def swap(x, k):
@@ -392,6 +529,15 @@
 
 
 def shards(
+    tokens, filter_spectrum, skip_weight, norm_gain, mlp_gain, mix_in, up_weight, down_weight, mix_out
+):
+    return block(
+        tokens, filter_spectrum, skip_weight[None], norm_gain[None], mlp_gain[None], mix_in,
+        up_weight, down_weight, mix_out,
+    )
+
+
+def block(
     tokens, filter_spectrum, skip_weight, norm_gain, mlp_gain, mix_in, up_weight, down_weight, mix_out
 ):
     place = lax.axis_index("seq")
@@ -400,11 +546,10 @@
     first = (place == 0) | (place == 63)
     flags = jnp.stack([high, first, lane_of, place]).astype(jnp.int32)
     mine = jnp.where(high, HALF, 0)
-    theirs = jnp.where(high, 0, HALF)
-    give = lax.dynamic_slice_in_dim(filter_spectrum, theirs, HALF, 1).astype(BF16)
-    got = lax.ppermute(give, "seq", [(i, 63 - i) for i in range(64)])
-    sums = call(sums_kernel, shape((2, TOK), F32), 0, 1, name="sums")(tokens)
-    others = [swap(sums, k) for k in (1, 2, 3)]
+    sums = call(sums_kernel, shape((2, TOK), F32), "v")(tokens)
+    others = []
+    for k in (1, 2, 3):
+        others.append(swap(sums, k))
     own = lax.dynamic_slice_in_dim(filter_spectrum, mine, HALF, 1)
     pick_row = jnp.arange(TOK, dtype=jnp.int32)[:, None]
     pick_col = jnp.arange(NSEQ, dtype=jnp.int32)[None, :]
@@ -427,81 +572,91 @@
         (jnp.arange(NSEQ, dtype=jnp.int32)[:, None] * (jnp.arange(128, dtype=jnp.int32)[None, :])) % 64
     ).astype(F32) * (2.0 * math.pi / 64)
     alpha = jnp.stack([jnp.cos(turn), jnp.sin(turn)])
-    table = call(table_kernel, shape((TOK, TOK), BF16), 0, 2, name="table")(alpha, beta)
+    table, give = call(
+        table_kernel, (shape((TOK, TOK), BF16), shape((2, HALF, TOK), BF16)), "svvh",
+        scratch=[pltpu.VMEM((2, HALF, TOK), F32), pltpu.SemaphoreType.DMA(())],
+    )(flags, alpha, beta, in_hbm(filter_spectrum))
+    got = lax.ppermute(give, "seq", [(i, 63 - i) for i in range(64)])
     send, normed = call(
         forward_kernel,
         (shape((NSEQ, 2 * QUART, 128), BF16), shape((CH, TOK), BF16)),
-        0,
-        7,
-        name="forward",
-    )(tokens, sums, *others, norm_gain[:, None], table)
+        "v" * 7,
+        mib=20,
+    )(tokens, sums, *others, norm_gain, table)
     moved = lax.all_to_all(send, "seq", split_axis=0, concat_axis=0, tiled=True)
     gains, gains_first = call(
         filter_kernel,
-        (shape((2, NSEQ, QUART, 128), F32), shape((2, NSEQ, QUART, 128), F32)),
-        1,
-        4,
-        name="gains",
+        (pltpu.HBM((2, NSEQ, QUART, 128), F32), pltpu.HBM((2, NSEQ, QUART, 128), F32)),
+        "svvvv",
+        scratch=[
+            pltpu.VMEM((2, NSEQ, QUART, 128), F32),
+            pltpu.VMEM((2, NSEQ, QUART, 128), F32),
+            pltpu.SemaphoreType.DMA((3,)),
+        ],
+        outs="hh",
     )(flags, own, got, ca, cb)
-    mix_in_full = mix_in.reshape(CH, CH)
-    mix_in_t = mix_in_full.T
-    mix_out_t = mix_out.reshape(CH, CH).T
-    up_t = up_weight.reshape(CH, HID).T
-    down_t = down_weight.reshape(HID, CH).T
-    moved, gains, gains_first, mix_in_full, mix_in_t, mix_out_t, up_t, down_t = (
-        lax.optimization_barrier(
-            (moved, gains, gains_first, mix_in_full, mix_in_t, mix_out_t, up_t, down_t)
-        )
+    mix_in_full, mix_in_t, up_t, down_t, mix_out_t = call(
+        weights_kernel,
+        (
+            shape((CH, CH), BF16), shape((CH, CH), BF16), shape((HID, CH), BF16),
+            shape((CH, HID), BF16), shape((CH, CH), BF16),
+        ),
+        "vvvv",
+        scratch=[pltpu.VMEM((CH, CH), F32), pltpu.VMEM((CH, HID), F32), pltpu.VMEM((HID, CH), F32)],
+    )(mix_in, up_weight, down_weight, mix_out)
+    moved, mix_in_full, mix_in_t, down_t, up_t, mix_out_t = lax.optimization_barrier(
+        (moved, mix_in_full, mix_in_t, down_t, up_t, mix_out_t)
     )
     back = call(
         middle_kernel,
         shape((NSEQ, 2 * QUART, 128), BF16),
-        1,
-        3,
+        "svhh",
         scratch=[
             pltpu.VMEM((NSEQ, 2 * QUART, 128), F32),
             pltpu.VMEM((2, NSEQ, 8, 128), F32),
             pltpu.VMEM((2, NSEQ, 8, 128), F32),
             pltpu.VMEM((NSEQ, QUART, 128), F32),
+            pltpu.VMEM((2, NSEQ, QUART, 128), F32),
+            pltpu.VMEM((2, NSEQ, QUART, 128), F32),
+            pltpu.SemaphoreType.DMA((2,)),
         ],
-        name="middle",
-    )(flags, moved, gains, gains_first)
+    )(flags, moved, in_hbm(gains), in_hbm(gains_first))
     home = lax.all_to_all(back, "seq", split_axis=0, concat_axis=0, tiled=True)
-    residual, stats, *firsts = call(
-        back_kernel,
-        (shape((CH, TOK), BF16), shape((4, TOK), F32)) + (shape((PIECE, TOK), BF16),) * 4,
-        1,
-        9,
-        scratch=[pltpu.VMEM((CH, TOK), F32)],
-        name="back",
-    )(
-        flags, home, table, tokens, normed, skip_weight[:, None], mlp_gain[:, None],
-        mlp_gain[None, :], mix_in_full, mix_in_t,
-    )
-    all_stats = [stats] + [swap(stats, k) for k in (1, 2, 3)]
-    arrived = []
-    for c in range(CHUNKS):
-        pieces = [f[:, c * TC : (c + 1) * TC] for f in firsts]
-        arrived.append([pieces[0]] + [swap(pieces[k], k) for k in (1, 2, 3)])
-    returned = []
-    for c in range(CHUNKS):
+    piece = (shape((CH, TC), BF16),) + (shape((ROWS, TC), BF16),) * 4
+    small = [
+        pltpu.VMEM((CH, TC), F32),
+        pltpu.VMEM((8, TC), F32),
+        pltpu.VMEM((TC, TOK), BF16),
+        pltpu.SemaphoreType.DMA((TC // 256,)),
+    ]
+    rest = (in_hbm(table), tokens, normed, skip_weight, mlp_gain, mix_in_full, mix_in_t)
+    values, res_a, *first_a = call(
+        back_first_kernel, (shape((CH, TOK), BF16),) + piece, "svhvvvvvv",
+        scratch=[pltpu.VMEM((CH, TOK), F32)] + small, mib=20,
+    )(flags, home, *rest)
+    arrived_a = [first_a[0]] + [swap(first_a[k], k) for k in (1, 2, 3)]
+    res_b, *first_b = call(
+        back_second_kernel, piece, "svhvvvvvv", scratch=small, mib=20
+    )(flags, values, *rest)
+    arrived_b = [first_b[0]] + [swap(first_b[k], k) for k in (1, 2, 3)]
+
+    def mlp(arrived):
         lows = call(
-            functools.partial(mlp_kernel, chunk=c),
+            mlp_kernel,
             (shape((PIECE, TC), BF16),) * 4,
-            1,
-            10,
+            "s" + "v" * 6,
             scratch=[pltpu.VMEM((CH, TC), F32), pltpu.VMEM((CH, TC), F32)],
-            name="mlp",
-        )(flags, *arrived[c], *all_stats, up_t, down_t)
-        returned.append([lows[0]] + [swap(lows[k], k) for k in (1, 2, 3)])
+        )(flags, *arrived, up_t, down_t)
+        return [lows[0]] + [swap(lows[k], k) for k in (1, 2, 3)]
+
+    back_home_a = mlp(arrived_a)
+    back_home_b = mlp(arrived_b)
+    early = call(
+        final_first_kernel, shape((CH, TC), BF16), "s" + "v" * 6, scratch=[pltpu.VMEM((CH, TC), F32)],
+    )(flags, *back_home_a, res_a, mix_out_t)
     return call(
-        final_kernel,
-        shape((CH, TOK), BF16),
-        1,
-        10,
-        scratch=[pltpu.VMEM((CH, TOK), F32)],
-        name="final",
-    )(flags, *returned[0], *returned[1], residual, mix_out_t)
+        final_second_kernel, shape((CH, TOK), BF16), "s" + "v" * 7, scratch=[pltpu.VMEM((CH, TC), F32)],
+    )(flags, *back_home_b, res_b, mix_out_t, early)
 
 
 def solution(mesh):

time: 180 us -> 164 us (0.911)
  blocking collectives: 0 us -> 37.7 us
  local copies, waits for them, and re-layouts: 25.1 us -> 3.03 us
  starting transfers between devices: 59 us -> 38.6 us
  other arithmetic: 17.4 us -> 0.87 us
  Pallas kernels: 39.6 us -> 51.8 us
  waiting for transfers between devices: 35 us -> 29 us
    all_to_all x0 -> x1, blocking collectives: none -> 37.7 us  [block(): home = lax.all_to_all(back, 'seq', split_axis=0, concat_axis=0, tiled=True)]
    all_to_all x2 -> x1, waiting for transfers between devices: 21.2 us -> 0.01 us  [block(): moved = lax.all_to_all(send, 'seq', split_axis=0, concat_axis=0, tiled=True)]
    ppermute x3, waiting for transfers between devices: 6.96 us -> 23.9 us  [the longest x1 23.9 us: block(): got = lax.ppermute(give, 'seq', [(i, 63 - i) for i in range(64)])]
    unnamed x4 -> x0, other arithmetic: 16.5 us -> none
    all_to_all x2 -> x1, starting transfers between devices: 26.8 us -> 12.7 us  [block(): moved = lax.all_to_all(send, 'seq', split_axis=0, concat_axis=0, tiled=True)]
    pallas_call x9 -> x12, Pallas kernels: 39.6 us -> 51.8 us  [the longest x1 12.3 us: block(): call(weights_kernel, (shape((CH, CH), BF16), shape((CH, CH), BF16), shape...]
    reshape x8 -> x0, local copies, waits for them, and re-layouts: 9.19 us -> none  [the longest x2 3.27 us: shards(): mix_out_t = mix_out.reshape(CH, CH).T]
    unnamed x32 -> x20, local copies, waits for them, and re-layouts: 10.1 us -> 1.28 us
  transfers between devices with their start and end apart: 23 -> 19, of which waited for: 6 -> 4; matrix products, arithmetic and copies ran while one was open for 20% -> 3% of each run, Pallas kernels for 9% -> 21%
where the time goes in v1:
time: 164 us
  Pallas kernels  51.8 us (32%)
  starting transfers between devices  38.6 us (24%)
  blocking collectives  37.7 us (23%)
  waiting for transfers between devices  29 us (18%)
  local copies, waits for them, and re-layouts  3.03 us (2%)
  matrix products  2.53 us (2%)
    all_to_all x1, blocking collectives, block(): home = lax.all_to_all(back, 'seq', split_axis=0, concat_axis=0, tiled=True)  37.7 us
    ppermute x1, waiting for transfers between devices, block(): got = lax.ppermute(give, 'seq', [(i, 63 - i) for i in range(64)])  23.9 us
    ppermute x15, starting transfers between devices, swap(): return lax.ppermute(x, 'chan', [(i, i ^ k) for i in range(4)])  16.2 us
    all_to_all x1, starting transfers between devices, block(): moved = lax.all_to_all(send, 'seq', split_axis=0, concat_axis=0, tiled=True)  12.7 us
    pallas_call x1, Pallas kernels, block(): call(weights_kernel, (shape((CH, CH), BF16), shape((CH, CH), BF16), shape...  12.3 us
    ppermute x1, starting transfers between devices, block(): got = lax.ppermute(give, 'seq', [(i, 63 - i) for i in range(64)])  7.74 us
    pallas_call x1, Pallas kernels, block(): call(back_first_kernel, (shape((CH, TOK), BF16),) + piece, 'svhvvvvvv', s...  6.79 us
    pallas_call x1, Pallas kernels, block(): call(filter_kernel, (pltpu.HBM((2, NSEQ, QUART, 128), F32), pltpu.HBM((2,...  6.45 us
  transfers between devices with their start and end apart: 19, of which 4 were waited for; matrix products, arithmetic and copies ran while one was open for 3% of the time, Pallas kernels for 21%

profile of v1, /device:TPU:1, one launch (start us, length us, event | category | flops | bytes accessed | tf_op | source)
XLA Modules:
  0.0 163.8 jit_solution(1038373831206883485)
XLA Ops:
  0.0 1.1 copy-done.1
  1.3 3.1 %collective-permute-start.2 = (f32[2,2048]{1,0:T(2,128)S(1)}, f32[2,2048]{1,0:T(2,128)S(1)}, u32[]{:S(2)}, u32[]{:S(2)}) collective-permute-start(f32[2,2048]{1,0:T(2,128)S(1)} %shard_map.91.s0), channel_id=1, source_target_pairs={{0,3},{1,2},{2,1},{3,0},{4,7},{5,6},{6,5},{7,4},{8,11},{9,10},{10,... | collective-permute-start | bytes 49160 | tf_op jit(solution)/shard_map/ppermute | solution.py:528
  4.4 1.5 collective-permute-start.1
  6.2 0.6 fusion.14
  6.9 4.5 %shard_map.92 = (bf16[2048,2048]{1,0:T(8,128)(2,1)S(1)}, bf16[2,96,2048]{2,1,0:T(8,128)(2,1)}) custom-call(s32[4]{0:T(128)S(1)} %pad_add_fusion.flags, f32[2,64,128]{2,1,0:T(8,128)S(1)} %pad_maximum_fusion.1.alpha_ref, f32[2,32,1024]{2,1,0:T(8,128)S(1)} %pad_maximum_fusion.beta_ref, f32[2,192,2048]{2,1,0:T(8,128)} %filter_ref.1), custom_call_target="tpu_custom_call" | custom-call | tf_op jit(solution)/shard_map/pallas_call | solution.py:575
  11.4 3.4 %shard_map.93 = (bf16[64,48,128]{2,1,0:T(8,128)(2,1)}, bf16[192,2048]{1,0:T(8,128)(2,1)S(1)}) custom-call(bf16[192,2048]{1,0:T(8,128)(2,1)S(1)} %copy-done.2, f32[2,2048]{1,0:T(2,128)S(1)} %shard_map.91.s0, f32[2,2048]{1,0:T(2,128)S(1)} %collective-permute-done.s1, f32[2,2048]{1,0:T(2,128)S(1)} %collective-permute-done.1.s2, ...), custom_call_target="tpu_custom_call" | custom-call | tf_op jit(solution)/shard_map/pallas_call | solution.py:580
  14.9 12.7 %all-to-all-start = ((bf16[64,48,128]{2,1,0:T(8,128)(2,1)}), bf16[64,48,128]{2,1,0:T(8,128)(2,1)S(1)}, u32[]{:S(2)}, u32[]{:S(2)}) async-start(bf16[64,48,128]{2,1,0:T(8,128)(2,1)} %get-tuple-element.42), calls=%async_computation | async-start | bytes 1572864 | tf_op jit(solution)/shard_map/all_to_all | solution.py:586
  27.6 7.7 %collective-permute-start.3 = (bf16[2,96,2048]{2,1,0:T(8,128)(2,1)}, bf16[2,96,2048]{2,1,0:T(8,128)(2,1)}, u32[]{:S(2)}, u32[]{:S(2)}) collective-permute-start(bf16[2,96,2048]{2,1,0:T(8,128)(2,1)} %get-tuple-element.49), channel_id=1, source_target_pairs={{0,252},{4,248},{8,244},{12,240},{16,236},{20,232},{24,228},{28,22... | collective-permute-start | bytes 2359304 | tf_op jit(solution)/shard_map/ppermute | solution.py:579
  35.3 2.5 %fusion.2 = bf16[64,2,192]{2,0,1:T(8,128)(2,1)S(1)} fusion(f32[2,192,2048]{2,1,0:T(8,128)} %filter_ref.1, s32[64]{0:T(128)S(1)} %iota_multiply_fusion), kind=kOutput, calls=%fused_computation.2 | convolution fusion | flops 101605376 | bytes 3195136 | tf_op jit(solution)/shard_map/pcj,jg->pcg/dot_general | solution.py:557
  38.0 0.7 collective-permute-start.5
  38.6 1.3 collective-permute-start.4
  40.0 1.6 constant_dynamic-slice_fusion.own_ref
  41.7 12.3 %shard_map.94 = (bf16[192,192]{1,0:T(8,128)(2,1)S(1)}, bf16[192,192]{1,0:T(8,128)(2,1)S(1)}, bf16[768,192]{1,0:T(8,128)(2,1)S(1)}, bf16[192,768]{1,0:T(8,128)(2,1)S(1)}, bf16[192,192]{1,0:T(8,128)(2,1)S(1)}) custom-call(bf16[1,36864]{1,0:T(2,128)(2,1)S(1)} %copy-done.5, bf16[1,147456]{1,0:T(2,128)(2,1)S(1)} %copy-done.3, bf16[1,147456]{1,0:T(2,128)(2,1)S(1)} %copy-done.4, ...), custom_call_target="tpu_custom_call" | custom-call | tf_op jit(solution)/shard_map/pallas_call | solution.py:598
  54.0 23.9 %collective-permute-done.3.got_ref = bf16[2,96,2048]{2,1,0:T(8,128)(2,1)} collective-permute-done((bf16[2,96,2048]{2,1,0:T(8,128)(2,1)}, bf16[2,96,2048]{2,1,0:T(8,128)(2,1)}, u32[]{:S(2)}, u32[]{:S(2)}) %collective-permute-start.3) | collective-permute-done | bytes 786464 | tf_op jit(solution)/shard_map/ppermute | solution.py:579
  77.9 6.4 %shard_map.95 = (f32[2,64,24,128]{3,2,1,0:T(8,128)}, f32[2,64,24,128]{3,2,1,0:T(8,128)}) custom-call(s32[4]{0:T(128)S(1)} %pad_add_fusion.flags, f32[2,96,2048]{2,1,0:T(8,128)S(1)} %constant_dynamic-slice_fusion.own_ref, bf16[2,96,2048]{2,1,0:T(8,128)(2,1)} %collective-permute-done.3.got_ref, bf16[2,96,64]{2,1,0:T(8,128)(2,1)S(1)} %collective-permute-done.4.ca_ref, ...), custom_call_target="tpu_custom_call" | custom-call | tf_op jit(solution)/shard_map/pallas_call | solution.py:587
  84.4 5.5 %shard_map.96 = bf16[64,48,128]{2,1,0:T(8,128)(2,1)S(1)} custom-call(s32[4]{0:T(128)S(1)} %pad_add_fusion.flags, bf16[64,48,128]{2,1,0:T(8,128)(2,1)S(1)} %all-to-all-done.got_ref, f32[2,64,24,128]{3,2,1,0:T(8,128)} %get-tuple-element.50.g_in, f32[2,64,24,128]{3,2,1,0:T(8,128)} %get-tuple-element.51.g1_in), custom_call_target="tpu_custom_call" | custom-call | tf_op jit(solution)/shard_map/pallas_call | solution.py:610
  89.9 37.7 %all_to_all.10.got_ref = bf16[64,48,128]{2,1,0:T(8,128)(2,1)S(1)} all-to-all(bf16[64,48,128]{2,1,0:T(8,128)(2,1)S(1)} %shard_map.96), channel_id=1, replica_groups=mesh['seq'=64,'chan'=4] {'seq'}, dimensions={0} | all-to-all | bytes 1572864 | tf_op jit(solution)/shard_map/all_to_all | solution.py:624
  127.6 6.8 %shard_map.97 = (bf16[192,2048]{1,0:T(8,128)(2,1)S(1)}, bf16[192,1024]{1,0:T(8,128)(2,1)S(1)}, bf16[56,1024]{1,0:T(8,128)(2,1)S(1)}, bf16[56,1024]{1,0:T(8,128)(...) custom-call(s32[4]{0:T(128)S(1)} %pad_add_fusion.flags, ...), custom_call_target="tpu_custom_call" | custom-call | tf_op jit(solution)/shard_map/pallas_call | solution.py:633
  134.4 3.2 %collective-permute-start.12 = (bf16[56,1024]{1,0:T(8,128)(2,1)S(1)}, bf16[56,1024]{1,0:T(8,128)(2,1)S(1)}, u32[]{:S(2)}, u32[]{:S(2)}) collective-permute-start(bf16[56,1024]{1,0:T(8,128)(2,1)S(1)} %get-tuple-element.69), channel_id=1, source_target_pairs={{0,1},{1,0},{2,3},{3,2},{4,5},{5,4},{6,7},{7,6},{8,9},{9,8},{10,11... | collective-permute-start | bytes 344072 | tf_op jit(solution)/shard_map/ppermute | solution.py:528
  137.6 1.7 %collective-permute-start.14 = (bf16[56,1024]{1,0:T(8,128)(2,1)S(1)}, bf16[56,1024]{1,0:T(8,128)(2,1)S(1)}, u32[]{:S(2)}, u32[]{:S(2)}) collective-permute-start(bf16[56,1024]{1,0:T(8,128)(2,1)S(1)} %get-tuple-element.71), channel_id=1, source_target_pairs={{0,3},{1,2},{2,1},{3,0},{4,7},{5,6},{6,5},{7,4},{8,11},{9,10},{10,... | collective-permute-start | bytes 344072 | tf_op jit(solution)/shard_map/ppermute | solution.py:528
  139.3 5.7 %shard_map.98 = (bf16[192,1024]{1,0:T(8,128)(2,1)S(1)}, bf16[56,1024]{1,0:T(8,128)(2,1)S(1)}, bf16[56,1024]{1,0:T(8,128)(2,1)S(1)}, bf16[56,1024]{1,0:T(8,128)(2,1)S(1)}, bf16[56,1024]{1,0:T(8,128)(2,1)S(1)}) custom-call(s32[4]{0:T(128)S(1)} %pad_add_fusion.flags, bf16[192,2048]{1,0:T(8,128)(2,1)S(1)} %get-tuple-element.55.values_ref, ...), custom_call_target="tpu_custom_call" | custom-call | tf_op jit(solution)/shard_map/pallas_call | solution.py:638
  145.1 0.2 collective-permute-start.6
  145.3 2.0 %collective-permute-start.8 = (bf16[56,1024]{1,0:T(8,128)(2,1)S(1)}, bf16[56,1024]{1,0:T(8,128)(2,1)S(1)}, u32[]{:S(2)}, u32[]{:S(2)}) collective-permute-start(bf16[56,1024]{1,0:T(8,128)(2,1)S(1)} %get-tuple-element.59), channel_id=1, source_target_pairs={{0,3},{1,2},{2,1},{3,0},{4,7},{5,6},{6,5},{7,4},{8,11},{9,10},{10,... | collective-permute-start | bytes 344072 | tf_op jit(solution)/shard_map/ppermute | solution.py:528
  147.3 2.2 %shard_map.100 = (bf16[48,1024]{1,0:T(8,128)(2,1)S(1)}, bf16[48,1024]{1,0:T(8,128)(2,1)S(1)}, bf16[48,1024]{1,0:T(8,128)(2,1)S(1)}, bf16[48,1024]{1,0:T(8,128)(2,1)S(1)}) custom-call(s32[4]{0:T(128)S(1)} %pad_add_fusion.flags, bf16[56,1024]{1,0:T(8,128)(2,1)S(1)} %get-tuple-element.68.p0, bf16[56,1024]{1,0:T(8,128)(2,1)S(1)} %collective-permute-done.12.p1, ...), custom_call_target="tpu_custom_call" | custom-call | tf_op jit(solution)/shard_map/pallas_call | solution.py:644
  149.7 2.0 %collective-permute-start.17 = (bf16[48,1024]{1,0:T(8,128)(2,1)S(1)}, bf16[48,1024]{1,0:T(8,128)(2,1)S(1)}, u32[]{:S(2)}, u32[]{:S(2)}) collective-permute-start(bf16[48,1024]{1,0:T(8,128)(2,1)S(1)} %get-tuple-element.75), channel_id=1, source_target_pairs={{0,3},{1,2},{2,1},{3,0},{4,7},{5,6},{6,5},{7,4},{8,11},{9,10},{10,... | collective-permute-start | bytes 294920 | tf_op jit(solution)/shard_map/ppermute | solution.py:528
  151.7 1.4 collective-permute-done.8.p3
  153.1 2.2 %shard_map.99 = (bf16[48,1024]{1,0:T(8,128)(2,1)S(1)}, bf16[48,1024]{1,0:T(8,128)(2,1)S(1)}, bf16[48,1024]{1,0:T(8,128)(2,1)S(1)}, bf16[48,1024]{1,0:T(8,128)(2,1)S(1)}) custom-call(s32[4]{0:T(128)S(1)} %pad_add_fusion.flags, bf16[56,1024]{1,0:T(8,128)(2,1)S(1)} %get-tuple-element.56.p0, bf16[56,1024]{1,0:T(8,128)(2,1)S(1)} %collective-permute-done.6.p1, ...), custom_call_target="tpu_custom_call" | custom-call | tf_op jit(solution)/shard_map/pallas_call | solution.py:644
  155.5 2.0 %collective-permute-start.11 = (bf16[48,1024]{1,0:T(8,128)(2,1)S(1)}, bf16[48,1024]{1,0:T(8,128)(2,1)S(1)}, u32[]{:S(2)}, u32[]{:S(2)}) collective-permute-start(bf16[48,1024]{1,0:T(8,128)(2,1)S(1)} %get-tuple-element.65), channel_id=1, source_target_pairs={{0,3},{1,2},{2,1},{3,0},{4,7},{5,6},{6,5},{7,4},{8,11},{9,10},{10,... | collective-permute-start | bytes 294920 | tf_op jit(solution)/shard_map/ppermute | solution.py:528
  157.5 0.9 shard_map.101.early_ref
  158.4 1.0 collective-permute-done.10.p2
  159.4 2.7 %collective-permute-done.11.p3 = bf16[48,1024]{1,0:T(8,128)(2,1)S(1)} collective-permute-done((bf16[48,1024]{1,0:T(8,128)(2,1)S(1)}, bf16[48,1024]{1,0:T(8,128)(2,1)S(1)}, u32[]{:S(2)}, u32[]{:S(2)}) %collective-permute-start.11) | collective-permute-done | bytes 98336 | tf_op jit(solution)/shard_map/ppermute | solution.py:528
  162.1 1.7 %shard_map.102 = bf16[192,2048]{1,0:T(8,128)(2,1)} custom-call(s32[4]{0:T(128)S(1)} %pad_add_fusion.flags, bf16[48,1024]{1,0:T(8,128)(2,1)S(1)} %get-tuple-element.62.p0, bf16[48,1024]{1,0:T(8,128)(2,1)S(1)} %collective-permute-done.9.p1, bf16[48,1024]{1,0:T(8,128)(2,1)S(1)} %collective-permute-done.10.p2, bf16[48,1024]{1,0:T(8,128)(2,1)S(1)} %collective-permute-done.11.p3, ...), custom_call_target="tpu_custom_call" | custom-call | tf_op jit(solution)/shard_map/pallas_call | solution.py:657
  (52 shorter events, 1.2 us)
Async XLA Ops:
  0.0 1.1 copy-start.1
  1.3 10.1 %collective-permute-start.2 = (f32[2,2048]{1,0:T(2,128)S(1)}, f32[2,2048]{1,0:T(2,128)S(1)}, u32[]{:S(2)}, u32[]{:S(2)}) collective-permute-start(f32[2,2048]{1,0:T(2,128)S(1)} %shard_map.91.s0), channel_id=1, source_target_pairs={{0,3},{1,2},{2,1},{3,0},{4,7},{5,6},{6,5},{7,4},{8,11},{9,10},{10,... | collective-permute-start | bytes 49160 | tf_op jit(solution)/shard_map/ppermute | solution.py:528
  4.4 7.0 %collective-permute-start.1 = (f32[2,2048]{1,0:T(2,128)S(1)}, f32[2,2048]{1,0:T(2,128)S(1)}, u32[]{:S(2)}, u32[]{:S(2)}) collective-permute-start(f32[2,2048]{1,0:T(2,128)S(1)} %shard_map.91.s0), channel_id=1, source_target_pairs={{0,2},{1,3},{2,0},{3,1},{4,6},{5,7},{6,4},{7,5},{8,10},{9,11},{10,... | collective-permute-start | bytes 49160 | tf_op jit(solution)/shard_map/ppermute | solution.py:528
  5.9 5.5 %collective-permute-start = (f32[2,2048]{1,0:T(2,128)S(1)}, f32[2,2048]{1,0:T(2,128)S(1)}, u32[]{:S(2)}, u32[]{:S(2)}) collective-permute-start(f32[2,2048]{1,0:T(2,128)S(1)} %shard_map.91.s0), channel_id=1, source_target_pairs={{0,1},{1,0},{2,3},{3,2},{4,5},{5,4},{6,7},{7,6},{8,9},{9,8},{10,11... | collective-permute-start | bytes 49160 | tf_op jit(solution)/shard_map/ppermute | solution.py:528
  6.9 4.6 %copy-start.2 = (bf16[192,2048]{1,0:T(8,128)(2,1)S(1)}, bf16[192,2048]{1,0:T(8,128)(2,1)}, u32[]{:S(2)}) copy-start(bf16[192,2048]{1,0:T(8,128)(2,1)} %x_ref.7) | copy-start | bytes 2359300
  6.9 4.6 %copy-start.9 = (f32[192]{0:T(256)S(1)}, f32[192]{0:T(256)}, u32[]{:S(2)}) copy-start(f32[192]{0:T(256)} %param.12) | copy-start | bytes 2308
  11.4 3.5 %copy-start = (bf16[2048,2048]{1,0:T(8,128)(2,1)}, bf16[2048,2048]{1,0:T(8,128)(2,1)S(1)}, u32[]{:S(2)}) copy-start(bf16[2048,2048]{1,0:T(8,128)(2,1)S(1)} %get-tuple-element.41.w_ref.w_hbm) | copy-start | bytes 25165828
  14.9 69.5 %all-to-all-start = ((bf16[64,48,128]{2,1,0:T(8,128)(2,1)}), bf16[64,48,128]{2,1,0:T(8,128)(2,1)S(1)}, u32[]{:S(2)}, u32[]{:S(2)}) async-start(bf16[64,48,128]{2,1,0:T(8,128)(2,1)} %get-tuple-element.42), calls=%async_computation | async-start | bytes 1572864 | tf_op jit(solution)/shard_map/all_to_all | solution.py:586
  27.6 50.3 %collective-permute-start.3 = (bf16[2,96,2048]{2,1,0:T(8,128)(2,1)}, bf16[2,96,2048]{2,1,0:T(8,128)(2,1)}, u32[]{:S(2)}, u32[]{:S(2)}) collective-permute-start(bf16[2,96,2048]{2,1,0:T(8,128)(2,1)} %get-tuple-element.49), channel_id=1, source_target_pairs={{0,252},{4,248},{8,244},{12,240},{16,236},{20,232},{24,228},{28,22... | collective-permute-start | bytes 2359304 | tf_op jit(solution)/shard_map/ppermute | solution.py:579
  38.0 16.0 %collective-permute-start.5 = (bf16[2,96,64]{2,1,0:T(8,128)(2,1)S(1)}, bf16[2,96,64]{2,1,0:T(8,128)(2,1)S(1)}, u32[]{:S(2)}, u32[]{:S(2)}) collective-permute-start(bf16[2,96,64]{2,1,0:T(8,128)(2,1)S(1)} %get-tuple-element.77), channel_id=1, source_target_pairs={{128,252},{132,128},{136,132},{140,136},{144,140},{148,144},{152,1... | collective-permute-start | bytes 73736 | tf_op jit(solution)/shard_map/ppermute | solution.py:561
  38.6 15.4 %collective-permute-start.4 = (bf16[2,96,64]{2,1,0:T(8,128)(2,1)S(1)}, bf16[2,96,64]{2,1,0:T(8,128)(2,1)S(1)}, u32[]{:S(2)}, u32[]{:S(2)}) collective-permute-start(bf16[2,96,64]{2,1,0:T(8,128)(2,1)S(1)} %get-tuple-element.78), channel_id=1, source_target_pairs={{128,0},{252,4},{248,8},{244,12},{240,16},{236,20},{232,24},{228,2... | collective-permute-start | bytes 73736 | tf_op jit(solution)/shard_map/ppermute | solution.py:560
  39.9 1.7 %copy-start.3 = (bf16[1,147456]{1,0:T(2,128)(2,1)S(1)}, bf16[1,147456]{1,0:T(2,128)(2,1)}, u32[]{:S(2)}) copy-start(bf16[1,147456]{1,0:T(2,128)(2,1)} %up_ref.1) | copy-start | bytes 884740
  40.0 1.7 %copy-start.4 = (bf16[1,147456]{1,0:T(2,128)(2,1)S(1)}, bf16[1,147456]{1,0:T(2,128)(2,1)}, u32[]{:S(2)}) copy-start(bf16[1,147456]{1,0:T(2,128)(2,1)} %down_ref.1) | copy-start | bytes 884740
  40.0 1.7 %copy-start.5 = (bf16[1,36864]{1,0:T(2,128)(2,1)S(1)}, bf16[1,36864]{1,0:T(2,128)(2,1)}, u32[]{:S(2)}) copy-start(bf16[1,36864]{1,0:T(2,128)(2,1)} %mix_in_ref.1) | copy-start | bytes 221188
  40.0 1.8 %copy-start.6 = (bf16[1,36864]{1,0:T(2,128)(2,1)S(1)}, bf16[1,36864]{1,0:T(2,128)(2,1)}, u32[]{:S(2)}) copy-start(bf16[1,36864]{1,0:T(2,128)(2,1)} %mix_out_ref.1) | copy-start | bytes 221188
  89.9 37.7 %copy-start.7 = (f32[192]{0:T(256)S(1)}, f32[192]{0:T(256)}, u32[]{:S(2)}) copy-start(f32[192]{0:T(256)} %param.11) | copy-start | bytes 2308
  89.9 37.7 %copy-start.8 = (f32[192]{0:T(256)S(1)}, f32[192]{0:T(256)}, u32[]{:S(2)}) copy-start(f32[192]{0:T(256)} %param.13) | copy-start | bytes 2308
  134.4 10.9 %collective-permute-start.12 = (bf16[56,1024]{1,0:T(8,128)(2,1)S(1)}, bf16[56,1024]{1,0:T(8,128)(2,1)S(1)}, u32[]{:S(2)}, u32[]{:S(2)}) collective-permute-start(bf16[56,1024]{1,0:T(8,128)(2,1)S(1)} %get-tuple-element.69), channel_id=1, source_target_pairs={{0,1},{1,0},{2,3},{3,2},{4,5},{5,4},{6,7},{7,6},{8,9},{9,8},{10,11... | collective-permute-start | bytes 344072 | tf_op jit(solution)/shard_map/ppermute | solution.py:528
  137.6 9.7 %collective-permute-start.13 = (bf16[56,1024]{1,0:T(8,128)(2,1)S(1)}, bf16[56,1024]{1,0:T(8,128)(2,1)S(1)}, u32[]{:S(2)}, u32[]{:S(2)}) collective-permute-start(bf16[56,1024]{1,0:T(8,128)(2,1)S(1)} %get-tuple-element.70), channel_id=1, source_target_pairs={{0,2},{1,3},{2,0},{3,1},{4,6},{5,7},{6,4},{7,5},{8,10},{9,11},{10,... | collective-permute-start | bytes 344072 | tf_op jit(solution)/shard_map/ppermute | solution.py:528
  137.6 9.7 %collective-permute-start.14 = (bf16[56,1024]{1,0:T(8,128)(2,1)S(1)}, bf16[56,1024]{1,0:T(8,128)(2,1)S(1)}, u32[]{:S(2)}, u32[]{:S(2)}) collective-permute-start(bf16[56,1024]{1,0:T(8,128)(2,1)S(1)} %get-tuple-element.71), channel_id=1, source_target_pairs={{0,3},{1,2},{2,1},{3,0},{4,7},{5,6},{6,5},{7,4},{8,11},{9,10},{10,... | collective-permute-start | bytes 344072 | tf_op jit(solution)/shard_map/ppermute | solution.py:528
  145.1 4.7 %collective-permute-start.6 = (bf16[56,1024]{1,0:T(8,128)(2,1)S(1)}, bf16[56,1024]{1,0:T(8,128)(2,1)S(1)}, u32[]{:S(2)}, u32[]{:S(2)}) collective-permute-start(bf16[56,1024]{1,0:T(8,128)(2,1)S(1)} %get-tuple-element.57), channel_id=1, source_target_pairs={{0,1},{1,0},{2,3},{3,2},{4,5},{5,4},{6,7},{7,6},{8,9},{9,8},{10,11... | collective-permute-start | bytes 344072 | tf_op jit(solution)/shard_map/ppermute | solution.py:528
  145.3 6.5 %collective-permute-start.7 = (bf16[56,1024]{1,0:T(8,128)(2,1)S(1)}, bf16[56,1024]{1,0:T(8,128)(2,1)S(1)}, u32[]{:S(2)}, u32[]{:S(2)}) collective-permute-start(bf16[56,1024]{1,0:T(8,128)(2,1)S(1)} %get-tuple-element.58), channel_id=1, source_target_pairs={{0,2},{1,3},{2,0},{3,1},{4,6},{5,7},{6,4},{7,5},{8,10},{9,11},{10,... | collective-permute-start | bytes 344072 | tf_op jit(solution)/shard_map/ppermute | solution.py:528
  145.3 7.8 %collective-permute-start.8 = (bf16[56,1024]{1,0:T(8,128)(2,1)S(1)}, bf16[56,1024]{1,0:T(8,128)(2,1)S(1)}, u32[]{:S(2)}, u32[]{:S(2)}) collective-permute-start(bf16[56,1024]{1,0:T(8,128)(2,1)S(1)} %get-tuple-element.59), channel_id=1, source_target_pairs={{0,3},{1,2},{2,1},{3,0},{4,7},{5,6},{6,5},{7,4},{8,11},{9,10},{10,... | collective-permute-start | bytes 344072 | tf_op jit(solution)/shard_map/ppermute | solution.py:528
  149.5 6.0 %collective-permute-start.15 = (bf16[48,1024]{1,0:T(8,128)(2,1)S(1)}, bf16[48,1024]{1,0:T(8,128)(2,1)S(1)}, u32[]{:S(2)}, u32[]{:S(2)}) collective-permute-start(bf16[48,1024]{1,0:T(8,128)(2,1)S(1)} %get-tuple-element.73), channel_id=1, source_target_pairs={{0,1},{1,0},{2,3},{3,2},{4,5},{5,4},{6,7},{7,6},{8,9},{9,8},{10,11... | collective-permute-start | bytes 294920 | tf_op jit(solution)/shard_map/ppermute | solution.py:528
  149.6 7.9 %collective-permute-start.16 = (bf16[48,1024]{1,0:T(8,128)(2,1)S(1)}, bf16[48,1024]{1,0:T(8,128)(2,1)S(1)}, u32[]{:S(2)}, u32[]{:S(2)}) collective-permute-start(bf16[48,1024]{1,0:T(8,128)(2,1)S(1)} %get-tuple-element.74), channel_id=1, source_target_pairs={{0,2},{1,3},{2,0},{3,1},{4,6},{5,7},{6,4},{7,5},{8,10},{9,11},{10,... | collective-permute-start | bytes 294920 | tf_op jit(solution)/shard_map/ppermute | solution.py:528
  149.7 7.8 %collective-permute-start.17 = (bf16[48,1024]{1,0:T(8,128)(2,1)S(1)}, bf16[48,1024]{1,0:T(8,128)(2,1)S(1)}, u32[]{:S(2)}, u32[]{:S(2)}) collective-permute-start(bf16[48,1024]{1,0:T(8,128)(2,1)S(1)} %get-tuple-element.75), channel_id=1, source_target_pairs={{0,3},{1,2},{2,1},{3,0},{4,7},{5,6},{6,5},{7,4},{8,11},{9,10},{10,... | collective-permute-start | bytes 294920 | tf_op jit(solution)/shard_map/ppermute | solution.py:528
  155.3 3.1 %collective-permute-start.9 = (bf16[48,1024]{1,0:T(8,128)(2,1)S(1)}, bf16[48,1024]{1,0:T(8,128)(2,1)S(1)}, u32[]{:S(2)}, u32[]{:S(2)}) collective-permute-start(bf16[48,1024]{1,0:T(8,128)(2,1)S(1)} %get-tuple-element.63), channel_id=1, source_target_pairs={{0,1},{1,0},{2,3},{3,2},{4,5},{5,4},{6,7},{7,6},{8,9},{9,8},{10,11... | collective-permute-start | bytes 294920 | tf_op jit(solution)/shard_map/ppermute | solution.py:528
  155.4 4.0 %collective-permute-start.10 = (bf16[48,1024]{1,0:T(8,128)(2,1)S(1)}, bf16[48,1024]{1,0:T(8,128)(2,1)S(1)}, u32[]{:S(2)}, u32[]{:S(2)}) collective-permute-start(bf16[48,1024]{1,0:T(8,128)(2,1)S(1)} %get-tuple-element.64), channel_id=1, source_target_pairs={{0,2},{1,3},{2,0},{3,1},{4,6},{5,7},{6,4},{7,5},{8,10},{9,11},{10,... | collective-permute-start | bytes 294920 | tf_op jit(solution)/shard_map/ppermute | solution.py:528
  155.5 6.6 %collective-permute-start.11 = (bf16[48,1024]{1,0:T(8,128)(2,1)S(1)}, bf16[48,1024]{1,0:T(8,128)(2,1)S(1)}, u32[]{:S(2)}, u32[]{:S(2)}) collective-permute-start(bf16[48,1024]{1,0:T(8,128)(2,1)S(1)} %get-tuple-element.65), channel_id=1, source_target_pairs={{0,3},{1,2},{2,1},{3,0},{4,7},{5,6},{6,5},{7,4},{8,11},{9,10},{10,... | collective-permute-start | bytes 294920 | tf_op jit(solution)/shard_map/ppermute | solution.py:528

commit v2 on v1

--- a/solution.py
+++ b/solution.py
@@ -66,19 +66,19 @@
 
 
 def regroup(parts):
-    rows = parts[0].shape[0]
-    lane = lane_group(rows)
-    low = lane < 64
-    even = (lane // 32) % 2 == 0
+    lane = lane_group(parts[0].shape[0])
     step = list(parts)
-    for a, b in ((0, 2), (1, 3)):
-        x, y = step[a], step[b]
-        step[a] = jnp.where(low, x, pltpu.roll(y, 64, 1))
-        step[b] = jnp.where(low, pltpu.roll(x, 64, 1), y)
-    for a, b in ((0, 1), (2, 3)):
-        x, y = step[a], step[b]
-        step[a] = jnp.where(even, x, pltpu.roll(y, 32, 1))
-        step[b] = jnp.where(even, pltpu.roll(x, 96, 1), y)
+    bit = len(parts) // 2
+    while bit:
+        d = 16 * bit
+        low = (lane // d) % 2 == 0
+        for a in range(len(parts)):
+            if a & bit:
+                continue
+            x, y = step[a], step[a | bit]
+            step[a] = jnp.where(low, x, pltpu.roll(y, d, 1))
+            step[a | bit] = jnp.where(low, pltpu.roll(x, 128 - d, 1), y)
+        bit //= 2
     return step
 
 
@@ -94,110 +94,168 @@
     out_ref[1:2, :] = jnp.sum(x * x, axis=0, keepdims=True)
 
 
-def table_kernel(flags, alpha_ref, beta_ref, filter_ref, w_ref, give_ref, held, sem):
+def give_kernel(flags, filter_ref, give_ref, held, ready, sems, out_sems):
     theirs = pl.multiple_of((1 - flags[0]) * HALF, HALF)
-    fetch = pltpu.make_async_copy(filter_ref.at[:, pl.ds(theirs, HALF), :], held, sem)
-    fetch.start()
-
+    rows = 32
+    fetches = []
+    for n in range(6):
+        part, k = n // 3, n % 3
+        fetches.append(
+            pltpu.make_async_copy(
+                filter_ref.at[part, pl.ds(theirs + rows * k, rows), :], held.at[n], sems.at[n]
+            )
+        )
+        fetches[-1].start()
+    sends = []
+    for n in range(6):
+        part, k = n // 3, n % 3
+        fetches[n].wait()
+        ready[n] = held[n].astype(BF16)
+        sends.append(
+            pltpu.make_async_copy(
+                ready.at[n], give_ref.at[part, rows * k : rows * (k + 1), :], out_sems.at[n]
+            )
+        )
+        sends[-1].start()
+    for send in sends:
+        send.wait()
+
+
+def table_kernel(alpha_ref, beta_ref, w_ref):
     def rows(b, carry):
-        ac = jnp.broadcast_to(alpha_ref[0, pl.ds(b, 1), :], (SHARE, 128))
-        as_ = jnp.broadcast_to(alpha_ref[1, pl.ds(b, 1), :], (SHARE, 128))
         start = pl.multiple_of(b * SHARE, SHARE)
-        for u in range(8):
-            bc = beta_ref[0, :, 128 * u : 128 * (u + 1)]
-            bs = beta_ref[1, :, 128 * u : 128 * (u + 1)]
-            w_ref[pl.ds(start, SHARE), 256 * u : 256 * u + 128] = (ac * bc - as_ * bs).astype(BF16)
-            w_ref[pl.ds(start, SHARE), 256 * u + 128 : 256 * (u + 1)] = (
-                -(as_ * bc + ac * bs)
-            ).astype(BF16)
+        for par in range(2):
+            ac = jnp.broadcast_to(alpha_ref[0, pl.ds(b + 32 * par, 1), :], (SHARE, 128))
+            as_ = jnp.broadcast_to(alpha_ref[1, pl.ds(b + 32 * par, 1), :], (SHARE, 128))
+            for u in range(4 * par, 4 * par + 4):
+                bc = beta_ref[0, :, 128 * u : 128 * (u + 1)]
+                bs = beta_ref[1, :, 128 * u : 128 * (u + 1)]
+                w_ref[pl.ds(start, SHARE), 256 * u : 256 * u + 128] = (ac * bc - as_ * bs).astype(
+                    BF16
+                )
+                w_ref[pl.ds(start, SHARE), 256 * u + 128 : 256 * (u + 1)] = (
+                    -(as_ * bc + ac * bs)
+                ).astype(BF16)
         return carry
 
-    lax.fori_loop(0, NSEQ, rows, 0)
-    fetch.wait()
-    give_ref[...] = held[...].astype(BF16)
-
-
-def forward_kernel(x_ref, s0, s1, s2, s3, gain_ref, w_ref, send_ref, normed_ref):
+    lax.fori_loop(0, 32, rows, 0)
+
+
+def forward_kernel(
+    x_ref, s0, s1, s2, s3, gain_ref, w_ref, send_ref, normed_ref, kept_ref, fold, sem
+):
+    keep = pltpu.make_async_copy(w_ref, kept_ref, sem)
+    keep.start()
     total = s0[...] + s1[...] + s2[...] + s3[...]
     mean = total[0:1, :] / D
     square = total[1:2, :] / D
     scale = lax.rsqrt(square - mean * mean + 1e-05)
     xn = ((x_ref[...].astype(F32) - mean) * scale * column_of(gain_ref)).astype(BF16)
     normed_ref[...] = xn
-    for u in range(8):
-        y = jnp.dot(normed_ref[...], w_ref[:, 256 * u : 256 * (u + 1)], preferred_element_type=F32)
+    left = xn[:, : TOK // 2].astype(F32)
+    right = xn[:, TOK // 2 :].astype(F32)
+    fold[0] = (left + right).astype(BF16)
+    fold[1] = (left - right).astype(BF16)
+    for b in range(4):
+        y = [
+            jnp.dot(
+                fold[par],
+                w_ref[:, 1024 * par + 256 * b : 1024 * par + 256 * (b + 1)],
+                preferred_element_type=F32,
+            )
+            for par in range(2)
+        ]
         for half in range(2):
             both = []
             for part in range(2):
                 both.append(
                     regroup(
                         [
-                            y[
+                            y[par][
                                 half * HALF + w * QUART : half * HALF + (w + 1) * QUART,
                                 128 * part : 128 * (part + 1),
                             ]
+                            for par in range(2)
                             for w in range(4)
                         ]
                     )
                 )
-            for v in range(4):
-                q = 4 * u + v
+            for v in range(8):
+                q = 8 * b + v
                 dest = 63 - q if half else q
                 send_ref[dest] = jnp.concatenate([both[0][v], both[1][v]], axis=0).astype(BF16)
-
-
-def filter_kernel(
-    flags, own_ref, got_ref, ca_ref, cb_ref, g_out, g1_out, g_ref, g1_ref, sems
-):
+    keep.wait()
+
+
+def lanes_of(rows):
+    lane = lax.broadcasted_iota(jnp.int32, (rows, 128), 1)
+    group = (lane // 16) % 4
+    return 2 * (lane % 16) + lane // 64, group
+
+
+def make_gains(flags, own_ref, got_ref, ca_ref, cb_ref, g_ref, g1_ref):
     high = flags[0] == 1
     first = flags[1] == 1
     row = lax.broadcasted_iota(jnp.int32, (128, 128), 0)
-    lane = lax.broadcasted_iota(jnp.int32, (128, 128), 1)
-    mirror = jnp.where((row + lane == 128) & (lane % SHARE != 0), 1.0, 0.0).astype(BF16)
+    freq, group = lanes_of(128)
+    lane = SHARE * group + freq
+    straight = jnp.where(row == lane, 1.0, 0.0)
+    mirror = jnp.where((row + lane == 128) & (freq != 0), 1.0, 0.0)
     crow = lax.broadcasted_iota(jnp.int32, (NSEQ, 128), 0)
-    clane = lax.broadcasted_iota(jnp.int32, (NSEQ, 128), 1)
+    cfreq, cgroup = lanes_of(NSEQ)
     keep = jnp.where(first, 0.0, 1.0)
 
-    def spread(target):
-        return jnp.where((clane % SHARE == 0) & (crow == target + clane // SHARE), 1.0, 0.0)
+    def column(part):
+        return (ca_ref[part].astype(F32) + cb_ref[part].astype(F32)).astype(BF16)
 
     for part in range(2):
-        column = (ca_ref[part].astype(F32) + cb_ref[part].astype(F32)).astype(BF16)
+        sign = 1.0 if part == 0 else -1.0
+        maps = jnp.concatenate([straight, sign * mirror], axis=0).astype(BF16)
+        crossed = jnp.concatenate(
+            [
+                jnp.where((cfreq == 0) & (crow == 63 - 4 * t - cgroup), sign * keep, 0.0)
+                for t in range(16)
+            ],
+            axis=1,
+        ).astype(BF16)
+        extra = jnp.dot(column(part), crossed, preferred_element_type=F32)
+        own = own_ref[part]
+        got = got_ref[part]
+        direct = jnp.where(high, got, own)
+        other = jnp.where(high, own, got)
         for t in range(16):
-            here = slice(128 * t, 128 * (t + 1))
-            there = slice(128 * (15 - t), 128 * (16 - t))
-            direct = jnp.where(high, got_ref[part, :, here].astype(F32), own_ref[part, :, here])
-            other = jnp.where(
-                high, own_ref[part, :, there], got_ref[part, :, there].astype(F32)
-            ).astype(BF16)
-            crossed = jnp.where(
-                (clane % SHARE == 0) & (crow == 63 - 4 * t - clane // SHARE), 1.0, 0.0
-            ).astype(BF16)
-            mirrored = jnp.dot(other, mirror, preferred_element_type=F32) + keep * jnp.dot(
-                column, crossed, preferred_element_type=F32
+            pair = jnp.concatenate(
+                [direct[:, 128 * t : 128 * (t + 1)], other[:, 128 * (15 - t) : 128 * (16 - t)]],
+                axis=1,
             )
-            both = direct + mirrored if part == 0 else direct - mirrored
+            both = (
+                jnp.dot(pair, maps, preferred_element_type=F32)
+                + extra[:, 128 * t : 128 * (t + 1)]
+            )
             out = regroup([both[w * QUART : (w + 1) * QUART] for w in range(4)])
             for v in range(4):
                 g_ref[part, 4 * t + v] = out[v]
-        pltpu.make_async_copy(g_ref.at[part], g_out.at[part], sems.at[part]).start()
 
     @pl.when(first)
     def _():
         for part in range(2):
-            column = (ca_ref[part].astype(F32) + cb_ref[part].astype(F32)).astype(BF16)
+            plain = jnp.concatenate(
+                [
+                    jnp.where((cfreq == 0) & (crow == 4 * t + cgroup), 1.0, 0.0)
+                    for t in range(16)
+                ],
+                axis=1,
+            ).astype(BF16)
+            alone = jnp.dot(column(part), plain, preferred_element_type=F32)
             for t in range(16):
-                plain = spread(4 * t).astype(BF16)
-                both = jnp.dot(column, plain, preferred_element_type=F32)
+                both = alone[:, 128 * t : 128 * (t + 1)]
                 out = regroup([both[w * QUART : (w + 1) * QUART] for w in range(4)])
                 for v in range(4):
-                    g1_ref[part, 4 * t + v] = out[v]
-        last = pltpu.make_async_copy(g1_ref, g1_out, sems.at[2])
-        last.start()
-        last.wait()
-
-    for part in range(2):
-        pltpu.make_async_copy(g_ref.at[part], g_out.at[part], sems.at[part]).wait()
+                    g1_ref[part, 4 * t + v] = packed([out[v][8 * k : 8 * k + 8] for k in range(3)])
+
+
+def packed(tiles):
+    return tiles[0] + pltpu.roll(tiles[1], 1, 1) + pltpu.roll(tiles[2], 2, 1)
 
 
 def turn_i(re, im, s):
@@ -269,47 +327,51 @@
 
 
 def middle_kernel(
-    flags, got_ref, g_in, g1_in, out_ref, xs, a_ref, b_ref, t1, g_ref, g1_ref, sems
+    flags, moved, own_ref, got, ca_ref, cb_ref, out_ref,
+    moved_ref, got_ref, g_ref, g1_ref, xs, a_ref, b_ref, t1, sems,
 ):
     first = flags[1] == 1
-    gains = pltpu.make_async_copy(g_in, g_ref, sems.at[0])
-    gains.start()
-    special = (lane_group(8) % SHARE == 0) & first
+    fetches = [
+        pltpu.make_async_copy(got, got_ref, sems.at[0]),
+        pltpu.make_async_copy(moved, moved_ref, sems.at[1]),
+    ]
+    for fetch in fetches:
+        fetch.start()
+    freq, _ = lanes_of(8)
+    special = (freq == 0) & first
+    fetches[0].wait()
+    make_gains(flags, own_ref, got_ref, ca_ref, cb_ref, g_ref, g1_ref)
+    fetches[1].wait()
 
     def widen(p, carry):
-        xs[p] = got_ref[p].astype(F32)
+        xs[p] = moved_ref[p].astype(F32)
         return carry
 
-    lax.fori_loop(0, NSEQ, widen, 0)
+    lax.fori_loop(0, NSEQ, widen, 0, unroll=8)
 
     def half_turn(p):
         return math.cos(2.0 * math.pi * p / 128.0), math.sin(2.0 * math.pi * p / 128.0)
 
     @pl.when(first)
     def _():
-        fetch = pltpu.make_async_copy(g1_in, g1_ref, sems.at[1])
-        fetch.start()
-        fetch.wait()
-
-        def alone(i, carry):
-            top = pl.ds(pl.multiple_of(i * 8, 8), 8)
-            bottom = pl.ds(pl.multiple_of(i * 8 + QUART, 8), 8)
-
-            def load(p):
-                c, s = half_turn(p)
-                im = jnp.where(special, xs[p, bottom, :], 0.0)
-                return im * c, im * (-s)
-
-            def store(p, re, im):
-                c, s = half_turn(p)
-                t1[p, top, :] = re * c - im * s
-
-            across(load, store, lambda g: (g1_ref[0, g, top, :], g1_ref[1, g, top, :]), a_ref, b_ref)
-            return carry
-
-        lax.fori_loop(0, 3, alone, 0)
-
-    gains.wait()
+        def load(p):
+            c, s = half_turn(p)
+            im = packed(
+                [
+                    jnp.where(special, xs[p, QUART + 8 * k : QUART + 8 * k + 8, :], 0.0)
+                    for k in range(3)
+                ]
+            )
+            return im * c, im * (-s)
+
+        def store(p, re, im):
+            c, s = half_turn(p)
+            turned = re * c - im * s
+            t1[p, 0:8, :] = turned
+            t1[p, 8:16, :] = pltpu.roll(turned, 127, 1)
+            t1[p, 16:24, :] = pltpu.roll(turned, 126, 1)
+
+        across(load, store, lambda g: (g1_ref[0, g], g1_ref[1, g]), a_ref, b_ref)
 
     def every(i, carry):
         top = pl.ds(pl.multiple_of(i * 8, 8), 8)
@@ -331,7 +393,7 @@
         out_ref[p] = xs[p].astype(BF16)
         return carry
 
-    lax.fori_loop(0, NSEQ, narrow, 0)
+    lax.fori_loop(0, NSEQ, narrow, 0, unroll=8)
 
 
 def in_three(x):
@@ -356,28 +418,39 @@
     )
     for k, part in enumerate(in_three(weight)[:2]):
         st[5 + k : 6 + k, 0:CH] = part.astype(F32)
-    for n in range(TC // 256):
-        here = slice(256 * n, 256 * (n + 1))
-        cols = slice(chunk * TC + 256 * n, chunk * TC + 256 * (n + 1))
+    for n in range(TC // 512):
+        mine = slice(256 * n, 256 * (n + 1))
         fetches[n].wait()
-        conv = lax.dot_general(
-            values, w_ref[here, :], (((1,), (1,)), ((), ())), preferred_element_type=F32
+        even, odd = (
+            lax.dot_general(
+                values[:, 1024 * par : 1024 * (par + 1)],
+                w_ref[mine, 1024 * par : 1024 * (par + 1)],
+                (((1,), (1,)), ((), ())),
+                preferred_element_type=F32,
+            )
+            for par in range(2)
         )
-        res = (
-            x_ref[:, cols].astype(F32)
-            + conv * (1.0 / LENGTH)
-            + skip * normed_ref[:, cols].astype(F32)
-        ).astype(BF16)
-        res_ref[:, here] = res
-        r = res.astype(F32)
-        mean = jnp.sum(r, axis=0, keepdims=True) * (1.0 / CH)
-        centred = r - mean
-        for k, part in enumerate(in_three(mean)):
-            st[k : k + 1, here] = part.astype(F32)
-        for k, part in enumerate(in_three(jnp.sum(centred * centred, axis=0, keepdims=True))[:2]):
-            st[3 + k : 4 + k, here] = part.astype(F32)
-        z = (centred * gain).astype(BF16)
-        tm[:, here] = jnp.dot(mix_t_ref[...], z, preferred_element_type=F32)
+        for side, conv in enumerate((even + odd, even - odd)):
+            here = slice(side * TC // 2 + 256 * n, side * TC // 2 + 256 * (n + 1))
+            start = side * TOK // 2 + chunk * TC // 2 + 256 * n
+            cols = slice(start, start + 256)
+            res = (
+                x_ref[:, cols].astype(F32)
+                + conv * (1.0 / LENGTH)
+                + skip * normed_ref[:, cols].astype(F32)
+            ).astype(BF16)
+            res_ref[:, here] = res
+            r = res.astype(F32)
+            mean = jnp.sum(r, axis=0, keepdims=True) * (1.0 / CH)
+            centred = r - mean
+            for k, part in enumerate(in_three(mean)):
+                st[k : k + 1, here] = part.astype(F32)
+            for k, part in enumerate(
+                in_three(jnp.sum(centred * centred, axis=0, keepdims=True))[:2]
+            ):
+                st[3 + k : 4 + k, here] = part.astype(F32)
+            z = (centred * gain).astype(BF16)
+            tm[:, here] = jnp.dot(mix_t_ref[...], z, preferred_element_type=F32)
     for k in range(4):
         rows = pl.ds(pl.multiple_of((me ^ k) * PIECE, PIECE), PIECE)
         outs[k][...] = jnp.concatenate([tm[rows, :], st[...]], axis=0).astype(BF16)
@@ -385,9 +458,9 @@
 
 def fetch_table(w_hbm, w_ref, sems, chunk):
     fetches = []
-    for n in range(TC // 256):
+    for n in range(TC // 512):
         here = slice(256 * n, 256 * (n + 1))
-        there = slice(chunk * TC + 256 * n, chunk * TC + 256 * (n + 1))
+        there = slice(chunk * TC // 2 + 256 * n, chunk * TC // 2 + 256 * (n + 1))
         fetches.append(pltpu.make_async_copy(w_hbm.at[there, :], w_ref.at[here, :], sems.at[n]))
         fetches[-1].start()
     return fetches
@@ -399,16 +472,17 @@
 ):
     fetches = fetch_table(w_hbm, w_ref, sems, 0)
     for half in range(2):
-        for u in range(8):
+        for b in range(4):
             parts = []
-            for v in range(4):
-                q = 4 * u + v
+            for v in range(8):
+                q = 8 * b + v
                 parts.append(got_ref[63 - q if half else q].astype(F32))
             out = regroup(parts)
-            for w in range(4):
-                low = half * HALF + w * QUART
-                tall[low : low + QUART, 256 * u : 256 * u + 128] = out[w][:QUART]
-                tall[low : low + QUART, 256 * u + 128 : 256 * (u + 1)] = out[w][QUART:]
+            for k in range(8):
+                low = half * HALF + (k % 4) * QUART
+                left = 1024 * (k // 4) + 256 * b
+                tall[low : low + QUART, left : left + 128] = out[k][:QUART]
+                tall[low : low + QUART, left + 128 : left + 256] = out[k][QUART:]
     values = tall[...].astype(BF16)
     values_ref[...] = values
     tokens_back(
@@ -516,10 +590,13 @@
 
 
 def final_second_kernel(flags, p0, p1, p2, p3, res_ref, mix_t_ref, early_ref, out_ref, f_ref):
-    out_ref[:, 0:TC] = early_ref[...]
+    side = TC // 2
+    for k in range(2):
+        out_ref[:, 2 * k * side : (2 * k + 1) * side] = early_ref[:, k * side : (k + 1) * side]
 
     def store(cols, x):
-        out_ref[:, cols.start + TC : cols.stop + TC] = x
+        start = cols.start + (side if cols.start < side else 2 * side)
+        out_ref[:, start : start + 256] = x
 
     tokens_out(flags, (p0, p1, p2, p3), res_ref, mix_t_ref, f_ref, store)
 
@@ -546,11 +623,20 @@
     first = (place == 0) | (place == 63)
     flags = jnp.stack([high, first, lane_of, place]).astype(jnp.int32)
     mine = jnp.where(high, HALF, 0)
+    give = call(
+        give_kernel, pltpu.HBM((2, HALF, TOK), BF16), "sh",
+        scratch=[
+            pltpu.VMEM((6, 32, TOK), F32), pltpu.VMEM((6, 32, TOK), BF16),
+            pltpu.SemaphoreType.DMA((6,)), pltpu.SemaphoreType.DMA((6,)),
+        ],
+        outs="h",
+    )(flags, in_hbm(filter_spectrum))
+    got = lax.ppermute(give, "seq", [(i, 63 - i) for i in range(64)])
     sums = call(sums_kernel, shape((2, TOK), F32), "v")(tokens)
     others = []
     for k in (1, 2, 3):
         others.append(swap(sums, k))
-    own = lax.dynamic_slice_in_dim(filter_spectrum, mine, HALF, 1)
+    own = lax.dynamic_slice_in_dim(filter_spectrum, mine, HALF, 1).astype(BF16)
     pick_row = jnp.arange(TOK, dtype=jnp.int32)[:, None]
     pick_col = jnp.arange(NSEQ, dtype=jnp.int32)[None, :]
     pick = (pick_row == SHARE * pick_col).astype(BF16)
@@ -559,7 +645,8 @@
     ).astype(BF16)
     ca = lax.ppermute(column[:, :HALF], "seq", [(32, 0)] + [(64 - i, i) for i in range(1, 32)])
     cb = lax.ppermute(column[:, HALF:], "seq", [(32, 63)] + [(i + 1, i) for i in range(32, 63)])
-    freq = jnp.arange(TOK // 2, dtype=jnp.int32)
+    slot = jnp.arange(TOK // 2, dtype=jnp.int32)
+    freq = 256 * (slot // 128 % 4) + 2 * (slot % 128) + slot // 512
     step = jnp.arange(SHARE, dtype=jnp.int32)
     angle = (freq[None, :] * (64 * step[:, None] + place) % LENGTH).astype(F32) * (
         2.0 * math.pi / LENGTH
@@ -568,33 +655,43 @@
     beta = jnp.stack(
         [jnp.cos(angle), jnp.where(freq[None, :] == 0, -parity[:, None], jnp.sin(angle))]
     )
-    turn = (
-        (jnp.arange(NSEQ, dtype=jnp.int32)[:, None] * (jnp.arange(128, dtype=jnp.int32)[None, :])) % 64
-    ).astype(F32) * (2.0 * math.pi / 64)
+    half_row = jnp.arange(64, dtype=jnp.int32)[:, None]
+    half_freq = 2 * jnp.arange(128, dtype=jnp.int32)[None, :] + half_row // 32
+    turn = ((half_row % 32) * half_freq % 64).astype(F32) * (2.0 * math.pi / 64)
     alpha = jnp.stack([jnp.cos(turn), jnp.sin(turn)])
-    table, give = call(
-        table_kernel, (shape((TOK, TOK), BF16), shape((2, HALF, TOK), BF16)), "svvh",
-        scratch=[pltpu.VMEM((2, HALF, TOK), F32), pltpu.SemaphoreType.DMA(())],
-    )(flags, alpha, beta, in_hbm(filter_spectrum))
-    got = lax.ppermute(give, "seq", [(i, 63 - i) for i in range(64)])
-    send, normed = call(
+    table = call(table_kernel, shape((TOK // 2, TOK), BF16), "vv")(alpha, beta)
+    send, normed, kept = call(
         forward_kernel,
-        (shape((NSEQ, 2 * QUART, 128), BF16), shape((CH, TOK), BF16)),
+        (
+            shape((NSEQ, 2 * QUART, 128), BF16),
+            shape((CH, TOK), BF16),
+            pltpu.HBM((TOK // 2, TOK), BF16),
+        ),
         "v" * 7,
+        scratch=[pltpu.VMEM((2, CH, TOK // 2), BF16), pltpu.SemaphoreType.DMA(())],
+        outs="vvh",
         mib=20,
     )(tokens, sums, *others, norm_gain, table)
     moved = lax.all_to_all(send, "seq", split_axis=0, concat_axis=0, tiled=True)
-    gains, gains_first = call(
-        filter_kernel,
-        (pltpu.HBM((2, NSEQ, QUART, 128), F32), pltpu.HBM((2, NSEQ, QUART, 128), F32)),
-        "svvvv",
+    back = call(
+        middle_kernel,
+        shape((NSEQ, 2 * QUART, 128), BF16),
+        "shvhvv",
         scratch=[
+            pltpu.VMEM((NSEQ, 2 * QUART, 128), BF16),
+            pltpu.VMEM((2, HALF, TOK), BF16),
             pltpu.VMEM((2, NSEQ, QUART, 128), F32),
-            pltpu.VMEM((2, NSEQ, QUART, 128), F32),
-            pltpu.SemaphoreType.DMA((3,)),
+            pltpu.VMEM((2, NSEQ, 8, 128), F32),
+            pltpu.VMEM((NSEQ, 2 * QUART, 128), F32),
+            pltpu.VMEM((2, NSEQ, 8, 128), F32),
+            pltpu.VMEM((2, NSEQ, 8, 128), F32),
+            pltpu.VMEM((NSEQ, QUART, 128), F32),
+            pltpu.SemaphoreType.DMA((2,)),
         ],
-        outs="hh",
-    )(flags, own, got, ca, cb)
+    )(flags, in_hbm(moved), own, in_hbm(got), ca, cb)
+    back, mix_in, up_weight, down_weight, mix_out = lax.optimization_barrier(
+        (back, mix_in, up_weight, down_weight, mix_out)
+    )
     mix_in_full, mix_in_t, up_t, down_t, mix_out_t = call(
         weights_kernel,
         (
@@ -604,32 +701,18 @@
         "vvvv",
         scratch=[pltpu.VMEM((CH, CH), F32), pltpu.VMEM((CH, HID), F32), pltpu.VMEM((HID, CH), F32)],
     )(mix_in, up_weight, down_weight, mix_out)
-    moved, mix_in_full, mix_in_t, down_t, up_t, mix_out_t = lax.optimization_barrier(
-        (moved, mix_in_full, mix_in_t, down_t, up_t, mix_out_t)
-    )
-    back = call(
-        middle_kernel,
-        shape((NSEQ, 2 * QUART, 128), BF16),
-        "svhh",
-        scratch=[
-            pltpu.VMEM((NSEQ, 2 * QUART, 128), F32),
-            pltpu.VMEM((2, NSEQ, 8, 128), F32),
-            pltpu.VMEM((2, NSEQ, 8, 128), F32),
-            pltpu.VMEM((NSEQ, QUART, 128), F32),
-            pltpu.VMEM((2, NSEQ, QUART, 128), F32),
-            pltpu.VMEM((2, NSEQ, QUART, 128), F32),
-            pltpu.SemaphoreType.DMA((2,)),
-        ],
-    )(flags, moved, in_hbm(gains), in_hbm(gains_first))
     home = lax.all_to_all(back, "seq", split_axis=0, concat_axis=0, tiled=True)
+    home, mix_in_full, mix_in_t, down_t, up_t, mix_out_t = lax.optimization_barrier(
+        (home, mix_in_full, mix_in_t, down_t, up_t, mix_out_t)
+    )
     piece = (shape((CH, TC), BF16),) + (shape((ROWS, TC), BF16),) * 4
     small = [
         pltpu.VMEM((CH, TC), F32),
         pltpu.VMEM((8, TC), F32),
-        pltpu.VMEM((TC, TOK), BF16),
-        pltpu.SemaphoreType.DMA((TC // 256,)),
+        pltpu.VMEM((TC // 2, TOK), BF16),
+        pltpu.SemaphoreType.DMA((TC // 512,)),
     ]
-    rest = (in_hbm(table), tokens, normed, skip_weight, mlp_gain, mix_in_full, mix_in_t)
+    rest = (in_hbm(kept), tokens, normed, skip_weight, mlp_gain, mix_in_full, mix_in_t)
     values, res_a, *first_a = call(
         back_first_kernel, (shape((CH, TOK), BF16),) + piece, "svhvvvvvv",
         scratch=[pltpu.VMEM((CH, TOK), F32)] + small, mib=20,

time: 164 us -> 154 us (0.939)
  blocking collectives: 37.7 us -> 0 us
  waiting for transfers between devices: 29 us -> 45.9 us
  starting transfers between devices: 38.6 us -> 55.4 us
  Pallas kernels: 51.8 us -> 44.2 us
  local copies, waits for them, and re-layouts: 3.03 us -> 5.88 us
  matrix products: 2.53 us -> 0.65 us
    all_to_all x1 -> x0, blocking collectives: 37.7 us -> none  [block(): home = lax.all_to_all(back, 'seq', split_axis=0, concat_axis=0, tiled=True)]
    all_to_all x0 -> x1, starting transfers between devices: none -> 14.1 us  [block(): home = lax.all_to_all(back, 'seq', split_axis=0, concat_axis=0, tiled=True)]
    ppermute x1, waiting for transfers between devices: 23.9 us -> 31.8 us  [block(): got = lax.ppermute(give, 'seq', [(i, 63 - i) for i in range(64)])]
    all_to_all x0 -> x1, waiting for transfers between devices: none -> 5.6 us  [block(): home = lax.all_to_all(back, 'seq', split_axis=0, concat_axis=0, tiled=True)]
    ppermute x1, waiting for transfers between devices: 0.01 us -> 3.21 us  [block(): lax.ppermute(column[:, :HALF], 'seq', [(32, 0)] + [(64 - i, i) for i in r...]
    unnamed x20, local copies, waits for them, and re-layouts: 1.28 us -> 4.2 us
    pallas_call x1, Pallas kernels: 6.79 us -> 4.07 us  [block(): call(back_first_kernel, (shape((CH, TOK), BF16),) + piece, 'svhvvvvvv', s...]
    ppermute x15, starting transfers between devices: 16.2 us -> 18.8 us  [swap(): return lax.ppermute(x, 'chan', [(i, i ^ k) for i in range(4)])]
  transfers between devices with their start and end apart: 19 -> 20, of which waited for: 4 -> 6; matrix products, arithmetic and copies ran while one was open for 3% -> 2% of each run, Pallas kernels for 21% -> 17%
where the time goes in v2:
time: 154 us; the launch traced here: 153 us
  starting transfers between devices  55.4 us (36%)
  waiting for transfers between devices  45.9 us (30%)
  Pallas kernels  44.2 us (29%)
  local copies, waits for them, and re-layouts  5.88 us (4%)
    ppermute x1, waiting for transfers between devices, block(): got = lax.ppermute(give, 'seq', [(i, 63 - i) for i in range(64)])  31.8 us
    ppermute x15, starting transfers between devices, swap(): return lax.ppermute(x, 'chan', [(i, i ^ k) for i in range(4)])  18.8 us
    all_to_all x1, starting transfers between devices, block(): home = lax.all_to_all(back, 'seq', split_axis=0, concat_axis=0, tiled=True)  14.1 us
    all_to_all x1, starting transfers between devices, block(): moved = lax.all_to_all(send, 'seq', split_axis=0, concat_axis=0, tiled=True)  12.8 us
    pallas_call x1, Pallas kernels, block(): call(weights_kernel, (shape((CH, CH), BF16), shape((CH, CH), BF16), shape...  12.3 us
    pallas_call x1, Pallas kernels, block(): call(middle_kernel, shape((NSEQ, 2 * QUART, 128), BF16), 'shvhvv', scratc...  9.69 us
    ppermute x1, starting transfers between devices, block(): got = lax.ppermute(give, 'seq', [(i, 63 - i) for i in range(64)])  7.67 us
    all_to_all x1, waiting for transfers between devices, block(): home = lax.all_to_all(back, 'seq', split_axis=0, concat_axis=0, tiled=True)  5.6 us
  transfers between devices with their start and end apart: 20, of which 6 were waited for; matrix products, arithmetic and copies ran while one was open for 2% of the time, Pallas kernels for 17%

profile of v2, /device:TPU:1, one launch (start us, length us, event | category | flops | bytes accessed | tf_op | source)
XLA Modules:
  0.0 153.3 jit_solution(1282128905084010712)
XLA Ops:
  0.0 1.1 copy-done
  1.3 3.3 %collective-permute-start = (f32[2,2048]{1,0:T(2,128)S(1)}, f32[2,2048]{1,0:T(2,128)S(1)}, u32[]{:S(2)}, u32[]{:S(2)}) collective-permute-start(f32[2,2048]{1,0:T(2,128)S(1)} %shard_map.91.s0), channel_id=1, source_target_pairs={{0,1},{1,0},{2,3},{3,2},{4,5},{5,4},{6,7},{7,6},{8,9},{9,8},{10,11... | collective-permute-start | bytes 49160 | tf_op jit(solution)/shard_map/ppermute | solution.py:605
  4.6 1.7 %collective-permute-start.2 = (f32[2,2048]{1,0:T(2,128)S(1)}, f32[2,2048]{1,0:T(2,128)S(1)}, u32[]{:S(2)}, u32[]{:S(2)}) collective-permute-start(f32[2,2048]{1,0:T(2,128)S(1)} %shard_map.91.s0), channel_id=1, source_target_pairs={{0,3},{1,2},{2,1},{3,0},{4,7},{5,6},{6,5},{7,4},{8,11},{9,10},{10,... | collective-permute-start | bytes 49160 | tf_op jit(solution)/shard_map/ppermute | solution.py:605
  7.3 1.5 shard_map.92.w_ref
  8.8 2.9 %shard_map.93 = (bf16[64,48,128]{2,1,0:T(8,128)(2,1)}, bf16[192,2048]{1,0:T(8,128)(2,1)S(1)}, bf16[1024,2048]{1,0:T(8,128)(2,1)}) custom-call(bf16[192,2048]{1,0:T(8,128)(2,1)S(1)} %copy-done.1, f32[2,2048]{1,0:T(2,128)S(1)} %shard_map.91.s0, f32[2,2048]{1,0:T(2,128)S(1)} %collective-permute-done.s1, f32[2,2048]{1,0:T(2,128)S(1)} %collective-permute-done.1.s2, ...), custom_call_target="tpu_custom_call" | custom-call | tf_op jit(solution)/shard_map/pallas_call | solution.py:663
  11.7 12.8 %all-to-all-start = ((bf16[64,48,128]{2,1,0:T(8,128)(2,1)}), bf16[64,48,128]{2,1,0:T(8,128)(2,1)}, u32[]{:S(2)}, u32[]{:S(2)}) async-start(bf16[64,48,128]{2,1,0:T(8,128)(2,1)} %get-tuple-element.43), calls=%async_computation | async-start | bytes 1572864 | tf_op jit(solution)/shard_map/all_to_all | solution.py:675
  24.7 3.0 %shard_map.94 = bf16[2,96,2048]{2,1,0:T(8,128)(2,1)} custom-call(s32[4]{0:T(128)S(1)} %pad_add_fusion.flags, f32[2,192,2048]{2,1,0:T(8,128)} %filter_ref.1), custom_call_target="tpu_custom_call" | custom-call | tf_op jit(solution)/shard_map/pallas_call | solution.py:626
  27.6 7.7 %collective-permute-start.3 = (bf16[2,96,2048]{2,1,0:T(8,128)(2,1)}, bf16[2,96,2048]{2,1,0:T(8,128)(2,1)}, u32[]{:S(2)}, u32[]{:S(2)}) collective-permute-start(bf16[2,96,2048]{2,1,0:T(8,128)(2,1)} %shard_map.94), channel_id=1, source_target_pairs={{0,252},{4,248},{8,244},{12,240},{16,236},{20,232},{24,228},{28,22... | collective-permute-start | bytes 2359304 | tf_op jit(solution)/shard_map/ppermute | solution.py:634
  36.1 1.3 collective-permute-start.4
  38.1 1.5 %dynamic-slice_convert_fusion.own_ref = bf16[2,96,2048]{2,1,0:T(8,128)(2,1)S(1)} fusion(f32[2,192,2048]{2,1,0:T(8,128)} %filter_ref.1, s32[]{:T(128)S(6)} %select_n.152), kind=kLoop, calls=%fused_computation.2 | loop fusion | bytes 1572868 | tf_op jit(solution)/shard_map/convert_element_type | solution.py:639
  39.7 3.2 %collective-permute-done.4.ca_ref = bf16[2,96,64]{2,1,0:T(8,128)(2,1)S(1)} collective-permute-done((bf16[2,96,64]{2,1,0:T(8,128)(2,1)S(1)}, bf16[2,96,64]{2,1,0:T(8,128)(2,1)S(1)}, u32[]{:S(2)}, u32[]{:S(2)}) %collective-permute-start.4) | collective-permute-done | bytes 24608 | tf_op jit(solution)/shard_map/ppermute | solution.py:646
  42.9 31.8 %collective-permute-done.3.got = bf16[2,96,2048]{2,1,0:T(8,128)(2,1)} collective-permute-done((bf16[2,96,2048]{2,1,0:T(8,128)(2,1)}, bf16[2,96,2048]{2,1,0:T(8,128)(2,1)}, u32[]{:S(2)}, u32[]{:S(2)}) %collective-permute-start.3) | collective-permute-done | bytes 786464 | tf_op jit(solution)/shard_map/ppermute | solution.py:634
  74.7 9.7 %shard_map.95 = bf16[64,48,128]{2,1,0:T(8,128)(2,1)} custom-call(s32[4]{0:T(128)S(1)} %pad_add_fusion.flags, bf16[64,48,128]{2,1,0:T(8,128)(2,1)} %all-to-all-done.moved, bf16[2,96,2048]{2,1,0:T(8,128)(2,1)S(1)} %dynamic-slice_convert_fusion.own_ref, bf16[2,96,2048]{2,1,0:T(8,128)(2,1)} %collective-permute-done.3.got, ...), custom_call_target="tpu_custom_call" | custom-call | tf_op jit(solution)/shard_map/pallas_call | solution.py:676
  84.4 14.1 %all-to-all-start.1 = ((bf16[64,48,128]{2,1,0:T(8,128)(2,1)}), bf16[64,48,128]{2,1,0:T(8,128)(2,1)S(1)}, u32[]{:S(2)}, u32[]{:S(2)}) async-start(bf16[64,48,128]{2,1,0:T(8,128)(2,1)} %shard_map.95), calls=%async_computation.1 | async-start | bytes 1572864 | tf_op jit(solution)/shard_map/all_to_all | solution.py:704
  98.5 1.1 copy-done.2
  99.6 1.1 copy-done.3
  100.6 0.9 copy-done.5
  101.5 12.3 %shard_map.96 = (bf16[192,192]{1,0:T(8,128)(2,1)S(1)}, bf16[192,192]{1,0:T(8,128)(2,1)S(1)}, bf16[768,192]{1,0:T(8,128)(2,1)S(1)}, bf16[192,768]{1,0:T(8,128)(2,1)S(1)}, bf16[192,192]{1,0:T(8,128)(2,1)S(1)}) custom-call(bf16[1,36864]{1,0:T(2,128)(2,1)S(1)} %copy-done.4, bf16[1,147456]{1,0:T(2,128)(2,1)S(1)} %copy-done.2, bf16[1,147456]{1,0:T(2,128)(2,1)S(1)} %copy-done.3, ...), custom_call_target="tpu_custom_call" | custom-call | tf_op jit(solution)/shard_map/pallas_call | solution.py:695
  113.8 5.6 %all-to-all-done.1.got_ref = bf16[64,48,128]{2,1,0:T(8,128)(2,1)S(1)} async-done(((bf16[64,48,128]{2,1,0:T(8,128)(2,1)}), bf16[64,48,128]{2,1,0:T(8,128)(2,1)S(1)}, u32[]{:S(2)}, u32[]{:S(2)}) %all-to-all-start.1) | async-done | bytes 786464 | tf_op jit(solution)/shard_map/all_to_all | solution.py:704
  119.4 4.1 %shard_map.97 = (bf16[192,2048]{1,0:T(8,128)(2,1)S(1)}, bf16[192,1024]{1,0:T(8,128)(2,1)S(1)}, bf16[56,1024]{1,0:T(8,128)(2,1)S(1)}, bf16[56,1024]{1,0:T(8,128)(...) custom-call(s32[4]{0:T(128)S(1)} %pad_add_fusion.flags, ...), custom_call_target="tpu_custom_call" | custom-call | tf_op jit(solution)/shard_map/pallas_call | solution.py:716
  123.5 5.1 %collective-permute-start.12 = (bf16[56,1024]{1,0:T(8,128)(2,1)S(1)}, bf16[56,1024]{1,0:T(8,128)(2,1)S(1)}, u32[]{:S(2)}, u32[]{:S(2)}) collective-permute-start(bf16[56,1024]{1,0:T(8,128)(2,1)S(1)} %get-tuple-element.73), channel_id=1, source_target_pairs={{0,1},{1,0},{2,3},{3,2},{4,5},{5,4},{6,7},{7,6},{8,9},{9,8},{10,11... | collective-permute-start | bytes 344072 | tf_op jit(solution)/shard_map/ppermute | solution.py:605
  128.6 2.1 %collective-permute-start.13 = (bf16[56,1024]{1,0:T(8,128)(2,1)S(1)}, bf16[56,1024]{1,0:T(8,128)(2,1)S(1)}, u32[]{:S(2)}, u32[]{:S(2)}) collective-permute-start(bf16[56,1024]{1,0:T(8,128)(2,1)S(1)} %get-tuple-element.74), channel_id=1, source_target_pairs={{0,2},{1,3},{2,0},{3,1},{4,6},{5,7},{6,4},{7,5},{8,10},{9,11},{10,... | collective-permute-start | bytes 344072 | tf_op jit(solution)/shard_map/ppermute | solution.py:605
  130.8 3.6 %shard_map.98 = (bf16[192,1024]{1,0:T(8,128)(2,1)S(1)}, bf16[56,1024]{1,0:T(8,128)(2,1)S(1)}, bf16[56,1024]{1,0:T(8,128)(2,1)S(1)}, bf16[56,1024]{1,0:T(8,128)(2,1)S(1)}, bf16[56,1024]{1,0:T(8,128)(2,1)S(1)}) custom-call(s32[4]{0:T(128)S(1)} %pad_add_fusion.flags, bf16[192,2048]{1,0:T(8,128)(2,1)S(1)} %get-tuple-element.59.values_ref, ...), custom_call_target="tpu_custom_call" | custom-call | tf_op jit(solution)/shard_map/pallas_call | solution.py:721
  134.8 1.5 collective-permute-start.7
  136.7 2.2 %shard_map.100 = (bf16[48,1024]{1,0:T(8,128)(2,1)S(1)}, bf16[48,1024]{1,0:T(8,128)(2,1)S(1)}, bf16[48,1024]{1,0:T(8,128)(2,1)S(1)}, bf16[48,1024]{1,0:T(8,128)(2,1)S(1)}) custom-call(s32[4]{0:T(128)S(1)} %pad_add_fusion.flags, bf16[56,1024]{1,0:T(8,128)(2,1)S(1)} %get-tuple-element.72.p0, bf16[56,1024]{1,0:T(8,128)(2,1)S(1)} %collective-permute-done.12.p1, ...), custom_call_target="tpu_custom_call" | custom-call | tf_op jit(solution)/shard_map/pallas_call | solution.py:727
  139.3 1.4 collective-permute-start.16
  141.1 1.5 collective-permute-done.8.p3
  142.6 2.2 %shard_map.99 = (bf16[48,1024]{1,0:T(8,128)(2,1)S(1)}, bf16[48,1024]{1,0:T(8,128)(2,1)S(1)}, bf16[48,1024]{1,0:T(8,128)(2,1)S(1)}, bf16[48,1024]{1,0:T(8,128)(2,1)S(1)}) custom-call(s32[4]{0:T(128)S(1)} %pad_add_fusion.flags, bf16[56,1024]{1,0:T(8,128)(2,1)S(1)} %get-tuple-element.60.p0, bf16[56,1024]{1,0:T(8,128)(2,1)S(1)} %collective-permute-done.6.p1, ...), custom_call_target="tpu_custom_call" | custom-call | tf_op jit(solution)/shard_map/pallas_call | solution.py:727
  144.8 1.6 %collective-permute-start.10 = (bf16[48,1024]{1,0:T(8,128)(2,1)S(1)}, bf16[48,1024]{1,0:T(8,128)(2,1)S(1)}, u32[]{:S(2)}, u32[]{:S(2)}) collective-permute-start(bf16[48,1024]{1,0:T(8,128)(2,1)S(1)} %get-tuple-element.68), channel_id=1, source_target_pairs={{0,2},{1,3},{2,0},{3,1},{4,6},{5,7},{6,4},{7,5},{8,10},{9,11},{10,... | collective-permute-start | bytes 294920 | tf_op jit(solution)/shard_map/ppermute | solution.py:605
  147.8 1.6 %collective-permute-done.10.p2 = bf16[48,1024]{1,0:T(8,128)(2,1)S(1)} collective-permute-done((bf16[48,1024]{1,0:T(8,128)(2,1)S(1)}, bf16[48,1024]{1,0:T(8,128)(2,1)S(1)}, u32[]{:S(2)}, u32[]{:S(2)}) %collective-permute-start.10) | collective-permute-done | bytes 98336 | tf_op jit(solution)/shard_map/ppermute | solution.py:605
  149.4 2.2 %collective-permute-done.11.p3 = bf16[48,1024]{1,0:T(8,128)(2,1)S(1)} collective-permute-done((bf16[48,1024]{1,0:T(8,128)(2,1)S(1)}, bf16[48,1024]{1,0:T(8,128)(2,1)S(1)}, u32[]{:S(2)}, u32[]{:S(2)}) %collective-permute-start.11) | collective-permute-done | bytes 98336 | tf_op jit(solution)/shard_map/ppermute | solution.py:605
  151.6 1.7 %shard_map.102 = bf16[192,2048]{1,0:T(8,128)(2,1)} custom-call(s32[4]{0:T(128)S(1)} %pad_add_fusion.flags, bf16[48,1024]{1,0:T(8,128)(2,1)S(1)} %get-tuple-element.66.p0, bf16[48,1024]{1,0:T(8,128)(2,1)S(1)} %collective-permute-done.9.p1, bf16[48,1024]{1,0:T(8,128)(2,1)S(1)} %collective-permute-done.10.p2, bf16[48,1024]{1,0:T(8,128)(2,1)S(1)} %collective-permute-done.11.p3, ...), custom_call_target="tpu_custom_call" | custom-call | tf_op jit(solution)/shard_map/pallas_call | solution.py:740
  (56 shorter events, 5.6 us)
Async XLA Ops:
  0.0 1.1 copy-start
  1.1 7.7 %copy-start.1 = (bf16[192,2048]{1,0:T(8,128)(2,1)S(1)}, bf16[192,2048]{1,0:T(8,128)(2,1)}, u32[]{:S(2)}) copy-start(bf16[192,2048]{1,0:T(8,128)(2,1)} %x_ref.7) | copy-start | bytes 2359300
  1.1 7.7 %copy-start.8 = (f32[192]{0:T(256)S(1)}, f32[192]{0:T(256)}, u32[]{:S(2)}) copy-start(f32[192]{0:T(256)} %param.12) | copy-start | bytes 2308
  1.3 7.5 %collective-permute-start = (f32[2,2048]{1,0:T(2,128)S(1)}, f32[2,2048]{1,0:T(2,128)S(1)}, u32[]{:S(2)}, u32[]{:S(2)}) collective-permute-start(f32[2,2048]{1,0:T(2,128)S(1)} %shard_map.91.s0), channel_id=1, source_target_pairs={{0,1},{1,0},{2,3},{3,2},{4,5},{5,4},{6,7},{7,6},{8,9},{9,8},{10,11... | collective-permute-start | bytes 49160 | tf_op jit(solution)/shard_map/ppermute | solution.py:605
  4.6 4.2 %collective-permute-start.1 = (f32[2,2048]{1,0:T(2,128)S(1)}, f32[2,2048]{1,0:T(2,128)S(1)}, u32[]{:S(2)}, u32[]{:S(2)}) collective-permute-start(f32[2,2048]{1,0:T(2,128)S(1)} %shard_map.91.s0), channel_id=1, source_target_pairs={{0,2},{1,3},{2,0},{3,1},{4,6},{5,7},{6,4},{7,5},{8,10},{9,11},{10,... | collective-permute-start | bytes 49160 | tf_op jit(solution)/shard_map/ppermute | solution.py:605
  4.6 4.2 %collective-permute-start.2 = (f32[2,2048]{1,0:T(2,128)S(1)}, f32[2,2048]{1,0:T(2,128)S(1)}, u32[]{:S(2)}, u32[]{:S(2)}) collective-permute-start(f32[2,2048]{1,0:T(2,128)S(1)} %shard_map.91.s0), channel_id=1, source_target_pairs={{0,3},{1,2},{2,1},{3,0},{4,7},{5,6},{6,5},{7,4},{8,11},{9,10},{10,... | collective-permute-start | bytes 49160 | tf_op jit(solution)/shard_map/ppermute | solution.py:605
  11.7 62.9 %all-to-all-start = ((bf16[64,48,128]{2,1,0:T(8,128)(2,1)}), bf16[64,48,128]{2,1,0:T(8,128)(2,1)}, u32[]{:S(2)}, u32[]{:S(2)}) async-start(bf16[64,48,128]{2,1,0:T(8,128)(2,1)} %get-tuple-element.43), calls=%async_computation | async-start | bytes 1572864 | tf_op jit(solution)/shard_map/all_to_all | solution.py:675
  24.6 10.7 %copy-start.9 = (f32[2,192,2048]{2,1,0:T(8,128)S(1)}, f32[2,192,2048]{2,1,0:T(8,128)}, u32[]{:S(2)}) copy-start(f32[2,192,2048]{2,1,0:T(8,128)} %filter_ref.1) | copy-start | bytes 9437188
  27.6 47.0 %collective-permute-start.3 = (bf16[2,96,2048]{2,1,0:T(8,128)(2,1)}, bf16[2,96,2048]{2,1,0:T(8,128)(2,1)}, u32[]{:S(2)}, u32[]{:S(2)}) collective-permute-start(bf16[2,96,2048]{2,1,0:T(8,128)(2,1)} %shard_map.94), channel_id=1, source_target_pairs={{0,252},{4,248},{8,244},{12,240},{16,236},{20,232},{24,228},{28,22... | collective-permute-start | bytes 2359304 | tf_op jit(solution)/shard_map/ppermute | solution.py:634
  36.1 6.8 %collective-permute-start.4 = (bf16[2,96,64]{2,1,0:T(8,128)(2,1)S(1)}, bf16[2,96,64]{2,1,0:T(8,128)(2,1)S(1)}, u32[]{:S(2)}, u32[]{:S(2)}) collective-permute-start(bf16[2,96,64]{2,1,0:T(8,128)(2,1)S(1)} %get-tuple-element.82), channel_id=1, source_target_pairs={{128,0},{252,4},{248,8},{244,12},{240,16},{236,20},{232,24},{228,2... | collective-permute-start | bytes 73736 | tf_op jit(solution)/shard_map/ppermute | solution.py:646
  37.4 5.5 %collective-permute-start.5 = (bf16[2,96,64]{2,1,0:T(8,128)(2,1)S(1)}, bf16[2,96,64]{2,1,0:T(8,128)(2,1)S(1)}, u32[]{:S(2)}, u32[]{:S(2)}) collective-permute-start(bf16[2,96,64]{2,1,0:T(8,128)(2,1)S(1)} %get-tuple-element.81), channel_id=1, source_target_pairs={{128,252},{132,128},{136,132},{140,136},{144,140},{148,144},{152,1... | collective-permute-start | bytes 73736 | tf_op jit(solution)/shard_map/ppermute | solution.py:647
  38.1 60.4 %copy-start.4 = (bf16[1,36864]{1,0:T(2,128)(2,1)S(1)}, bf16[1,36864]{1,0:T(2,128)(2,1)}, u32[]{:S(2)}) copy-start(bf16[1,36864]{1,0:T(2,128)(2,1)} %mix_in_ref) | copy-start | bytes 221188
  39.6 79.8 %copy-start.6 = (f32[192]{0:T(256)S(1)}, f32[192]{0:T(256)}, u32[]{:S(2)}) copy-start(f32[192]{0:T(256)} %param.11) | copy-start | bytes 2308
  39.7 79.8 %copy-start.7 = (f32[192]{0:T(256)S(1)}, f32[192]{0:T(256)}, u32[]{:S(2)}) copy-start(f32[192]{0:T(256)} %param.13) | copy-start | bytes 2308
  84.4 35.1 %all-to-all-start.1 = ((bf16[64,48,128]{2,1,0:T(8,128)(2,1)}), bf16[64,48,128]{2,1,0:T(8,128)(2,1)S(1)}, u32[]{:S(2)}, u32[]{:S(2)}) async-start(bf16[64,48,128]{2,1,0:T(8,128)(2,1)} %shard_map.95), calls=%async_computation.1 | async-start | bytes 1572864 | tf_op jit(solution)/shard_map/all_to_all | solution.py:704
  98.5 1.1 copy-start.2
  99.6 1.1 copy-start.3
  100.6 0.9 copy-start.5
  123.5 12.8 %collective-permute-start.12 = (bf16[56,1024]{1,0:T(8,128)(2,1)S(1)}, bf16[56,1024]{1,0:T(8,128)(2,1)S(1)}, u32[]{:S(2)}, u32[]{:S(2)}) collective-permute-start(bf16[56,1024]{1,0:T(8,128)(2,1)S(1)} %get-tuple-element.73), channel_id=1, source_target_pairs={{0,1},{1,0},{2,3},{3,2},{4,5},{5,4},{6,7},{7,6},{8,9},{9,8},{10,11... | collective-permute-start | bytes 344072 | tf_op jit(solution)/shard_map/ppermute | solution.py:605
  128.6 8.1 %collective-permute-start.13 = (bf16[56,1024]{1,0:T(8,128)(2,1)S(1)}, bf16[56,1024]{1,0:T(8,128)(2,1)S(1)}, u32[]{:S(2)}, u32[]{:S(2)}) collective-permute-start(bf16[56,1024]{1,0:T(8,128)(2,1)S(1)} %get-tuple-element.74), channel_id=1, source_target_pairs={{0,2},{1,3},{2,0},{3,1},{4,6},{5,7},{6,4},{7,5},{8,10},{9,11},{10,... | collective-permute-start | bytes 344072 | tf_op jit(solution)/shard_map/ppermute | solution.py:605
  130.7 6.0 %collective-permute-start.14 = (bf16[56,1024]{1,0:T(8,128)(2,1)S(1)}, bf16[56,1024]{1,0:T(8,128)(2,1)S(1)}, u32[]{:S(2)}, u32[]{:S(2)}) collective-permute-start(bf16[56,1024]{1,0:T(8,128)(2,1)S(1)} %get-tuple-element.75), channel_id=1, source_target_pairs={{0,3},{1,2},{2,1},{3,0},{4,7},{5,6},{6,5},{7,4},{8,11},{9,10},{10,... | collective-permute-start | bytes 344072 | tf_op jit(solution)/shard_map/ppermute | solution.py:605
  134.4 6.3 %collective-permute-start.6 = (bf16[56,1024]{1,0:T(8,128)(2,1)S(1)}, bf16[56,1024]{1,0:T(8,128)(2,1)S(1)}, u32[]{:S(2)}, u32[]{:S(2)}) collective-permute-start(bf16[56,1024]{1,0:T(8,128)(2,1)S(1)} %get-tuple-element.61), channel_id=1, source_target_pairs={{0,1},{1,0},{2,3},{3,2},{4,5},{5,4},{6,7},{7,6},{8,9},{9,8},{10,11... | collective-permute-start | bytes 344072 | tf_op jit(solution)/shard_map/ppermute | solution.py:605
  134.8 6.3 %collective-permute-start.7 = (bf16[56,1024]{1,0:T(8,128)(2,1)S(1)}, bf16[56,1024]{1,0:T(8,128)(2,1)S(1)}, u32[]{:S(2)}, u32[]{:S(2)}) collective-permute-start(bf16[56,1024]{1,0:T(8,128)(2,1)S(1)} %get-tuple-element.62), channel_id=1, source_target_pairs={{0,2},{1,3},{2,0},{3,1},{4,6},{5,7},{6,4},{7,5},{8,10},{9,11},{10,... | collective-permute-start | bytes 344072 | tf_op jit(solution)/shard_map/ppermute | solution.py:605
  136.3 6.3 %collective-permute-start.8 = (bf16[56,1024]{1,0:T(8,128)(2,1)S(1)}, bf16[56,1024]{1,0:T(8,128)(2,1)S(1)}, u32[]{:S(2)}, u32[]{:S(2)}) collective-permute-start(bf16[56,1024]{1,0:T(8,128)(2,1)S(1)} %get-tuple-element.63), channel_id=1, source_target_pairs={{0,3},{1,2},{2,1},{3,0},{4,7},{5,6},{6,5},{7,4},{8,11},{9,10},{10,... | collective-permute-start | bytes 344072 | tf_op jit(solution)/shard_map/ppermute | solution.py:605
  138.9 7.7 %collective-permute-start.15 = (bf16[48,1024]{1,0:T(8,128)(2,1)S(1)}, bf16[48,1024]{1,0:T(8,128)(2,1)S(1)}, u32[]{:S(2)}, u32[]{:S(2)}) collective-permute-start(bf16[48,1024]{1,0:T(8,128)(2,1)S(1)} %get-tuple-element.77), channel_id=1, source_target_pairs={{0,1},{1,0},{2,3},{3,2},{4,5},{5,4},{6,7},{7,6},{8,9},{9,8},{10,11... | collective-permute-start | bytes 294920 | tf_op jit(solution)/shard_map/ppermute | solution.py:605
  139.3 7.7 %collective-permute-start.16 = (bf16[48,1024]{1,0:T(8,128)(2,1)S(1)}, bf16[48,1024]{1,0:T(8,128)(2,1)S(1)}, u32[]{:S(2)}, u32[]{:S(2)}) collective-permute-start(bf16[48,1024]{1,0:T(8,128)(2,1)S(1)} %get-tuple-element.78), channel_id=1, source_target_pairs={{0,2},{1,3},{2,0},{3,1},{4,6},{5,7},{6,4},{7,5},{8,10},{9,11},{10,... | collective-permute-start | bytes 294920 | tf_op jit(solution)/shard_map/ppermute | solution.py:605
  140.7 6.2 %collective-permute-start.17 = (bf16[48,1024]{1,0:T(8,128)(2,1)S(1)}, bf16[48,1024]{1,0:T(8,128)(2,1)S(1)}, u32[]{:S(2)}, u32[]{:S(2)}) collective-permute-start(bf16[48,1024]{1,0:T(8,128)(2,1)S(1)} %get-tuple-element.79), channel_id=1, source_target_pairs={{0,3},{1,2},{2,1},{3,0},{4,7},{5,6},{6,5},{7,4},{8,11},{9,10},{10,... | collective-permute-start | bytes 294920 | tf_op jit(solution)/shard_map/ppermute | solution.py:605
  144.8 4.6 %collective-permute-start.10 = (bf16[48,1024]{1,0:T(8,128)(2,1)S(1)}, bf16[48,1024]{1,0:T(8,128)(2,1)S(1)}, u32[]{:S(2)}, u32[]{:S(2)}) collective-permute-start(bf16[48,1024]{1,0:T(8,128)(2,1)S(1)} %get-tuple-element.68), channel_id=1, source_target_pairs={{0,2},{1,3},{2,0},{3,1},{4,6},{5,7},{6,4},{7,5},{8,10},{9,11},{10,... | collective-permute-start | bytes 294920 | tf_op jit(solution)/shard_map/ppermute | solution.py:605
  146.4 5.2 %collective-permute-start.11 = (bf16[48,1024]{1,0:T(8,128)(2,1)S(1)}, bf16[48,1024]{1,0:T(8,128)(2,1)S(1)}, u32[]{:S(2)}, u32[]{:S(2)}) collective-permute-start(bf16[48,1024]{1,0:T(8,128)(2,1)S(1)} %get-tuple-element.69), channel_id=1, source_target_pairs={{0,3},{1,2},{2,1},{3,0},{4,7},{5,6},{6,5},{7,4},{8,11},{9,10},{10,... | collective-permute-start | bytes 294920 | tf_op jit(solution)/shard_map/ppermute | solution.py:605
  146.5 5.0 %collective-permute-start.9 = (bf16[48,1024]{1,0:T(8,128)(2,1)S(1)}, bf16[48,1024]{1,0:T(8,128)(2,1)S(1)}, u32[]{:S(2)}, u32[]{:S(2)}) collective-permute-start(bf16[48,1024]{1,0:T(8,128)(2,1)S(1)} %get-tuple-element.67), channel_id=1, source_target_pairs={{0,1},{1,0},{2,3},{3,2},{4,5},{5,4},{6,7},{7,6},{8,9},{9,8},{10,11... | collective-permute-start | bytes 294920 | tf_op jit(solution)/shard_map/ppermute | solution.py:605

commit v3 on v2

--- a/solution.py
+++ b/solution.py
@@ -193,7 +193,7 @@
     return 2 * (lane % 16) + lane // 64, group
 
 
-def make_gains(flags, own_ref, got_ref, ca_ref, cb_ref, g_ref, g1_ref):
+def make_gains(flags, own_ref, got_ref, ca_ref, cb_ref, g_ref, lhs, prod):
     high = flags[0] == 1
     first = flags[1] == 1
     row = lax.broadcasted_iota(jnp.int32, (128, 128), 0)
@@ -224,34 +224,53 @@
         direct = jnp.where(high, got, own)
         other = jnp.where(high, own, got)
         for t in range(16):
-            pair = jnp.concatenate(
-                [direct[:, 128 * t : 128 * (t + 1)], other[:, 128 * (15 - t) : 128 * (16 - t)]],
-                axis=1,
+            rows = slice(HALF * t, HALF * (t + 1))
+            lhs[rows, 0:128] = direct[:, 128 * t : 128 * (t + 1)]
+            lhs[rows, 128:256] = other[:, 128 * (15 - t) : 128 * (16 - t)]
+        prod[...] = jnp.dot(lhs[...], maps, preferred_element_type=F32)
+        for t in range(16):
+            out = regroup(
+                [
+                    prod[HALF * t + w * QUART : HALF * t + (w + 1) * QUART, :]
+                    + extra[w * QUART : (w + 1) * QUART, 128 * t : 128 * (t + 1)]
+                    for w in range(4)
+                ]
             )
-            both = (
-                jnp.dot(pair, maps, preferred_element_type=F32)
-                + extra[:, 128 * t : 128 * (t + 1)]
-            )
-            out = regroup([both[w * QUART : (w + 1) * QUART] for w in range(4)])
             for v in range(4):
-                g_ref[part, 4 * t + v] = out[v]
+                g_ref[part, 4 * t + v, 0:QUART, :] = out[v]
 
     @pl.when(first)
     def _():
-        for part in range(2):
+        wide = [ca_ref[part].astype(F32) + cb_ref[part].astype(F32) for part in range(2)]
+        alone = None
+        for k in range(3):
             plain = jnp.concatenate(
                 [
-                    jnp.where((cfreq == 0) & (crow == 4 * t + cgroup), 1.0, 0.0)
+                    jnp.where((cfreq == 2 * k) & (crow == 4 * t + cgroup), 1.0, 0.0)
                     for t in range(16)
                 ],
                 axis=1,
             ).astype(BF16)
-            alone = jnp.dot(column(part), plain, preferred_element_type=F32)
+            rows = jnp.concatenate(
+                [
+                    wide[part][w * QUART + 8 * k : w * QUART + 8 * k + 8]
+                    for part in range(2)
+                    for w in range(4)
+                ],
+                axis=0,
+            ).astype(BF16)
+            more = jnp.dot(rows, plain, preferred_element_type=F32)
+            alone = more if alone is None else alone + more
+        for part in range(2):
             for t in range(16):
-                both = alone[:, 128 * t : 128 * (t + 1)]
-                out = regroup([both[w * QUART : (w + 1) * QUART] for w in range(4)])
+                out = regroup(
+                    [
+                        alone[32 * part + 8 * w : 32 * part + 8 * w + 8, 128 * t : 128 * (t + 1)]
+                        for w in range(4)
+                    ]
+                )
                 for v in range(4):
-                    g1_ref[part, 4 * t + v] = packed([out[v][8 * k : 8 * k + 8] for k in range(3)])
+                    g_ref[part, 4 * t + v, QUART:32, :] = out[v]
 
 
 def packed(tiles):
@@ -328,7 +347,7 @@
 
 def middle_kernel(
     flags, moved, own_ref, got, ca_ref, cb_ref, out_ref,
-    moved_ref, got_ref, g_ref, g1_ref, xs, a_ref, b_ref, t1, sems,
+    moved_ref, got_ref, g_ref, lhs, prod, xr_ref, xi_ref, a_ref, b_ref, sems,
 ):
     first = flags[1] == 1
     fetches = [
@@ -337,14 +356,16 @@
     ]
     for fetch in fetches:
         fetch.start()
-    freq, _ = lanes_of(8)
+    freq, _ = lanes_of(QUART)
     special = (freq == 0) & first
     fetches[0].wait()
-    make_gains(flags, own_ref, got_ref, ca_ref, cb_ref, g_ref, g1_ref)
+    make_gains(flags, own_ref, got_ref, ca_ref, cb_ref, g_ref, lhs, prod)
     fetches[1].wait()
 
     def widen(p, carry):
-        xs[p] = moved_ref[p].astype(F32)
+        both = moved_ref[p].astype(F32)
+        xr_ref[p, 0:QUART, :] = both[:QUART]
+        xi_ref[p, 0:QUART, :] = jnp.where(special, 0.0, both[QUART:])
         return carry
 
     lax.fori_loop(0, NSEQ, widen, 0, unroll=8)
@@ -354,43 +375,40 @@
 
     @pl.when(first)
     def _():
+        for p in range(NSEQ):
+            c, s = half_turn(p)
+            im = jnp.where(special, moved_ref[p].astype(F32)[QUART:], 0.0)
+            im = packed([im[8 * k : 8 * k + 8] for k in range(3)])
+            xr_ref[p, QUART:32, :] = im * c
+            xi_ref[p, QUART:32, :] = im * (-s)
+
+    def every(i, carry):
+        rows = pl.ds(pl.multiple_of(i * 8, 8), 8)
+
         def load(p):
+            return xr_ref[p, rows, :], xi_ref[p, rows, :]
+
+        def store(p, re, im):
+            xr_ref[p, rows, :] = re
+            xi_ref[p, rows, :] = im
+
+        across(load, store, lambda g: (g_ref[0, g, rows, :], g_ref[1, g, rows, :]), a_ref, b_ref)
+        return carry
+
+    lax.fori_loop(0, 3 + flags[1], every, 0)
+
+    @pl.when(first)
+    def _():
+        for p in range(NSEQ):
             c, s = half_turn(p)
-            im = packed(
-                [
-                    jnp.where(special, xs[p, QUART + 8 * k : QUART + 8 * k + 8, :], 0.0)
-                    for k in range(3)
-                ]
-            )
-            return im * c, im * (-s)
-
-        def store(p, re, im):
-            c, s = half_turn(p)
-            turned = re * c - im * s
-            t1[p, 0:8, :] = turned
-            t1[p, 8:16, :] = pltpu.roll(turned, 127, 1)
-            t1[p, 16:24, :] = pltpu.roll(turned, 126, 1)
-
-        across(load, store, lambda g: (g1_ref[0, g], g1_ref[1, g]), a_ref, b_ref)
-
-    def every(i, carry):
-        top = pl.ds(pl.multiple_of(i * 8, 8), 8)
-        bottom = pl.ds(pl.multiple_of(i * 8 + QUART, 8), 8)
-
-        def load(p):
-            return xs[p, top, :], jnp.where(special, 0.0, xs[p, bottom, :])
-
-        def store(p, re, im):
-            xs[p, top, :] = re
-            xs[p, bottom, :] = jnp.where(special, t1[p, top, :], im)
-
-        across(load, store, lambda g: (g_ref[0, g, top, :], g_ref[1, g, top, :]), a_ref, b_ref)
-        return carry
-
-    lax.fori_loop(0, 3, every, 0)
+            one = xr_ref[p, QUART:32, :] * c - xi_ref[p, QUART:32, :] * s
+            alone = jnp.concatenate([one, pltpu.roll(one, 127, 1), pltpu.roll(one, 126, 1)], axis=0)
+            xi_ref[p, 0:QUART, :] = jnp.where(special, alone, xi_ref[p, 0:QUART, :])
 
     def narrow(p, carry):
-        out_ref[p] = xs[p].astype(BF16)
+        out_ref[p] = jnp.concatenate(
+            [xr_ref[p, 0:QUART, :], xi_ref[p, 0:QUART, :]], axis=0
+        ).astype(BF16)
         return carry
 
     lax.fori_loop(0, NSEQ, narrow, 0, unroll=8)
@@ -404,20 +422,14 @@
 
 
 def tokens_back(
-    flags, values, w_ref, x_ref, normed_ref, skip_row, gain_row, mix_ref, mix_t_ref, res_ref, outs, tm, st,
+    flags, values, w_ref, x_ref, normed_ref, skip, gain, st_in, mix_t_ref, res_ref, outs, tm, st,
     fetches,
     chunk,
 ):
     me = flags[2]
-    skip = column_of(skip_row)
-    gain = column_of(gain_row)
-    st[...] = jnp.zeros((8, TC), F32)
-    weight = jnp.dot(
-        gain_row[...], mix_ref[...].astype(F32), preferred_element_type=F32,
-        precision=lax.Precision.HIGHEST,
-    )
-    for k, part in enumerate(in_three(weight)[:2]):
-        st[5 + k : 6 + k, 0:CH] = part.astype(F32)
+    skip = skip[...]
+    gain = gain[...]
+    st[...] = st_in[...]
     for n in range(TC // 512):
         mine = slice(256 * n, 256 * (n + 1))
         fetches[n].wait()
@@ -467,7 +479,7 @@
 
 
 def back_first_kernel(
-    flags, got_ref, w_hbm, x_ref, normed_ref, skip_row, gain_row, mix_ref, mix_t_ref,
+    flags, got_ref, w_hbm, x_ref, normed_ref, skip_ref, gain_ref, st_in, mix_t_ref,
     values_ref, res_ref, u0, u1, u2, u3, tall, tm, st, w_ref, sems,
 ):
     fetches = fetch_table(w_hbm, w_ref, sems, 0)
@@ -486,18 +498,18 @@
     values = tall[...].astype(BF16)
     values_ref[...] = values
     tokens_back(
-        flags, values_ref[...], w_ref, x_ref, normed_ref, skip_row, gain_row, mix_ref, mix_t_ref, res_ref,
+        flags, values_ref[...], w_ref, x_ref, normed_ref, skip_ref, gain_ref, st_in, mix_t_ref, res_ref,
         (u0, u1, u2, u3), tm, st, fetches, 0,
     )
 
 
 def back_second_kernel(
-    flags, values_ref, w_hbm, x_ref, normed_ref, skip_row, gain_row, mix_ref, mix_t_ref,
+    flags, values_ref, w_hbm, x_ref, normed_ref, skip_ref, gain_ref, st_in, mix_t_ref,
     res_ref, u0, u1, u2, u3, tm, st, w_ref, sems,
 ):
     fetches = fetch_table(w_hbm, w_ref, sems, 1)
     tokens_back(
-        flags, values_ref[...], w_ref, x_ref, normed_ref, skip_row, gain_row, mix_ref, mix_t_ref, res_ref,
+        flags, values_ref[...], w_ref, x_ref, normed_ref, skip_ref, gain_ref, st_in, mix_t_ref, res_ref,
         (u0, u1, u2, u3), tm, st, fetches, 1,
     )
 
@@ -534,9 +546,10 @@
         o[...] = low_ref[pl.ds(pl.multiple_of((me ^ k) * PIECE, PIECE), PIECE), :].astype(BF16)
 
 
-def weights_kernel(
-    mix_in_ref, up_ref, down_ref, mix_out_ref, in_ref, in_t, up_t, down_t, out_t, square, wide, tall
-):
+def up_kernel(skip_row, gain_row, mix_in_ref, up_ref, skip_ref, gain_ref, st_ref, in_t, up_t, square, wide):
+    skip_ref[...] = column_of(skip_row)
+    gain_ref[...] = column_of(gain_row)
+
     def unroll(src, dst, rows, cols):
         def step(i, carry):
             for k in range(8):
@@ -549,11 +562,19 @@
 
     unroll(up_ref, wide, CH, HID)
     up_t[...] = wide[...].T.astype(BF16)
-    for src, dst in ((mix_in_ref, in_t), (mix_out_ref, out_t)):
-        paired(src, square, CH)
-        if dst is in_t:
-            in_ref[...] = square[...].astype(BF16)
-        dst[...] = square[...].T.astype(BF16)
+    paired(mix_in_ref, square, CH)
+    in_t[...] = square[...].T.astype(BF16)
+    st_ref[...] = jnp.zeros((8, TC), F32)
+    weight = jnp.dot(
+        gain_row[...], square[...], preferred_element_type=F32, precision=lax.Precision.HIGHEST
+    )
+    for k, part in enumerate(in_three(weight)[:2]):
+        st_ref[5 + k : 6 + k, 0:CH] = part.astype(F32)
+
+
+def down_kernel(down_ref, mix_out_ref, down_t, out_t, square, tall):
+    paired(mix_out_ref, square, CH)
+    out_t[...] = square[...].T.astype(BF16)
     paired(down_ref, tall, HID)
     down_t[...] = tall[...].T.astype(BF16)
 
@@ -673,6 +694,18 @@
         mib=20,
     )(tokens, sums, *others, norm_gain, table)
     moved = lax.all_to_all(send, "seq", split_axis=0, concat_axis=0, tiled=True)
+    skip_col, gain_col, st_in, mix_in_t, up_t = call(
+        up_kernel,
+        (
+            shape((CH, 1), F32), shape((CH, 1), F32), shape((8, TC), F32), shape((CH, CH), BF16),
+            shape((HID, CH), BF16),
+        ),
+        "vvvv",
+        scratch=[pltpu.VMEM((CH, CH), F32), pltpu.VMEM((CH, HID), F32)],
+    )(skip_weight, mlp_gain, mix_in, up_weight)
+    moved, skip_col, gain_col, st_in, mix_in_t, up_t = lax.optimization_barrier(
+        (moved, skip_col, gain_col, st_in, mix_in_t, up_t)
+    )
     back = call(
         middle_kernel,
         shape((NSEQ, 2 * QUART, 128), BF16),
@@ -680,31 +713,25 @@
         scratch=[
             pltpu.VMEM((NSEQ, 2 * QUART, 128), BF16),
             pltpu.VMEM((2, HALF, TOK), BF16),
-            pltpu.VMEM((2, NSEQ, QUART, 128), F32),
-            pltpu.VMEM((2, NSEQ, 8, 128), F32),
-            pltpu.VMEM((NSEQ, 2 * QUART, 128), F32),
+            pltpu.VMEM((2, NSEQ, 32, 128), F32),
+            pltpu.VMEM((16 * HALF, 256), BF16),
+            pltpu.VMEM((16 * HALF, 128), F32),
+            pltpu.VMEM((NSEQ, 32, 128), F32),
+            pltpu.VMEM((NSEQ, 32, 128), F32),
             pltpu.VMEM((2, NSEQ, 8, 128), F32),
             pltpu.VMEM((2, NSEQ, 8, 128), F32),
-            pltpu.VMEM((NSEQ, QUART, 128), F32),
             pltpu.SemaphoreType.DMA((2,)),
         ],
     )(flags, in_hbm(moved), own, in_hbm(got), ca, cb)
-    back, mix_in, up_weight, down_weight, mix_out = lax.optimization_barrier(
-        (back, mix_in, up_weight, down_weight, mix_out)
-    )
-    mix_in_full, mix_in_t, up_t, down_t, mix_out_t = call(
-        weights_kernel,
-        (
-            shape((CH, CH), BF16), shape((CH, CH), BF16), shape((HID, CH), BF16),
-            shape((CH, HID), BF16), shape((CH, CH), BF16),
-        ),
-        "vvvv",
-        scratch=[pltpu.VMEM((CH, CH), F32), pltpu.VMEM((CH, HID), F32), pltpu.VMEM((HID, CH), F32)],
-    )(mix_in, up_weight, down_weight, mix_out)
+    back, down_weight, mix_out = lax.optimization_barrier((back, down_weight, mix_out))
+    down_t, mix_out_t = call(
+        down_kernel,
+        (shape((CH, HID), BF16), shape((CH, CH), BF16)),
+        "vv",
+        scratch=[pltpu.VMEM((CH, CH), F32), pltpu.VMEM((HID, CH), F32)],
+    )(down_weight, mix_out)
     home = lax.all_to_all(back, "seq", split_axis=0, concat_axis=0, tiled=True)
-    home, mix_in_full, mix_in_t, down_t, up_t, mix_out_t = lax.optimization_barrier(
-        (home, mix_in_full, mix_in_t, down_t, up_t, mix_out_t)
-    )
+    home, down_t, mix_out_t = lax.optimization_barrier((home, down_t, mix_out_t))
     piece = (shape((CH, TC), BF16),) + (shape((ROWS, TC), BF16),) * 4
     small = [
         pltpu.VMEM((CH, TC), F32),
@@ -712,7 +739,7 @@
         pltpu.VMEM((TC // 2, TOK), BF16),
         pltpu.SemaphoreType.DMA((TC // 512,)),
     ]
-    rest = (in_hbm(kept), tokens, normed, skip_weight, mlp_gain, mix_in_full, mix_in_t)
+    rest = (in_hbm(kept), tokens, normed, skip_col, gain_col, st_in, mix_in_t)
     values, res_a, *first_a = call(
         back_first_kernel, (shape((CH, TOK), BF16),) + piece, "svhvvvvvv",
         scratch=[pltpu.VMEM((CH, TOK), F32)] + small, mib=20,

time: 154 us -> 153 us (level)
  starting transfers between devices: 55.4 us -> 53.4 us
  local copies, waits for them, and re-layouts: 5.88 us -> 7.57 us
    all_to_all x1, waiting for transfers between devices: 5.6 us -> 12.7 us  [block(): home = lax.all_to_all(back, 'seq', split_axis=0, concat_axis=0, tiled=True)]
    ppermute x1, waiting for transfers between devices: 31.8 us -> 25.9 us  [block(): got = lax.ppermute(give, 'seq', [(i, 63 - i) for i in range(64)])]
    ppermute x15, starting transfers between devices: 18.8 us -> 15.5 us  [swap(): return lax.ppermute(x, 'chan', [(i, i ^ k) for i in range(4)])]
    ppermute x1, waiting for transfers between devices: 3.21 us -> 0.01 us  [block(): lax.ppermute(column[:, :HALF], 'seq', [(32, 0)] + [(64 - i, i) for i in r...]
    all_to_all x1, waiting for transfers between devices: 0.01 us -> 2.68 us  [block(): moved = lax.all_to_all(send, 'seq', split_axis=0, concat_axis=0, tiled=True)]
    pallas_call x1, Pallas kernels: 9.69 us -> 7.35 us  [block(): call(middle_kernel, shape((NSEQ, 2 * QUART, 128), BF16), 'shvhvv', scratc...]
    unnamed x20 -> x28, local copies, waits for them, and re-layouts: 4.2 us -> 5.3 us
    pallas_call x1 -> x2, Pallas kernels: 12.3 us -> 12.6 us  [the longest x1 9.64 us: block(): call(down_kernel, (shape((CH, HID), BF16), shape((CH, CH), BF16)), 'vv',...]
  transfers between devices with their start and end apart: 20 -> 20, of which waited for: 6 -> 6; matrix products, arithmetic and copies ran while one was open for 2% -> 3% of each run, Pallas kernels for 17% -> 17%
where the time goes in v3:
time: 153 us; the launch traced here: 152 us
  starting transfers between devices  53.4 us (35%)
  waiting for transfers between devices  46.5 us (30%)
  Pallas kernels  42.7 us (28%)
  local copies, waits for them, and re-layouts  7.57 us (5%)
    ppermute x1, waiting for transfers between devices, block(): got = lax.ppermute(give, 'seq', [(i, 63 - i) for i in range(64)])  25.9 us
    ppermute x15, starting transfers between devices, swap(): return lax.ppermute(x, 'chan', [(i, i ^ k) for i in range(4)])  15.5 us
    all_to_all x1, starting transfers between devices, block(): home = lax.all_to_all(back, 'seq', split_axis=0, concat_axis=0, tiled=True)  14.8 us
    all_to_all x1, starting transfers between devices, block(): moved = lax.all_to_all(send, 'seq', split_axis=0, concat_axis=0, tiled=True)  12.8 us
    all_to_all x1, waiting for transfers between devices, block(): home = lax.all_to_all(back, 'seq', split_axis=0, concat_axis=0, tiled=True)  12.7 us
    pallas_call x1, Pallas kernels, block(): call(down_kernel, (shape((CH, HID), BF16), shape((CH, CH), BF16)), 'vv',...  9.64 us
    ppermute x1, starting transfers between devices, block(): got = lax.ppermute(give, 'seq', [(i, 63 - i) for i in range(64)])  7.67 us
    pallas_call x1, Pallas kernels, block(): call(middle_kernel, shape((NSEQ, 2 * QUART, 128), BF16), 'shvhvv', scratc...  7.35 us
  transfers between devices with their start and end apart: 20, of which 6 were waited for; matrix products, arithmetic and copies ran while one was open for 3% of the time, Pallas kernels for 17%

profile of v3, /device:TPU:1, one launch (start us, length us, event | category | flops | bytes accessed | tf_op | source)
XLA Modules:
  0.0 152.1 jit_solution(12443993408171097848)
XLA Ops:
  0.0 1.1 copy-done
  1.3 3.3 %collective-permute-start = (f32[2,2048]{1,0:T(2,128)S(1)}, f32[2,2048]{1,0:T(2,128)S(1)}, u32[]{:S(2)}, u32[]{:S(2)}) collective-permute-start(f32[2,2048]{1,0:T(2,128)S(1)} %shard_map.91.s0), channel_id=1, source_target_pairs={{0,1},{1,0},{2,3},{3,2},{4,5},{5,4},{6,7},{7,6},{8,9},{9,8},{10,11... | collective-permute-start | bytes 49160 | tf_op jit(solution)/shard_map/ppermute | solution.py:626
  4.6 1.7 %collective-permute-start.2 = (f32[2,2048]{1,0:T(2,128)S(1)}, f32[2,2048]{1,0:T(2,128)S(1)}, u32[]{:S(2)}, u32[]{:S(2)}) collective-permute-start(f32[2,2048]{1,0:T(2,128)S(1)} %shard_map.91.s0), channel_id=1, source_target_pairs={{0,3},{1,2},{2,1},{3,0},{4,7},{5,6},{6,5},{7,4},{8,11},{9,10},{10,... | collective-permute-start | bytes 49160 | tf_op jit(solution)/shard_map/ppermute | solution.py:626
  7.3 1.5 shard_map.92.w_ref
  8.8 2.9 %shard_map.93 = (bf16[64,48,128]{2,1,0:T(8,128)(2,1)}, bf16[192,2048]{1,0:T(8,128)(2,1)S(1)}, bf16[1024,2048]{1,0:T(8,128)(2,1)}) custom-call(bf16[192,2048]{1,0:T(8,128)(2,1)S(1)} %copy-done.1, f32[2,2048]{1,0:T(2,128)S(1)} %shard_map.91.s0, f32[2,2048]{1,0:T(2,128)S(1)} %collective-permute-done.s1, f32[2,2048]{1,0:T(2,128)S(1)} %collective-permute-done.1.s2, ...), custom_call_target="tpu_custom_call" | custom-call | tf_op jit(solution)/shard_map/pallas_call | solution.py:684
  11.7 12.8 %all-to-all-start = ((bf16[64,48,128]{2,1,0:T(8,128)(2,1)}), bf16[64,48,128]{2,1,0:T(8,128)(2,1)}, u32[]{:S(2)}, u32[]{:S(2)}) async-start(bf16[64,48,128]{2,1,0:T(8,128)(2,1)} %get-tuple-element.46), calls=%async_computation | async-start | bytes 1572864 | tf_op jit(solution)/shard_map/all_to_all | solution.py:696
  24.6 3.0 %shard_map.95 = bf16[2,96,2048]{2,1,0:T(8,128)(2,1)} custom-call(s32[4]{0:T(128)S(1)} %pad_add_fusion.flags, f32[2,192,2048]{2,1,0:T(8,128)} %filter_ref.1), custom_call_target="tpu_custom_call" | custom-call | tf_op jit(solution)/shard_map/pallas_call | solution.py:647
  27.7 7.7 %collective-permute-start.3 = (bf16[2,96,2048]{2,1,0:T(8,128)(2,1)}, bf16[2,96,2048]{2,1,0:T(8,128)(2,1)}, u32[]{:S(2)}, u32[]{:S(2)}) collective-permute-start(bf16[2,96,2048]{2,1,0:T(8,128)(2,1)} %shard_map.95), channel_id=1, source_target_pairs={{0,252},{4,248},{8,244},{12,240},{16,236},{20,232},{24,228},{28,22... | collective-permute-start | bytes 2359304 | tf_op jit(solution)/shard_map/ppermute | solution.py:655
  36.8 1.3 collective-permute-start.4
  38.1 1.3 collective-permute-start.5
  39.3 1.5 dynamic-slice_convert_fusion.own_ref
  41.8 3.0 %shard_map.94 = (f32[192,1]{1,0:T(8,128)S(1)}, f32[192,1]{1,0:T(8,128)S(1)}, f32[8,1024]{1,0:T(8,128)S(1)}, bf16[192,192]{1,0:T(8,128)(2,1)S(1)}, bf16[768,192]{1,0:T(8,128)(2,1)S(1)}) custom-call(f32[1,192]{1,0:T(1,128)S(1)} %bitcast.11, f32[1,192]{1,0:T(1,128)S(1)} %bitcast.12, bf16[1,36864]{1,0:T(2,128)(2,1)S(1)} %copy-done.6, bf16[1,147456]{1,0:T(2,128)(2,1)S(1)} %copy-done.2), custom_call_target="tpu_custom_call" | custom-call | tf_op jit(solution)/shard_map/pallas_call | solution.py:697
  46.1 2.7 %all-to-all-done.moved = bf16[64,48,128]{2,1,0:T(8,128)(2,1)} async-done(((bf16[64,48,128]{2,1,0:T(8,128)(2,1)}), bf16[64,48,128]{2,1,0:T(8,128)(2,1)}, u32[]{:S(2)}, u32[]{:S(2)}) %all-to-all-start) | async-done | bytes 786464 | tf_op jit(solution)/shard_map/all_to_all | solution.py:696
  48.7 25.9 %collective-permute-done.3.got = bf16[2,96,2048]{2,1,0:T(8,128)(2,1)} collective-permute-done((bf16[2,96,2048]{2,1,0:T(8,128)(2,1)}, bf16[2,96,2048]{2,1,0:T(8,128)(2,1)}, u32[]{:S(2)}, u32[]{:S(2)}) %collective-permute-start.3) | collective-permute-done | bytes 786464 | tf_op jit(solution)/shard_map/ppermute | solution.py:655
  74.6 7.3 %shard_map.96 = bf16[64,48,128]{2,1,0:T(8,128)(2,1)} custom-call(s32[4]{0:T(128)S(1)} %pad_add_fusion.flags, bf16[64,48,128]{2,1,0:T(8,128)(2,1)} %all-to-all-done.moved, bf16[2,96,2048]{2,1,0:T(8,128)(2,1)S(1)} %dynamic-slice_convert_fusion.own_ref, bf16[2,96,2048]{2,1,0:T(8,128)(2,1)} %collective-permute-done.3.got, ...), custom_call_target="tpu_custom_call" | custom-call | tf_op jit(solution)/shard_map/pallas_call | solution.py:709
  82.0 14.8 %all-to-all-start.1 = ((bf16[64,48,128]{2,1,0:T(8,128)(2,1)}), bf16[64,48,128]{2,1,0:T(8,128)(2,1)S(1)}, u32[]{:S(2)}, u32[]{:S(2)}) async-start(bf16[64,48,128]{2,1,0:T(8,128)(2,1)} %shard_map.96), calls=%async_computation.1 | async-start | bytes 1572864 | tf_op jit(solution)/shard_map/all_to_all | solution.py:733
  96.8 1.1 copy-done.3
  98.8 9.6 %shard_map.97 = (bf16[192,768]{1,0:T(8,128)(2,1)S(1)}, bf16[192,192]{1,0:T(8,128)(2,1)S(1)}) custom-call(bf16[1,147456]{1,0:T(2,128)(2,1)S(1)} %copy-done.3, bf16[1,36864]{1,0:T(2,128)(2,1)S(1)} %copy-done.7), custom_call_target="tpu_custom_call" | custom-call | tf_op jit(solution)/shard_map/pallas_call | solution.py:727
  108.4 12.7 %all-to-all-done.1.got_ref = bf16[64,48,128]{2,1,0:T(8,128)(2,1)S(1)} async-done(((bf16[64,48,128]{2,1,0:T(8,128)(2,1)}), bf16[64,48,128]{2,1,0:T(8,128)(2,1)S(1)}, u32[]{:S(2)}, u32[]{:S(2)}) %all-to-all-start.1) | async-done | bytes 786464 | tf_op jit(solution)/shard_map/all_to_all | solution.py:733
  121.2 4.8 %shard_map.98 = (bf16[192,2048]{1,0:T(8,128)(2,1)S(1)}, bf16[192,1024]{1,0:T(8,128)(2,1)S(1)}, bf16[56,1024]{1,0:T(8,128)(2,1)S(1)}, bf16[56,1024]{1,0:T(8,128)(...) custom-call(s32[4]{0:T(128)S(1)} %pad_add_fusion.flags, ...), custom_call_target="tpu_custom_call" | custom-call | tf_op jit(solution)/shard_map/pallas_call | solution.py:743
  126.0 2.4 %collective-permute-start.12 = (bf16[56,1024]{1,0:T(8,128)(2,1)S(1)}, bf16[56,1024]{1,0:T(8,128)(2,1)S(1)}, u32[]{:S(2)}, u32[]{:S(2)}) collective-permute-start(bf16[56,1024]{1,0:T(8,128)(2,1)S(1)} %get-tuple-element.79), channel_id=1, source_target_pairs={{0,1},{1,0},{2,3},{3,2},{4,5},{5,4},{6,7},{7,6},{8,9},{9,8},{10,11... | collective-permute-start | bytes 344072 | tf_op jit(solution)/shard_map/ppermute | solution.py:626
  128.3 1.7 %collective-permute-start.14 = (bf16[56,1024]{1,0:T(8,128)(2,1)S(1)}, bf16[56,1024]{1,0:T(8,128)(2,1)S(1)}, u32[]{:S(2)}, u32[]{:S(2)}) collective-permute-start(bf16[56,1024]{1,0:T(8,128)(2,1)S(1)} %get-tuple-element.81), channel_id=1, source_target_pairs={{0,3},{1,2},{2,1},{3,0},{4,7},{5,6},{6,5},{7,4},{8,11},{9,10},{10,... | collective-permute-start | bytes 344072 | tf_op jit(solution)/shard_map/ppermute | solution.py:626
  130.1 3.5 %shard_map.99 = (bf16[192,1024]{1,0:T(8,128)(2,1)S(1)}, bf16[56,1024]{1,0:T(8,128)(2,1)S(1)}, bf16[56,1024]{1,0:T(8,128)(2,1)S(1)}, bf16[56,1024]{1,0:T(8,128)(2,1)S(1)}, bf16[56,1024]{1,0:T(8,128)(2,1)S(1)}) custom-call(s32[4]{0:T(128)S(1)} %pad_add_fusion.flags, bf16[192,2048]{1,0:T(8,128)(2,1)S(1)} %get-tuple-element.65.values_ref, ...), custom_call_target="tpu_custom_call" | custom-call | tf_op jit(solution)/shard_map/pallas_call | solution.py:748
  133.8 2.0 %collective-permute-start.8 = (bf16[56,1024]{1,0:T(8,128)(2,1)S(1)}, bf16[56,1024]{1,0:T(8,128)(2,1)S(1)}, u32[]{:S(2)}, u32[]{:S(2)}) collective-permute-start(bf16[56,1024]{1,0:T(8,128)(2,1)S(1)} %get-tuple-element.69), channel_id=1, source_target_pairs={{0,3},{1,2},{2,1},{3,0},{4,7},{5,6},{6,5},{7,4},{8,11},{9,10},{10,... | collective-permute-start | bytes 344072 | tf_op jit(solution)/shard_map/ppermute | solution.py:626
  135.8 2.2 %shard_map.101 = (bf16[48,1024]{1,0:T(8,128)(2,1)S(1)}, bf16[48,1024]{1,0:T(8,128)(2,1)S(1)}, bf16[48,1024]{1,0:T(8,128)(2,1)S(1)}, bf16[48,1024]{1,0:T(8,128)(2,1)S(1)}) custom-call(s32[4]{0:T(128)S(1)} %pad_add_fusion.flags, bf16[56,1024]{1,0:T(8,128)(2,1)S(1)} %get-tuple-element.78.p0, bf16[56,1024]{1,0:T(8,128)(2,1)S(1)} %collective-permute-done.12.p1, ...), custom_call_target="tpu_custom_call" | custom-call | tf_op jit(solution)/shard_map/pallas_call | solution.py:754
  138.3 1.9 %collective-permute-start.17 = (bf16[48,1024]{1,0:T(8,128)(2,1)S(1)}, bf16[48,1024]{1,0:T(8,128)(2,1)S(1)}, u32[]{:S(2)}, u32[]{:S(2)}) collective-permute-start(bf16[48,1024]{1,0:T(8,128)(2,1)S(1)} %get-tuple-element.85), channel_id=1, source_target_pairs={{0,3},{1,2},{2,1},{3,0},{4,7},{5,6},{6,5},{7,4},{8,11},{9,10},{10,... | collective-permute-start | bytes 294920 | tf_op jit(solution)/shard_map/ppermute | solution.py:626
  140.2 1.4 collective-permute-done.8.p3
  141.6 2.2 %shard_map.100 = (bf16[48,1024]{1,0:T(8,128)(2,1)S(1)}, bf16[48,1024]{1,0:T(8,128)(2,1)S(1)}, bf16[48,1024]{1,0:T(8,128)(2,1)S(1)}, bf16[48,1024]{1,0:T(8,128)(2,1)S(1)}) custom-call(s32[4]{0:T(128)S(1)} %pad_add_fusion.flags, bf16[56,1024]{1,0:T(8,128)(2,1)S(1)} %get-tuple-element.66.p0, bf16[56,1024]{1,0:T(8,128)(2,1)S(1)} %collective-permute-done.6.p1, ...), custom_call_target="tpu_custom_call" | custom-call | tf_op jit(solution)/shard_map/pallas_call | solution.py:754
  143.9 0.9 collective-permute-start.11
  146.6 1.8 %collective-permute-done.10.p2 = bf16[48,1024]{1,0:T(8,128)(2,1)S(1)} collective-permute-done((bf16[48,1024]{1,0:T(8,128)(2,1)S(1)}, bf16[48,1024]{1,0:T(8,128)(2,1)S(1)}, u32[]{:S(2)}, u32[]{:S(2)}) %collective-permute-start.10) | collective-permute-done | bytes 98336 | tf_op jit(solution)/shard_map/ppermute | solution.py:626
  148.4 2.0 %collective-permute-done.11.p3 = bf16[48,1024]{1,0:T(8,128)(2,1)S(1)} collective-permute-done((bf16[48,1024]{1,0:T(8,128)(2,1)S(1)}, bf16[48,1024]{1,0:T(8,128)(2,1)S(1)}, u32[]{:S(2)}, u32[]{:S(2)}) %collective-permute-start.11) | collective-permute-done | bytes 98336 | tf_op jit(solution)/shard_map/ppermute | solution.py:626
  150.4 1.7 %shard_map.103 = bf16[192,2048]{1,0:T(8,128)(2,1)} custom-call(s32[4]{0:T(128)S(1)} %pad_add_fusion.flags, bf16[48,1024]{1,0:T(8,128)(2,1)S(1)} %get-tuple-element.72.p0, bf16[48,1024]{1,0:T(8,128)(2,1)S(1)} %collective-permute-done.9.p1, bf16[48,1024]{1,0:T(8,128)(2,1)S(1)} %collective-permute-done.10.p2, bf16[48,1024]{1,0:T(8,128)(2,1)S(1)} %collective-permute-done.11.p3, ...), custom_call_target="tpu_custom_call" | custom-call | tf_op jit(solution)/shard_map/pallas_call | solution.py:767
  (65 shorter events, 8.1 us)
Async XLA Ops:
  0.0 1.1 copy-start
  1.1 7.7 %copy-start.1 = (bf16[192,2048]{1,0:T(8,128)(2,1)S(1)}, bf16[192,2048]{1,0:T(8,128)(2,1)}, u32[]{:S(2)}) copy-start(bf16[192,2048]{1,0:T(8,128)(2,1)} %x_ref.7) | copy-start | bytes 2359300
  1.1 7.7 %copy-start.12 = (f32[192]{0:T(256)S(1)}, f32[192]{0:T(256)}, u32[]{:S(2)}) copy-start(f32[192]{0:T(256)} %param.12) | copy-start | bytes 2308
  1.3 7.5 %collective-permute-start = (f32[2,2048]{1,0:T(2,128)S(1)}, f32[2,2048]{1,0:T(2,128)S(1)}, u32[]{:S(2)}, u32[]{:S(2)}) collective-permute-start(f32[2,2048]{1,0:T(2,128)S(1)} %shard_map.91.s0), channel_id=1, source_target_pairs={{0,1},{1,0},{2,3},{3,2},{4,5},{5,4},{6,7},{7,6},{8,9},{9,8},{10,11... | collective-permute-start | bytes 49160 | tf_op jit(solution)/shard_map/ppermute | solution.py:626
  4.6 4.2 %collective-permute-start.1 = (f32[2,2048]{1,0:T(2,128)S(1)}, f32[2,2048]{1,0:T(2,128)S(1)}, u32[]{:S(2)}, u32[]{:S(2)}) collective-permute-start(f32[2,2048]{1,0:T(2,128)S(1)} %shard_map.91.s0), channel_id=1, source_target_pairs={{0,2},{1,3},{2,0},{3,1},{4,6},{5,7},{6,4},{7,5},{8,10},{9,11},{10,... | collective-permute-start | bytes 49160 | tf_op jit(solution)/shard_map/ppermute | solution.py:626
  4.6 4.2 %collective-permute-start.2 = (f32[2,2048]{1,0:T(2,128)S(1)}, f32[2,2048]{1,0:T(2,128)S(1)}, u32[]{:S(2)}, u32[]{:S(2)}) collective-permute-start(f32[2,2048]{1,0:T(2,128)S(1)} %shard_map.91.s0), channel_id=1, source_target_pairs={{0,3},{1,2},{2,1},{3,0},{4,7},{5,6},{6,5},{7,4},{8,11},{9,10},{10,... | collective-permute-start | bytes 49160 | tf_op jit(solution)/shard_map/ppermute | solution.py:626
  11.7 37.0 %all-to-all-start = ((bf16[64,48,128]{2,1,0:T(8,128)(2,1)}), bf16[64,48,128]{2,1,0:T(8,128)(2,1)}, u32[]{:S(2)}, u32[]{:S(2)}) async-start(bf16[64,48,128]{2,1,0:T(8,128)(2,1)} %get-tuple-element.46), calls=%async_computation | async-start | bytes 1572864 | tf_op jit(solution)/shard_map/all_to_all | solution.py:696
  24.5 10.8 %copy-start.13 = (f32[2,192,2048]{2,1,0:T(8,128)S(1)}, f32[2,192,2048]{2,1,0:T(8,128)}, u32[]{:S(2)}) copy-start(f32[2,192,2048]{2,1,0:T(8,128)} %filter_ref.1) | copy-start | bytes 9437188
  27.6 13.2 %copy-start.2 = (bf16[1,147456]{1,0:T(2,128)(2,1)S(1)}, bf16[1,147456]{1,0:T(2,128)(2,1)}, u32[]{:S(2)}) copy-start(bf16[1,147456]{1,0:T(2,128)(2,1)} %up_ref.1) | copy-start | bytes 884740
  27.6 13.2 %copy-start.10 = (f32[192]{0:T(256)S(1)}, f32[192]{0:T(256)}, u32[]{:S(2)}) copy-start(f32[192]{0:T(256)} %param.11) | copy-start | bytes 2308
  27.7 13.2 %copy-start.11 = (f32[192]{0:T(256)S(1)}, f32[192]{0:T(256)}, u32[]{:S(2)}) copy-start(f32[192]{0:T(256)} %param.13) | copy-start | bytes 2308
  27.7 47.0 %collective-permute-start.3 = (bf16[2,96,2048]{2,1,0:T(8,128)(2,1)}, bf16[2,96,2048]{2,1,0:T(8,128)(2,1)}, u32[]{:S(2)}, u32[]{:S(2)}) collective-permute-start(bf16[2,96,2048]{2,1,0:T(8,128)(2,1)} %shard_map.95), channel_id=1, source_target_pairs={{0,252},{4,248},{8,244},{12,240},{16,236},{20,232},{24,228},{28,22... | collective-permute-start | bytes 2359304 | tf_op jit(solution)/shard_map/ppermute | solution.py:655
  36.8 12.0 %collective-permute-start.4 = (bf16[2,96,64]{2,1,0:T(8,128)(2,1)}, bf16[2,96,64]{2,1,0:T(8,128)(2,1)}, u32[]{:S(2)}, u32[]{:S(2)}) collective-permute-start(bf16[2,96,64]{2,1,0:T(8,128)(2,1)} %get-tuple-element.88), channel_id=1, source_target_pairs={{128,0},{252,4},{248,8},{244,12},{240,16},{236,20},{232,24},{228,2... | collective-permute-start | bytes 73736 | tf_op jit(solution)/shard_map/ppermute | solution.py:667
  38.1 10.7 %collective-permute-start.5 = (bf16[2,96,64]{2,1,0:T(8,128)(2,1)}, bf16[2,96,64]{2,1,0:T(8,128)(2,1)}, u32[]{:S(2)}, u32[]{:S(2)}) collective-permute-start(bf16[2,96,64]{2,1,0:T(8,128)(2,1)} %get-tuple-element.87), channel_id=1, source_target_pairs={{128,252},{132,128},{136,132},{140,136},{144,140},{148,144},{152,1... | collective-permute-start | bytes 73736 | tf_op jit(solution)/shard_map/ppermute | solution.py:668
  40.9 0.9 copy-start.6
  48.7 72.4 %copy-start.5 = (bf16[192,192]{1,0:T(8,128)(2,1)S(1)}, bf16[192,192]{1,0:T(8,128)(2,1)}, u32[]{:S(2)}) copy-start(bf16[192,192]{1,0:T(8,128)(2,1)} %copy-done.4) | copy-start | bytes 221188
  48.7 72.4 %copy-start.9 = (f32[8,1024]{1,0:T(8,128)S(1)}, f32[8,1024]{1,0:T(8,128)}, u32[]{:S(2)}) copy-start(f32[8,1024]{1,0:T(8,128)} %copy-done.8) | copy-start | bytes 98308
  82.0 39.2 %all-to-all-start.1 = ((bf16[64,48,128]{2,1,0:T(8,128)(2,1)}), bf16[64,48,128]{2,1,0:T(8,128)(2,1)S(1)}, u32[]{:S(2)}, u32[]{:S(2)}) async-start(bf16[64,48,128]{2,1,0:T(8,128)(2,1)} %shard_map.96), calls=%async_computation.1 | async-start | bytes 1572864 | tf_op jit(solution)/shard_map/all_to_all | solution.py:733
  96.8 1.1 copy-start.3
  97.9 0.9 copy-start.7
  126.0 7.8 %collective-permute-start.12 = (bf16[56,1024]{1,0:T(8,128)(2,1)S(1)}, bf16[56,1024]{1,0:T(8,128)(2,1)S(1)}, u32[]{:S(2)}, u32[]{:S(2)}) collective-permute-start(bf16[56,1024]{1,0:T(8,128)(2,1)S(1)} %get-tuple-element.79), channel_id=1, source_target_pairs={{0,1},{1,0},{2,3},{3,2},{4,5},{5,4},{6,7},{7,6},{8,9},{9,8},{10,11... | collective-permute-start | bytes 344072 | tf_op jit(solution)/shard_map/ppermute | solution.py:626
  128.3 7.5 %collective-permute-start.13 = (bf16[56,1024]{1,0:T(8,128)(2,1)S(1)}, bf16[56,1024]{1,0:T(8,128)(2,1)S(1)}, u32[]{:S(2)}, u32[]{:S(2)}) collective-permute-start(bf16[56,1024]{1,0:T(8,128)(2,1)S(1)} %get-tuple-element.80), channel_id=1, source_target_pairs={{0,2},{1,3},{2,0},{3,1},{4,6},{5,7},{6,4},{7,5},{8,10},{9,11},{10,... | collective-permute-start | bytes 344072 | tf_op jit(solution)/shard_map/ppermute | solution.py:626
  128.3 7.5 %collective-permute-start.14 = (bf16[56,1024]{1,0:T(8,128)(2,1)S(1)}, bf16[56,1024]{1,0:T(8,128)(2,1)S(1)}, u32[]{:S(2)}, u32[]{:S(2)}) collective-permute-start(bf16[56,1024]{1,0:T(8,128)(2,1)S(1)} %get-tuple-element.81), channel_id=1, source_target_pairs={{0,3},{1,2},{2,1},{3,0},{4,7},{5,6},{6,5},{7,4},{8,11},{9,10},{10,... | collective-permute-start | bytes 344072 | tf_op jit(solution)/shard_map/ppermute | solution.py:626
  133.6 4.8 %collective-permute-start.6 = (bf16[56,1024]{1,0:T(8,128)(2,1)S(1)}, bf16[56,1024]{1,0:T(8,128)(2,1)S(1)}, u32[]{:S(2)}, u32[]{:S(2)}) collective-permute-start(bf16[56,1024]{1,0:T(8,128)(2,1)S(1)} %get-tuple-element.67), channel_id=1, source_target_pairs={{0,1},{1,0},{2,3},{3,2},{4,5},{5,4},{6,7},{7,6},{8,9},{9,8},{10,11... | collective-permute-start | bytes 344072 | tf_op jit(solution)/shard_map/ppermute | solution.py:626
  133.8 6.4 %collective-permute-start.7 = (bf16[56,1024]{1,0:T(8,128)(2,1)S(1)}, bf16[56,1024]{1,0:T(8,128)(2,1)S(1)}, u32[]{:S(2)}, u32[]{:S(2)}) collective-permute-start(bf16[56,1024]{1,0:T(8,128)(2,1)S(1)} %get-tuple-element.68), channel_id=1, source_target_pairs={{0,2},{1,3},{2,0},{3,1},{4,6},{5,7},{6,4},{7,5},{8,10},{9,11},{10,... | collective-permute-start | bytes 344072 | tf_op jit(solution)/shard_map/ppermute | solution.py:626
  133.8 7.8 %collective-permute-start.8 = (bf16[56,1024]{1,0:T(8,128)(2,1)S(1)}, bf16[56,1024]{1,0:T(8,128)(2,1)S(1)}, u32[]{:S(2)}, u32[]{:S(2)}) collective-permute-start(bf16[56,1024]{1,0:T(8,128)(2,1)S(1)} %get-tuple-element.69), channel_id=1, source_target_pairs={{0,3},{1,2},{2,1},{3,0},{4,7},{5,6},{6,5},{7,4},{8,11},{9,10},{10,... | collective-permute-start | bytes 344072 | tf_op jit(solution)/shard_map/ppermute | solution.py:626
  138.0 6.9 %collective-permute-start.15 = (bf16[48,1024]{1,0:T(8,128)(2,1)S(1)}, bf16[48,1024]{1,0:T(8,128)(2,1)S(1)}, u32[]{:S(2)}, u32[]{:S(2)}) collective-permute-start(bf16[48,1024]{1,0:T(8,128)(2,1)S(1)} %get-tuple-element.83), channel_id=1, source_target_pairs={{0,1},{1,0},{2,3},{3,2},{4,5},{5,4},{6,7},{7,6},{8,9},{9,8},{10,11... | collective-permute-start | bytes 294920 | tf_op jit(solution)/shard_map/ppermute | solution.py:626
  138.1 7.7 %collective-permute-start.16 = (bf16[48,1024]{1,0:T(8,128)(2,1)S(1)}, bf16[48,1024]{1,0:T(8,128)(2,1)S(1)}, u32[]{:S(2)}, u32[]{:S(2)}) collective-permute-start(bf16[48,1024]{1,0:T(8,128)(2,1)S(1)} %get-tuple-element.84), channel_id=1, source_target_pairs={{0,2},{1,3},{2,0},{3,1},{4,6},{5,7},{6,4},{7,5},{8,10},{9,11},{10,... | collective-permute-start | bytes 294920 | tf_op jit(solution)/shard_map/ppermute | solution.py:626
  138.3 7.4 %collective-permute-start.17 = (bf16[48,1024]{1,0:T(8,128)(2,1)S(1)}, bf16[48,1024]{1,0:T(8,128)(2,1)S(1)}, u32[]{:S(2)}, u32[]{:S(2)}) collective-permute-start(bf16[48,1024]{1,0:T(8,128)(2,1)S(1)} %get-tuple-element.85), channel_id=1, source_target_pairs={{0,3},{1,2},{2,1},{3,0},{4,7},{5,6},{6,5},{7,4},{8,11},{9,10},{10,... | collective-permute-start | bytes 294920 | tf_op jit(solution)/shard_map/ppermute | solution.py:626
  143.8 4.6 %collective-permute-start.10 = (bf16[48,1024]{1,0:T(8,128)(2,1)S(1)}, bf16[48,1024]{1,0:T(8,128)(2,1)S(1)}, u32[]{:S(2)}, u32[]{:S(2)}) collective-permute-start(bf16[48,1024]{1,0:T(8,128)(2,1)S(1)} %get-tuple-element.74), channel_id=1, source_target_pairs={{0,2},{1,3},{2,0},{3,1},{4,6},{5,7},{6,4},{7,5},{8,10},{9,11},{10,... | collective-permute-start | bytes 294920 | tf_op jit(solution)/shard_map/ppermute | solution.py:626
  143.9 6.5 %collective-permute-start.11 = (bf16[48,1024]{1,0:T(8,128)(2,1)S(1)}, bf16[48,1024]{1,0:T(8,128)(2,1)S(1)}, u32[]{:S(2)}, u32[]{:S(2)}) collective-permute-start(bf16[48,1024]{1,0:T(8,128)(2,1)S(1)} %get-tuple-element.75), channel_id=1, source_target_pairs={{0,3},{1,2},{2,1},{3,0},{4,7},{5,6},{6,5},{7,4},{8,11},{9,10},{10,... | collective-permute-start | bytes 294920 | tf_op jit(solution)/shard_map/ppermute | solution.py:626
  144.8 5.5 %collective-permute-start.9 = (bf16[48,1024]{1,0:T(8,128)(2,1)S(1)}, bf16[48,1024]{1,0:T(8,128)(2,1)S(1)}, u32[]{:S(2)}, u32[]{:S(2)}) collective-permute-start(bf16[48,1024]{1,0:T(8,128)(2,1)S(1)} %get-tuple-element.73), channel_id=1, source_target_pairs={{0,1},{1,0},{2,3},{3,2},{4,5},{5,4},{6,7},{7,6},{8,9},{9,8},{10,11... | collective-permute-start | bytes 294920 | tf_op jit(solution)/shard_map/ppermute | solution.py:626
  (2 other events, 1.3 us)

commit v4 on v3

--- a/solution.py
+++ b/solution.py
@@ -94,7 +94,7 @@
     out_ref[1:2, :] = jnp.sum(x * x, axis=0, keepdims=True)
 
 
-def give_kernel(flags, filter_ref, give_ref, held, ready, sems, out_sems):
+def give_kernel(flags, filter_ref, give_ref, held, sems):
     theirs = pl.multiple_of((1 - flags[0]) * HALF, HALF)
     rows = 32
     fetches = []
@@ -106,19 +106,10 @@
             )
         )
         fetches[-1].start()
-    sends = []
     for n in range(6):
         part, k = n // 3, n % 3
         fetches[n].wait()
-        ready[n] = held[n].astype(BF16)
-        sends.append(
-            pltpu.make_async_copy(
-                ready.at[n], give_ref.at[part, rows * k : rows * (k + 1), :], out_sems.at[n]
-            )
-        )
-        sends[-1].start()
-    for send in sends:
-        send.wait()
+        give_ref[part, rows * k : rows * (k + 1), :] = held[n].astype(BF16)
 
 
 def table_kernel(alpha_ref, beta_ref, w_ref):
@@ -432,16 +423,18 @@
     st[...] = st_in[...]
     for n in range(TC // 512):
         mine = slice(256 * n, 256 * (n + 1))
-        fetches[n].wait()
-        even, odd = (
-            lax.dot_general(
-                values[:, 1024 * par : 1024 * (par + 1)],
-                w_ref[mine, 1024 * par : 1024 * (par + 1)],
-                (((1,), (1,)), ((), ())),
-                preferred_element_type=F32,
+        sums = []
+        for par in range(2):
+            fetches[2 * n + par].wait()
+            sums.append(
+                lax.dot_general(
+                    values[:, 1024 * par : 1024 * (par + 1)],
+                    w_ref[mine, 1024 * par : 1024 * (par + 1)],
+                    (((1,), (1,)), ((), ())),
+                    preferred_element_type=F32,
+                )
             )
-            for par in range(2)
-        )
+        even, odd = sums
         for side, conv in enumerate((even + odd, even - odd)):
             here = slice(side * TC // 2 + 256 * n, side * TC // 2 + 256 * (n + 1))
             start = side * TOK // 2 + chunk * TC // 2 + 256 * n
@@ -473,8 +466,14 @@
     for n in range(TC // 512):
         here = slice(256 * n, 256 * (n + 1))
         there = slice(chunk * TC // 2 + 256 * n, chunk * TC // 2 + 256 * (n + 1))
-        fetches.append(pltpu.make_async_copy(w_hbm.at[there, :], w_ref.at[here, :], sems.at[n]))
-        fetches[-1].start()
+        for par in range(2):
+            cols = slice(1024 * par, 1024 * (par + 1))
+            fetches.append(
+                pltpu.make_async_copy(
+                    w_hbm.at[there, cols], w_ref.at[here, cols], sems.at[2 * n + par]
+                )
+            )
+            fetches[-1].start()
     return fetches
 
 
@@ -645,12 +644,8 @@
     flags = jnp.stack([high, first, lane_of, place]).astype(jnp.int32)
     mine = jnp.where(high, HALF, 0)
     give = call(
-        give_kernel, pltpu.HBM((2, HALF, TOK), BF16), "sh",
-        scratch=[
-            pltpu.VMEM((6, 32, TOK), F32), pltpu.VMEM((6, 32, TOK), BF16),
-            pltpu.SemaphoreType.DMA((6,)), pltpu.SemaphoreType.DMA((6,)),
-        ],
-        outs="h",
+        give_kernel, shape((2, HALF, TOK), BF16), "sh",
+        scratch=[pltpu.VMEM((6, 32, TOK), F32), pltpu.SemaphoreType.DMA((6,))],
     )(flags, in_hbm(filter_spectrum))
     got = lax.ppermute(give, "seq", [(i, 63 - i) for i in range(64)])
     sums = call(sums_kernel, shape((2, TOK), F32), "v")(tokens)
@@ -737,7 +732,7 @@
         pltpu.VMEM((CH, TC), F32),
         pltpu.VMEM((8, TC), F32),
         pltpu.VMEM((TC // 2, TOK), BF16),
-        pltpu.SemaphoreType.DMA((TC // 512,)),
+        pltpu.SemaphoreType.DMA((TC // 256,)),
     ]
     rest = (in_hbm(kept), tokens, normed, skip_col, gain_col, st_in, mix_in_t)
     values, res_a, *first_a = call(

time: 153 us -> 154 us (level)
  local copies, waits for them, and re-layouts: 7.57 us -> 9.91 us
  waiting for transfers between devices: 46.5 us -> 44.7 us
    unnamed x28 -> x36, local copies, waits for them, and re-layouts: 5.3 us -> 7.63 us
    all_to_all x1, waiting for transfers between devices: 2.68 us -> 1.08 us  [block(): moved = lax.all_to_all(send, 'seq', split_axis=0, concat_axis=0, tiled=True)]
where the time goes in v4:
time: 154 us
  starting transfers between devices  53.8 us (35%)
  waiting for transfers between devices  44.7 us (29%)
  Pallas kernels  43.3 us (28%)
  local copies, waits for them, and re-layouts  9.91 us (6%)
    ppermute x1, waiting for transfers between devices, block(): got = lax.ppermute(give, 'seq', [(i, 63 - i) for i in range(64)])  25.8 us
    ppermute x15, starting transfers between devices, swap(): return lax.ppermute(x, 'chan', [(i, i ^ k) for i in range(4)])  15.8 us
    all_to_all x1, starting transfers between devices, block(): home = lax.all_to_all(back, 'seq', split_axis=0, concat_axis=0, tiled=True)  15 us
    all_to_all x1, starting transfers between devices, block(): moved = lax.all_to_all(send, 'seq', split_axis=0, concat_axis=0, tiled=True)  12.8 us
    all_to_all x1, waiting for transfers between devices, block(): home = lax.all_to_all(back, 'seq', split_axis=0, concat_axis=0, tiled=True)  12.7 us
    pallas_call x1, Pallas kernels, block(): call(down_kernel, (shape((CH, HID), BF16), shape((CH, CH), BF16)), 'vv',...  9.64 us
    ppermute x1, starting transfers between devices, block(): got = lax.ppermute(give, 'seq', [(i, 63 - i) for i in range(64)])  7.67 us
    unnamed x36, local copies, waits for them, and re-layouts  7.63 us
  transfers between devices with their start and end apart: 20, of which 6 were waited for; matrix products, arithmetic and copies ran while one was open for 3% of the time, Pallas kernels for 17%

profile of v4, /device:TPU:1, one launch (start us, length us, event | category | flops | bytes accessed | tf_op | source)
XLA Modules:
  0.0 153.7 jit_solution(8022796246027777605)
XLA Ops:
  0.0 1.1 copy-done
  1.3 3.3 %collective-permute-start = (f32[2,2048]{1,0:T(2,128)S(1)}, f32[2,2048]{1,0:T(2,128)S(1)}, u32[]{:S(2)}, u32[]{:S(2)}) collective-permute-start(f32[2,2048]{1,0:T(2,128)S(1)} %shard_map.91.s0), channel_id=1, source_target_pairs={{0,1},{1,0},{2,3},{3,2},{4,5},{5,4},{6,7},{7,6},{8,9},{9,8},{10,11... | collective-permute-start | bytes 49160 | tf_op jit(solution)/shard_map/ppermute | solution.py:625
  4.6 1.7 %collective-permute-start.2 = (f32[2,2048]{1,0:T(2,128)S(1)}, f32[2,2048]{1,0:T(2,128)S(1)}, u32[]{:S(2)}, u32[]{:S(2)}) collective-permute-start(f32[2,2048]{1,0:T(2,128)S(1)} %shard_map.91.s0), channel_id=1, source_target_pairs={{0,3},{1,2},{2,1},{3,0},{4,7},{5,6},{6,5},{7,4},{8,11},{9,10},{10,... | collective-permute-start | bytes 49160 | tf_op jit(solution)/shard_map/ppermute | solution.py:625
  7.3 1.5 shard_map.92.w_ref
  8.8 2.9 %shard_map.93 = (bf16[64,48,128]{2,1,0:T(8,128)(2,1)}, bf16[192,2048]{1,0:T(8,128)(2,1)S(1)}, bf16[1024,2048]{1,0:T(8,128)(2,1)}) custom-call(bf16[192,2048]{1,0:T(8,128)(2,1)S(1)} %copy-done.1, f32[2,2048]{1,0:T(2,128)S(1)} %shard_map.91.s0, f32[2,2048]{1,0:T(2,128)S(1)} %collective-permute-done.s1, f32[2,2048]{1,0:T(2,128)S(1)} %collective-permute-done.1.s2, ...), custom_call_target="tpu_custom_call" | custom-call | tf_op jit(solution)/shard_map/pallas_call | solution.py:679
  11.7 12.8 %all-to-all-start = ((bf16[64,48,128]{2,1,0:T(8,128)(2,1)}), bf16[64,48,128]{2,1,0:T(8,128)(2,1)}, u32[]{:S(2)}, u32[]{:S(2)}) async-start(bf16[64,48,128]{2,1,0:T(8,128)(2,1)} %get-tuple-element.46), calls=%async_computation | async-start | bytes 1572864 | tf_op jit(solution)/shard_map/all_to_all | solution.py:691
  24.6 2.3 %shard_map.95 = bf16[2,96,2048]{2,1,0:T(8,128)(2,1)S(1)} custom-call(s32[4]{0:T(128)S(1)} %pad_add_fusion.flags, f32[2,192,2048]{2,1,0:T(8,128)} %filter_ref.1), custom_call_target="tpu_custom_call" | custom-call | tf_op jit(solution)/shard_map/pallas_call | solution.py:646
  26.9 7.7 %collective-permute-start.3 = (bf16[2,96,2048]{2,1,0:T(8,128)(2,1)S(1)}, bf16[2,96,2048]{2,1,0:T(8,128)(2,1)}, u32[]{:S(2)}, u32[]{:S(2)}) collective-permute-start(bf16[2,96,2048]{2,1,0:T(8,128)(2,1)S(1)} %shard_map.95), channel_id=1, source_target_pairs={{0,252},{4,248},{8,244},{12,240},{16,236},{20,232},{24,228},{28,22... | collective-permute-start | bytes 2359304 | tf_op jit(solution)/shard_map/ppermute | solution.py:650
  36.0 1.3 collective-permute-start.4
  37.3 1.3 collective-permute-start.5
  38.6 1.5 dynamic-slice_convert_fusion.own_ref
  40.1 1.1 copy-done.2
  42.1 3.0 %shard_map.94 = (f32[192,1]{1,0:T(8,128)S(1)}, f32[192,1]{1,0:T(8,128)S(1)}, f32[8,1024]{1,0:T(8,128)S(1)}, bf16[192,192]{1,0:T(8,128)(2,1)S(1)}, bf16[768,192]{1,0:T(8,128)(2,1)S(1)}) custom-call(f32[1,192]{1,0:T(1,128)S(1)} %bitcast.11, f32[1,192]{1,0:T(1,128)S(1)} %bitcast.12, bf16[1,36864]{1,0:T(2,128)(2,1)S(1)} %copy-done.10, ...), custom_call_target="tpu_custom_call" | custom-call | tf_op jit(solution)/shard_map/pallas_call | solution.py:692
  47.6 1.1 all-to-all-done.moved
  48.7 25.8 %collective-permute-done.3.got = bf16[2,96,2048]{2,1,0:T(8,128)(2,1)} collective-permute-done((bf16[2,96,2048]{2,1,0:T(8,128)(2,1)S(1)}, bf16[2,96,2048]{2,1,0:T(8,128)(2,1)}, u32[]{:S(2)}, u32[]{:S(2)}) %collective-permute-start.3) | collective-permute-done | bytes 786464 | tf_op jit(solution)/shard_map/ppermute | solution.py:650
  74.5 7.4 %shard_map.96 = bf16[64,48,128]{2,1,0:T(8,128)(2,1)} custom-call(s32[4]{0:T(128)S(1)} %pad_add_fusion.flags, bf16[64,48,128]{2,1,0:T(8,128)(2,1)} %all-to-all-done.moved, bf16[2,96,2048]{2,1,0:T(8,128)(2,1)S(1)} %dynamic-slice_convert_fusion.own_ref, bf16[2,96,2048]{2,1,0:T(8,128)(2,1)} %collective-permute-done.3.got, ...), custom_call_target="tpu_custom_call" | custom-call | tf_op jit(solution)/shard_map/pallas_call | solution.py:704
  81.9 15.0 %all-to-all-start.1 = ((bf16[64,48,128]{2,1,0:T(8,128)(2,1)}), bf16[64,48,128]{2,1,0:T(8,128)(2,1)S(1)}, u32[]{:S(2)}, u32[]{:S(2)}) async-start(bf16[64,48,128]{2,1,0:T(8,128)(2,1)} %shard_map.96), calls=%async_computation.1 | async-start | bytes 1572864 | tf_op jit(solution)/shard_map/all_to_all | solution.py:728
  96.9 1.1 copy-done.3
  98.9 9.6 %shard_map.97 = (bf16[192,768]{1,0:T(8,128)(2,1)S(1)}, bf16[192,192]{1,0:T(8,128)(2,1)S(1)}) custom-call(bf16[1,147456]{1,0:T(2,128)(2,1)S(1)} %copy-done.3, bf16[1,36864]{1,0:T(2,128)(2,1)S(1)} %copy-done.11), custom_call_target="tpu_custom_call" | custom-call | tf_op jit(solution)/shard_map/pallas_call | solution.py:722
  108.5 12.7 %all-to-all-done.1.got_ref = bf16[64,48,128]{2,1,0:T(8,128)(2,1)S(1)} async-done(((bf16[64,48,128]{2,1,0:T(8,128)(2,1)}), bf16[64,48,128]{2,1,0:T(8,128)(2,1)S(1)}, u32[]{:S(2)}, u32[]{:S(2)}) %all-to-all-start.1) | async-done | bytes 786464 | tf_op jit(solution)/shard_map/all_to_all | solution.py:728
  121.2 5.4 %shard_map.98 = (bf16[192,2048]{1,0:T(8,128)(2,1)S(1)}, bf16[192,1024]{1,0:T(8,128)(2,1)S(1)}, bf16[56,1024]{1,0:T(8,128)(2,1)S(1)}, bf16[56,1024]{1,0:T(8,128)(...) custom-call(s32[4]{0:T(128)S(1)} %pad_add_fusion.flags, ...), custom_call_target="tpu_custom_call" | custom-call | tf_op jit(solution)/shard_map/pallas_call | solution.py:738
  126.6 2.6 %collective-permute-start.12 = (bf16[56,1024]{1,0:T(8,128)(2,1)S(1)}, bf16[56,1024]{1,0:T(8,128)(2,1)S(1)}, u32[]{:S(2)}, u32[]{:S(2)}) collective-permute-start(bf16[56,1024]{1,0:T(8,128)(2,1)S(1)} %get-tuple-element.79), channel_id=1, source_target_pairs={{0,1},{1,0},{2,3},{3,2},{4,5},{5,4},{6,7},{7,6},{8,9},{9,8},{10,11... | collective-permute-start | bytes 344072 | tf_op jit(solution)/shard_map/ppermute | solution.py:625
  129.3 1.7 %collective-permute-start.14 = (bf16[56,1024]{1,0:T(8,128)(2,1)S(1)}, bf16[56,1024]{1,0:T(8,128)(2,1)S(1)}, u32[]{:S(2)}, u32[]{:S(2)}) collective-permute-start(bf16[56,1024]{1,0:T(8,128)(2,1)S(1)} %get-tuple-element.81), channel_id=1, source_target_pairs={{0,3},{1,2},{2,1},{3,0},{4,7},{5,6},{6,5},{7,4},{8,11},{9,10},{10,... | collective-permute-start | bytes 344072 | tf_op jit(solution)/shard_map/ppermute | solution.py:625
  131.0 4.1 %shard_map.99 = (bf16[192,1024]{1,0:T(8,128)(2,1)S(1)}, bf16[56,1024]{1,0:T(8,128)(2,1)S(1)}, bf16[56,1024]{1,0:T(8,128)(2,1)S(1)}, bf16[56,1024]{1,0:T(8,128)(2,1)S(1)}, bf16[56,1024]{1,0:T(8,128)(2,1)S(1)}) custom-call(s32[4]{0:T(128)S(1)} %pad_add_fusion.flags, bf16[192,2048]{1,0:T(8,128)(2,1)S(1)} %get-tuple-element.65.values_ref, ...), custom_call_target="tpu_custom_call" | custom-call | tf_op jit(solution)/shard_map/pallas_call | solution.py:743
  135.3 2.0 %collective-permute-start.8 = (bf16[56,1024]{1,0:T(8,128)(2,1)S(1)}, bf16[56,1024]{1,0:T(8,128)(2,1)S(1)}, u32[]{:S(2)}, u32[]{:S(2)}) collective-permute-start(bf16[56,1024]{1,0:T(8,128)(2,1)S(1)} %get-tuple-element.69), channel_id=1, source_target_pairs={{0,3},{1,2},{2,1},{3,0},{4,7},{5,6},{6,5},{7,4},{8,11},{9,10},{10,... | collective-permute-start | bytes 344072 | tf_op jit(solution)/shard_map/ppermute | solution.py:625
  137.3 2.2 %shard_map.101 = (bf16[48,1024]{1,0:T(8,128)(2,1)S(1)}, bf16[48,1024]{1,0:T(8,128)(2,1)S(1)}, bf16[48,1024]{1,0:T(8,128)(2,1)S(1)}, bf16[48,1024]{1,0:T(8,128)(2,1)S(1)}) custom-call(s32[4]{0:T(128)S(1)} %pad_add_fusion.flags, bf16[56,1024]{1,0:T(8,128)(2,1)S(1)} %get-tuple-element.78.p0, bf16[56,1024]{1,0:T(8,128)(2,1)S(1)} %collective-permute-done.12.p1, ...), custom_call_target="tpu_custom_call" | custom-call | tf_op jit(solution)/shard_map/pallas_call | solution.py:749
  139.7 2.0 %collective-permute-start.17 = (bf16[48,1024]{1,0:T(8,128)(2,1)S(1)}, bf16[48,1024]{1,0:T(8,128)(2,1)S(1)}, u32[]{:S(2)}, u32[]{:S(2)}) collective-permute-start(bf16[48,1024]{1,0:T(8,128)(2,1)S(1)} %get-tuple-element.85), channel_id=1, source_target_pairs={{0,3},{1,2},{2,1},{3,0},{4,7},{5,6},{6,5},{7,4},{8,11},{9,10},{10,... | collective-permute-start | bytes 294920 | tf_op jit(solution)/shard_map/ppermute | solution.py:625
  141.8 1.4 collective-permute-done.8.p3
  143.2 2.2 %shard_map.100 = (bf16[48,1024]{1,0:T(8,128)(2,1)S(1)}, bf16[48,1024]{1,0:T(8,128)(2,1)S(1)}, bf16[48,1024]{1,0:T(8,128)(2,1)S(1)}, bf16[48,1024]{1,0:T(8,128)(2,1)S(1)}) custom-call(s32[4]{0:T(128)S(1)} %pad_add_fusion.flags, bf16[56,1024]{1,0:T(8,128)(2,1)S(1)} %get-tuple-element.66.p0, bf16[56,1024]{1,0:T(8,128)(2,1)S(1)} %collective-permute-done.6.p1, ...), custom_call_target="tpu_custom_call" | custom-call | tf_op jit(solution)/shard_map/pallas_call | solution.py:749
  148.2 1.8 %collective-permute-done.10.p2 = bf16[48,1024]{1,0:T(8,128)(2,1)S(1)} collective-permute-done((bf16[48,1024]{1,0:T(8,128)(2,1)S(1)}, bf16[48,1024]{1,0:T(8,128)(2,1)S(1)}, u32[]{:S(2)}, u32[]{:S(2)}) %collective-permute-start.10) | collective-permute-done | bytes 98336 | tf_op jit(solution)/shard_map/ppermute | solution.py:625
  150.0 2.0 %collective-permute-done.11.p3 = bf16[48,1024]{1,0:T(8,128)(2,1)S(1)} collective-permute-done((bf16[48,1024]{1,0:T(8,128)(2,1)S(1)}, bf16[48,1024]{1,0:T(8,128)(2,1)S(1)}, u32[]{:S(2)}, u32[]{:S(2)}) %collective-permute-start.11) | collective-permute-done | bytes 98336 | tf_op jit(solution)/shard_map/ppermute | solution.py:625
  151.9 1.7 %shard_map.103 = bf16[192,2048]{1,0:T(8,128)(2,1)} custom-call(s32[4]{0:T(128)S(1)} %pad_add_fusion.flags, bf16[48,1024]{1,0:T(8,128)(2,1)S(1)} %get-tuple-element.72.p0, bf16[48,1024]{1,0:T(8,128)(2,1)S(1)} %collective-permute-done.9.p1, bf16[48,1024]{1,0:T(8,128)(2,1)S(1)} %collective-permute-done.10.p2, bf16[48,1024]{1,0:T(8,128)(2,1)S(1)} %collective-permute-done.11.p3, ...), custom_call_target="tpu_custom_call" | custom-call | tf_op jit(solution)/shard_map/pallas_call | solution.py:762
  (73 shorter events, 10.2 us)
Async XLA Ops:
  0.0 1.1 copy-start
  1.1 7.7 %copy-start.1 = (bf16[192,2048]{1,0:T(8,128)(2,1)S(1)}, bf16[192,2048]{1,0:T(8,128)(2,1)}, u32[]{:S(2)}) copy-start(bf16[192,2048]{1,0:T(8,128)(2,1)} %x_ref.7) | copy-start | bytes 2359300
  1.1 7.7 %copy-start.16 = (f32[192]{0:T(256)S(1)}, f32[192]{0:T(256)}, u32[]{:S(2)}) copy-start(f32[192]{0:T(256)} %param.12) | copy-start | bytes 2308
  1.3 7.5 %collective-permute-start = (f32[2,2048]{1,0:T(2,128)S(1)}, f32[2,2048]{1,0:T(2,128)S(1)}, u32[]{:S(2)}, u32[]{:S(2)}) collective-permute-start(f32[2,2048]{1,0:T(2,128)S(1)} %shard_map.91.s0), channel_id=1, source_target_pairs={{0,1},{1,0},{2,3},{3,2},{4,5},{5,4},{6,7},{7,6},{8,9},{9,8},{10,11... | collective-permute-start | bytes 49160 | tf_op jit(solution)/shard_map/ppermute | solution.py:625
  4.6 4.2 %collective-permute-start.1 = (f32[2,2048]{1,0:T(2,128)S(1)}, f32[2,2048]{1,0:T(2,128)S(1)}, u32[]{:S(2)}, u32[]{:S(2)}) collective-permute-start(f32[2,2048]{1,0:T(2,128)S(1)} %shard_map.91.s0), channel_id=1, source_target_pairs={{0,2},{1,3},{2,0},{3,1},{4,6},{5,7},{6,4},{7,5},{8,10},{9,11},{10,... | collective-permute-start | bytes 49160 | tf_op jit(solution)/shard_map/ppermute | solution.py:625
  4.6 4.2 %collective-permute-start.2 = (f32[2,2048]{1,0:T(2,128)S(1)}, f32[2,2048]{1,0:T(2,128)S(1)}, u32[]{:S(2)}, u32[]{:S(2)}) collective-permute-start(f32[2,2048]{1,0:T(2,128)S(1)} %shard_map.91.s0), channel_id=1, source_target_pairs={{0,3},{1,2},{2,1},{3,0},{4,7},{5,6},{6,5},{7,4},{8,11},{9,10},{10,... | collective-permute-start | bytes 49160 | tf_op jit(solution)/shard_map/ppermute | solution.py:625
  11.7 37.0 %all-to-all-start = ((bf16[64,48,128]{2,1,0:T(8,128)(2,1)}), bf16[64,48,128]{2,1,0:T(8,128)(2,1)}, u32[]{:S(2)}, u32[]{:S(2)}) async-start(bf16[64,48,128]{2,1,0:T(8,128)(2,1)} %get-tuple-element.46), calls=%async_computation | async-start | bytes 1572864 | tf_op jit(solution)/shard_map/all_to_all | solution.py:691
  24.5 10.1 %copy-start.17 = (f32[2,192,2048]{2,1,0:T(8,128)S(1)}, f32[2,192,2048]{2,1,0:T(8,128)}, u32[]{:S(2)}) copy-start(f32[2,192,2048]{2,1,0:T(8,128)} %filter_ref.1) | copy-start | bytes 9437188
  26.9 13.2 %copy-start.14 = (f32[192]{0:T(256)S(1)}, f32[192]{0:T(256)}, u32[]{:S(2)}) copy-start(f32[192]{0:T(256)} %param.11) | copy-start | bytes 2308
  26.9 13.2 %copy-start.15 = (f32[192]{0:T(256)S(1)}, f32[192]{0:T(256)}, u32[]{:S(2)}) copy-start(f32[192]{0:T(256)} %param.13) | copy-start | bytes 2308
  26.9 47.6 %collective-permute-start.3 = (bf16[2,96,2048]{2,1,0:T(8,128)(2,1)S(1)}, bf16[2,96,2048]{2,1,0:T(8,128)(2,1)}, u32[]{:S(2)}, u32[]{:S(2)}) collective-permute-start(bf16[2,96,2048]{2,1,0:T(8,128)(2,1)S(1)} %shard_map.95), channel_id=1, source_target_pairs={{0,252},{4,248},{8,244},{12,240},{16,236},{20,232},{24,228},{28,22... | collective-permute-start | bytes 2359304 | tf_op jit(solution)/shard_map/ppermute | solution.py:650
  36.0 12.7 %collective-permute-start.4 = (bf16[2,96,64]{2,1,0:T(8,128)(2,1)}, bf16[2,96,64]{2,1,0:T(8,128)(2,1)}, u32[]{:S(2)}, u32[]{:S(2)}) collective-permute-start(bf16[2,96,64]{2,1,0:T(8,128)(2,1)} %get-tuple-element.88), channel_id=1, source_target_pairs={{128,0},{252,4},{248,8},{244,12},{240,16},{236,20},{232,24},{228,2... | collective-permute-start | bytes 73736 | tf_op jit(solution)/shard_map/ppermute | solution.py:662
  37.3 11.4 %collective-permute-start.5 = (bf16[2,96,64]{2,1,0:T(8,128)(2,1)}, bf16[2,96,64]{2,1,0:T(8,128)(2,1)}, u32[]{:S(2)}, u32[]{:S(2)}) collective-permute-start(bf16[2,96,64]{2,1,0:T(8,128)(2,1)} %get-tuple-element.87), channel_id=1, source_target_pairs={{128,252},{132,128},{136,132},{140,136},{144,140},{148,144},{152,1... | collective-permute-start | bytes 73736 | tf_op jit(solution)/shard_map/ppermute | solution.py:663
  40.1 1.1 copy-start.2
  74.5 46.7 %copy-start.5 = (f32[192,1]{1,0:T(8,128)S(1)}, f32[192,1]{1,0:T(8,128)}, u32[]{:S(2)}) copy-start(f32[192,1]{1,0:T(8,128)} %copy-done.4) | copy-start | bytes 2308
  74.5 46.7 %copy-start.7 = (f32[192,1]{1,0:T(8,128)S(1)}, f32[192,1]{1,0:T(8,128)}, u32[]{:S(2)}) copy-start(f32[192,1]{1,0:T(8,128)} %copy-done.6) | copy-start | bytes 2308
  74.5 46.7 %copy-start.9 = (bf16[192,192]{1,0:T(8,128)(2,1)S(1)}, bf16[192,192]{1,0:T(8,128)(2,1)}, u32[]{:S(2)}) copy-start(bf16[192,192]{1,0:T(8,128)(2,1)} %copy-done.8) | copy-start | bytes 221188
  74.5 46.7 %copy-start.13 = (f32[8,1024]{1,0:T(8,128)S(1)}, f32[8,1024]{1,0:T(8,128)}, u32[]{:S(2)}) copy-start(f32[8,1024]{1,0:T(8,128)} %copy-done.12) | copy-start | bytes 98308
  81.9 39.3 %all-to-all-start.1 = ((bf16[64,48,128]{2,1,0:T(8,128)(2,1)}), bf16[64,48,128]{2,1,0:T(8,128)(2,1)S(1)}, u32[]{:S(2)}, u32[]{:S(2)}) async-start(bf16[64,48,128]{2,1,0:T(8,128)(2,1)} %shard_map.96), calls=%async_computation.1 | async-start | bytes 1572864 | tf_op jit(solution)/shard_map/all_to_all | solution.py:728
  96.9 1.1 copy-start.3
  126.6 8.7 %collective-permute-start.12 = (bf16[56,1024]{1,0:T(8,128)(2,1)S(1)}, bf16[56,1024]{1,0:T(8,128)(2,1)S(1)}, u32[]{:S(2)}, u32[]{:S(2)}) collective-permute-start(bf16[56,1024]{1,0:T(8,128)(2,1)S(1)} %get-tuple-element.79), channel_id=1, source_target_pairs={{0,1},{1,0},{2,3},{3,2},{4,5},{5,4},{6,7},{7,6},{8,9},{9,8},{10,11... | collective-permute-start | bytes 344072 | tf_op jit(solution)/shard_map/ppermute | solution.py:625
  129.3 8.1 %collective-permute-start.13 = (bf16[56,1024]{1,0:T(8,128)(2,1)S(1)}, bf16[56,1024]{1,0:T(8,128)(2,1)S(1)}, u32[]{:S(2)}, u32[]{:S(2)}) collective-permute-start(bf16[56,1024]{1,0:T(8,128)(2,1)S(1)} %get-tuple-element.80), channel_id=1, source_target_pairs={{0,2},{1,3},{2,0},{3,1},{4,6},{5,7},{6,4},{7,5},{8,10},{9,11},{10,... | collective-permute-start | bytes 344072 | tf_op jit(solution)/shard_map/ppermute | solution.py:625
  129.3 8.1 %collective-permute-start.14 = (bf16[56,1024]{1,0:T(8,128)(2,1)S(1)}, bf16[56,1024]{1,0:T(8,128)(2,1)S(1)}, u32[]{:S(2)}, u32[]{:S(2)}) collective-permute-start(bf16[56,1024]{1,0:T(8,128)(2,1)S(1)} %get-tuple-element.81), channel_id=1, source_target_pairs={{0,3},{1,2},{2,1},{3,0},{4,7},{5,6},{6,5},{7,4},{8,11},{9,10},{10,... | collective-permute-start | bytes 344072 | tf_op jit(solution)/shard_map/ppermute | solution.py:625
  135.1 4.6 %collective-permute-start.6 = (bf16[56,1024]{1,0:T(8,128)(2,1)S(1)}, bf16[56,1024]{1,0:T(8,128)(2,1)S(1)}, u32[]{:S(2)}, u32[]{:S(2)}) collective-permute-start(bf16[56,1024]{1,0:T(8,128)(2,1)S(1)} %get-tuple-element.67), channel_id=1, source_target_pairs={{0,1},{1,0},{2,3},{3,2},{4,5},{5,4},{6,7},{7,6},{8,9},{9,8},{10,11... | collective-permute-start | bytes 344072 | tf_op jit(solution)/shard_map/ppermute | solution.py:625
  135.3 6.4 %collective-permute-start.7 = (bf16[56,1024]{1,0:T(8,128)(2,1)S(1)}, bf16[56,1024]{1,0:T(8,128)(2,1)S(1)}, u32[]{:S(2)}, u32[]{:S(2)}) collective-permute-start(bf16[56,1024]{1,0:T(8,128)(2,1)S(1)} %get-tuple-element.68), channel_id=1, source_target_pairs={{0,2},{1,3},{2,0},{3,1},{4,6},{5,7},{6,4},{7,5},{8,10},{9,11},{10,... | collective-permute-start | bytes 344072 | tf_op jit(solution)/shard_map/ppermute | solution.py:625
  135.3 7.8 %collective-permute-start.8 = (bf16[56,1024]{1,0:T(8,128)(2,1)S(1)}, bf16[56,1024]{1,0:T(8,128)(2,1)S(1)}, u32[]{:S(2)}, u32[]{:S(2)}) collective-permute-start(bf16[56,1024]{1,0:T(8,128)(2,1)S(1)} %get-tuple-element.69), channel_id=1, source_target_pairs={{0,3},{1,2},{2,1},{3,0},{4,7},{5,6},{6,5},{7,4},{8,11},{9,10},{10,... | collective-permute-start | bytes 344072 | tf_op jit(solution)/shard_map/ppermute | solution.py:625
  139.5 6.9 %collective-permute-start.15 = (bf16[48,1024]{1,0:T(8,128)(2,1)S(1)}, bf16[48,1024]{1,0:T(8,128)(2,1)S(1)}, u32[]{:S(2)}, u32[]{:S(2)}) collective-permute-start(bf16[48,1024]{1,0:T(8,128)(2,1)S(1)} %get-tuple-element.83), channel_id=1, source_target_pairs={{0,1},{1,0},{2,3},{3,2},{4,5},{5,4},{6,7},{7,6},{8,9},{9,8},{10,11... | collective-permute-start | bytes 294920 | tf_op jit(solution)/shard_map/ppermute | solution.py:625
  139.6 7.7 %collective-permute-start.16 = (bf16[48,1024]{1,0:T(8,128)(2,1)S(1)}, bf16[48,1024]{1,0:T(8,128)(2,1)S(1)}, u32[]{:S(2)}, u32[]{:S(2)}) collective-permute-start(bf16[48,1024]{1,0:T(8,128)(2,1)S(1)} %get-tuple-element.84), channel_id=1, source_target_pairs={{0,2},{1,3},{2,0},{3,1},{4,6},{5,7},{6,4},{7,5},{8,10},{9,11},{10,... | collective-permute-start | bytes 294920 | tf_op jit(solution)/shard_map/ppermute | solution.py:625
  139.7 7.6 %collective-permute-start.17 = (bf16[48,1024]{1,0:T(8,128)(2,1)S(1)}, bf16[48,1024]{1,0:T(8,128)(2,1)S(1)}, u32[]{:S(2)}, u32[]{:S(2)}) collective-permute-start(bf16[48,1024]{1,0:T(8,128)(2,1)S(1)} %get-tuple-element.85), channel_id=1, source_target_pairs={{0,3},{1,2},{2,1},{3,0},{4,7},{5,6},{6,5},{7,4},{8,11},{9,10},{10,... | collective-permute-start | bytes 294920 | tf_op jit(solution)/shard_map/ppermute | solution.py:625
  145.4 4.6 %collective-permute-start.10 = (bf16[48,1024]{1,0:T(8,128)(2,1)S(1)}, bf16[48,1024]{1,0:T(8,128)(2,1)S(1)}, u32[]{:S(2)}, u32[]{:S(2)}) collective-permute-start(bf16[48,1024]{1,0:T(8,128)(2,1)S(1)} %get-tuple-element.74), channel_id=1, source_target_pairs={{0,2},{1,3},{2,0},{3,1},{4,6},{5,7},{6,4},{7,5},{8,10},{9,11},{10,... | collective-permute-start | bytes 294920 | tf_op jit(solution)/shard_map/ppermute | solution.py:625
  145.5 6.5 %collective-permute-start.11 = (bf16[48,1024]{1,0:T(8,128)(2,1)S(1)}, bf16[48,1024]{1,0:T(8,128)(2,1)S(1)}, u32[]{:S(2)}, u32[]{:S(2)}) collective-permute-start(bf16[48,1024]{1,0:T(8,128)(2,1)S(1)} %get-tuple-element.75), channel_id=1, source_target_pairs={{0,3},{1,2},{2,1},{3,0},{4,7},{5,6},{6,5},{7,4},{8,11},{9,10},{10,... | collective-permute-start | bytes 294920 | tf_op jit(solution)/shard_map/ppermute | solution.py:625
  146.4 5.5 %collective-permute-start.9 = (bf16[48,1024]{1,0:T(8,128)(2,1)S(1)}, bf16[48,1024]{1,0:T(8,128)(2,1)S(1)}, u32[]{:S(2)}, u32[]{:S(2)}) collective-permute-start(bf16[48,1024]{1,0:T(8,128)(2,1)S(1)} %get-tuple-element.73), channel_id=1, source_target_pairs={{0,1},{1,0},{2,3},{3,2},{4,5},{5,4},{6,7},{7,6},{8,9},{9,8},{10,11... | collective-permute-start | bytes 294920 | tf_op jit(solution)/shard_map/ppermute | solution.py:625
  (6 other events, 4.3 us)

commit v5 on v4

--- a/solution.py
+++ b/solution.py
@@ -423,9 +423,9 @@
     st[...] = st_in[...]
     for n in range(TC // 512):
         mine = slice(256 * n, 256 * (n + 1))
+        fetches[n].wait()
         sums = []
         for par in range(2):
-            fetches[2 * n + par].wait()
             sums.append(
                 lax.dot_general(
                     values[:, 1024 * par : 1024 * (par + 1)],
@@ -466,14 +466,8 @@
     for n in range(TC // 512):
         here = slice(256 * n, 256 * (n + 1))
         there = slice(chunk * TC // 2 + 256 * n, chunk * TC // 2 + 256 * (n + 1))
-        for par in range(2):
-            cols = slice(1024 * par, 1024 * (par + 1))
-            fetches.append(
-                pltpu.make_async_copy(
-                    w_hbm.at[there, cols], w_ref.at[here, cols], sems.at[2 * n + par]
-                )
-            )
-            fetches[-1].start()
+        fetches.append(pltpu.make_async_copy(w_hbm.at[there, :], w_ref.at[here, :], sems.at[n]))
+        fetches[-1].start()
     return fetches
 
 
@@ -545,22 +539,31 @@
         o[...] = low_ref[pl.ds(pl.multiple_of((me ^ k) * PIECE, PIECE), PIECE), :].astype(BF16)
 
 
-def up_kernel(skip_row, gain_row, mix_in_ref, up_ref, skip_ref, gain_ref, st_ref, in_t, up_t, square, wide):
+def unroll(src, dst, rows, cols):
+    def step(i, carry):
+        for k in range(8):
+            row = i * 8 + k
+            start = pl.multiple_of(row * cols, 128)
+            dst[pl.ds(row, 1), :] = src[:, pl.ds(start, cols)].astype(F32)
+        return carry
+
+    lax.fori_loop(0, rows // 8, step, 0)
+
+
+def up_kernel(
+    skip_row, gain_row, mix_in_ref, up_ref, skip_ref, gain_ref, st_ref, in_t, up_t, square, wide, tall
+):
     skip_ref[...] = column_of(skip_row)
     gain_ref[...] = column_of(gain_row)
-
-    def unroll(src, dst, rows, cols):
-        def step(i, carry):
-            for k in range(8):
-                row = i * 8 + k
-                start = pl.multiple_of(row * cols, 128)
-                dst[pl.ds(row, 1), :] = src[:, pl.ds(start, cols)].astype(F32)
-            return carry
-
-        lax.fori_loop(0, rows // 8, step, 0)
-
     unroll(up_ref, wide, CH, HID)
-    up_t[...] = wide[...].T.astype(BF16)
+    turned = wide[...].T
+    tall[0] = turned[:, 0:128]
+    tall[1, :, 0 : CH - 128] = turned[:, 128:CH]
+    for par in range(2):
+        rows = slice(par * HID // 2, (par + 1) * HID // 2)
+        picked = [tall[k, pl.ds(par, HID // 2, stride=2), :] for k in range(2)]
+        up_t[rows, 0:128] = picked[0].astype(BF16)
+        up_t[rows, 128:CH] = picked[1][:, 0 : CH - 128].astype(BF16)
     paired(mix_in_ref, square, CH)
     in_t[...] = square[...].T.astype(BF16)
     st_ref[...] = jnp.zeros((8, TC), F32)
@@ -571,11 +574,15 @@
         st_ref[5 + k : 6 + k, 0:CH] = part.astype(F32)
 
 
-def down_kernel(down_ref, mix_out_ref, down_t, out_t, square, tall):
+def down_kernel(down_ref, mix_out_ref, down_t, out_t, square, pairs):
     paired(mix_out_ref, square, CH)
     out_t[...] = square[...].T.astype(BF16)
-    paired(down_ref, tall, HID)
-    down_t[...] = tall[...].T.astype(BF16)
+    unroll(down_ref, pairs, HID // 2, 2 * CH)
+    both = pairs[...]
+    for par in range(2):
+        down_t[:, par * HID // 2 : (par + 1) * HID // 2] = both[:, par * CH : (par + 1) * CH].T.astype(
+            BF16
+        )
 
 
 def paired(src, dst, rows):
@@ -696,7 +703,9 @@
             shape((HID, CH), BF16),
         ),
         "vvvv",
-        scratch=[pltpu.VMEM((CH, CH), F32), pltpu.VMEM((CH, HID), F32)],
+        scratch=[
+            pltpu.VMEM((CH, CH), F32), pltpu.VMEM((CH, HID), F32), pltpu.VMEM((2, HID, 128), F32)
+        ],
     )(skip_weight, mlp_gain, mix_in, up_weight)
     moved, skip_col, gain_col, st_in, mix_in_t, up_t = lax.optimization_barrier(
         (moved, skip_col, gain_col, st_in, mix_in_t, up_t)
@@ -723,7 +732,7 @@
         down_kernel,
         (shape((CH, HID), BF16), shape((CH, CH), BF16)),
         "vv",
-        scratch=[pltpu.VMEM((CH, CH), F32), pltpu.VMEM((HID, CH), F32)],
+        scratch=[pltpu.VMEM((CH, CH), F32), pltpu.VMEM((HID // 2, 2 * CH), F32)],
     )(down_weight, mix_out)
     home = lax.all_to_all(back, "seq", split_axis=0, concat_axis=0, tiled=True)
     home, down_t, mix_out_t = lax.optimization_barrier((home, down_t, mix_out_t))
@@ -732,7 +741,7 @@
         pltpu.VMEM((CH, TC), F32),
         pltpu.VMEM((8, TC), F32),
         pltpu.VMEM((TC // 2, TOK), BF16),
-        pltpu.SemaphoreType.DMA((TC // 256,)),
+        pltpu.SemaphoreType.DMA((TC // 512,)),
     ]
     rest = (in_hbm(kept), tokens, normed, skip_col, gain_col, st_in, mix_in_t)
     values, res_a, *first_a = call(

time: 154 us -> 153 us (level)
  Pallas kernels: 43.3 us -> 36.1 us
  waiting for transfers between devices: 44.7 us -> 50.8 us
    pallas_call x1, Pallas kernels: 9.64 us -> 3.46 us  [block(): call(down_kernel, (shape((CH, HID), BF16), shape((CH, CH), BF16)), 'vv',...]
    all_to_all x1, waiting for transfers between devices: 12.7 us -> 18.9 us  [block(): home = lax.all_to_all(back, 'seq', split_axis=0, concat_axis=0, tiled=True)]
  transfers between devices with their start and end apart: 20 -> 20, of which waited for: 6 -> 6; matrix products, arithmetic and copies ran while one was open for 3% -> 3% of each run, Pallas kernels for 17% -> 13%
where the time goes in v5:
time: 153 us; the launch traced here: 152 us
  starting transfers between devices  53.8 us (35%)
  waiting for transfers between devices  50.8 us (33%)
  Pallas kernels  36.1 us (24%)
  local copies, waits for them, and re-layouts  9.91 us (6%)
    ppermute x1, waiting for transfers between devices, block(): got = lax.ppermute(give, 'seq', [(i, 63 - i) for i in range(64)])  25.8 us
    all_to_all x1, waiting for transfers between devices, block(): home = lax.all_to_all(back, 'seq', split_axis=0, concat_axis=0, tiled=True)  18.9 us
    ppermute x15, starting transfers between devices, swap(): return lax.ppermute(x, 'chan', [(i, i ^ k) for i in range(4)])  15.8 us
    all_to_all x1, starting transfers between devices, block(): home = lax.all_to_all(back, 'seq', split_axis=0, concat_axis=0, tiled=True)  15 us
    all_to_all x1, starting transfers between devices, block(): moved = lax.all_to_all(send, 'seq', split_axis=0, concat_axis=0, tiled=True)  12.8 us
    ppermute x1, starting transfers between devices, block(): got = lax.ppermute(give, 'seq', [(i, 63 - i) for i in range(64)])  7.67 us
    unnamed x36, local copies, waits for them, and re-layouts  7.63 us
    pallas_call x1, Pallas kernels, block(): call(middle_kernel, shape((NSEQ, 2 * QUART, 128), BF16), 'shvhvv', scratc...  7.39 us
  transfers between devices with their start and end apart: 20, of which 6 were waited for; matrix products, arithmetic and copies ran while one was open for 3% of the time, Pallas kernels for 13%

profile of v5, /device:TPU:1, one launch (start us, length us, event | category | flops | bytes accessed | tf_op | source)
XLA Modules:
  0.0 152.5 jit_solution(11889316439600239613)
XLA Ops:
  0.0 1.1 copy-done
  1.3 3.3 %collective-permute-start = (f32[2,2048]{1,0:T(2,128)S(1)}, f32[2,2048]{1,0:T(2,128)S(1)}, u32[]{:S(2)}, u32[]{:S(2)}) collective-permute-start(f32[2,2048]{1,0:T(2,128)S(1)} %shard_map.91.s0), channel_id=1, source_target_pairs={{0,1},{1,0},{2,3},{3,2},{4,5},{5,4},{6,7},{7,6},{8,9},{9,8},{10,11... | collective-permute-start | bytes 49160 | tf_op jit(solution)/shard_map/ppermute | solution.py:632
  4.6 1.7 %collective-permute-start.2 = (f32[2,2048]{1,0:T(2,128)S(1)}, f32[2,2048]{1,0:T(2,128)S(1)}, u32[]{:S(2)}, u32[]{:S(2)}) collective-permute-start(f32[2,2048]{1,0:T(2,128)S(1)} %shard_map.91.s0), channel_id=1, source_target_pairs={{0,3},{1,2},{2,1},{3,0},{4,7},{5,6},{6,5},{7,4},{8,11},{9,10},{10,... | collective-permute-start | bytes 49160 | tf_op jit(solution)/shard_map/ppermute | solution.py:632
  7.3 1.5 shard_map.92.w_ref
  8.8 2.9 %shard_map.93 = (bf16[64,48,128]{2,1,0:T(8,128)(2,1)}, bf16[192,2048]{1,0:T(8,128)(2,1)S(1)}, bf16[1024,2048]{1,0:T(8,128)(2,1)}) custom-call(bf16[192,2048]{1,0:T(8,128)(2,1)S(1)} %copy-done.1, f32[2,2048]{1,0:T(2,128)S(1)} %shard_map.91.s0, f32[2,2048]{1,0:T(2,128)S(1)} %collective-permute-done.s1, f32[2,2048]{1,0:T(2,128)S(1)} %collective-permute-done.1.s2, ...), custom_call_target="tpu_custom_call" | custom-call | tf_op jit(solution)/shard_map/pallas_call | solution.py:686
  11.7 12.8 %all-to-all-start = ((bf16[64,48,128]{2,1,0:T(8,128)(2,1)}), bf16[64,48,128]{2,1,0:T(8,128)(2,1)}, u32[]{:S(2)}, u32[]{:S(2)}) async-start(bf16[64,48,128]{2,1,0:T(8,128)(2,1)} %get-tuple-element.46), calls=%async_computation | async-start | bytes 1572864 | tf_op jit(solution)/shard_map/all_to_all | solution.py:698
  24.6 2.3 %shard_map.95 = bf16[2,96,2048]{2,1,0:T(8,128)(2,1)S(1)} custom-call(s32[4]{0:T(128)S(1)} %pad_add_fusion.flags, f32[2,192,2048]{2,1,0:T(8,128)} %filter_ref.1), custom_call_target="tpu_custom_call" | custom-call | tf_op jit(solution)/shard_map/pallas_call | solution.py:653
  26.9 7.7 %collective-permute-start.3 = (bf16[2,96,2048]{2,1,0:T(8,128)(2,1)S(1)}, bf16[2,96,2048]{2,1,0:T(8,128)(2,1)}, u32[]{:S(2)}, u32[]{:S(2)}) collective-permute-start(bf16[2,96,2048]{2,1,0:T(8,128)(2,1)S(1)} %shard_map.95), channel_id=1, source_target_pairs={{0,252},{4,248},{8,244},{12,240},{16,236},{20,232},{24,228},{28,22... | collective-permute-start | bytes 2359304 | tf_op jit(solution)/shard_map/ppermute | solution.py:657
  36.0 1.3 collective-permute-start.4
  37.3 1.3 collective-permute-start.5
  38.6 1.5 dynamic-slice_convert_fusion.own_ref
  40.1 1.1 copy-done.2
  42.1 3.2 %shard_map.94 = (f32[192,1]{1,0:T(8,128)S(1)}, f32[192,1]{1,0:T(8,128)S(1)}, f32[8,1024]{1,0:T(8,128)S(1)}, bf16[192,192]{1,0:T(8,128)(2,1)S(1)}, bf16[768,192]{1,0:T(8,128)(2,1)S(1)}) custom-call(f32[1,192]{1,0:T(1,128)S(1)} %bitcast.11, f32[1,192]{1,0:T(1,128)S(1)} %bitcast.12, bf16[1,36864]{1,0:T(2,128)(2,1)S(1)} %copy-done.10, ...), custom_call_target="tpu_custom_call" | custom-call | tf_op jit(solution)/shard_map/pallas_call | solution.py:699
  48.7 25.8 %collective-permute-done.3.got = bf16[2,96,2048]{2,1,0:T(8,128)(2,1)} collective-permute-done((bf16[2,96,2048]{2,1,0:T(8,128)(2,1)S(1)}, bf16[2,96,2048]{2,1,0:T(8,128)(2,1)}, u32[]{:S(2)}, u32[]{:S(2)}) %collective-permute-start.3) | collective-permute-done | bytes 786464 | tf_op jit(solution)/shard_map/ppermute | solution.py:657
  74.5 7.4 %shard_map.96 = bf16[64,48,128]{2,1,0:T(8,128)(2,1)} custom-call(s32[4]{0:T(128)S(1)} %pad_add_fusion.flags, bf16[64,48,128]{2,1,0:T(8,128)(2,1)} %all-to-all-done.moved, bf16[2,96,2048]{2,1,0:T(8,128)(2,1)S(1)} %dynamic-slice_convert_fusion.own_ref, bf16[2,96,2048]{2,1,0:T(8,128)(2,1)} %collective-permute-done.3.got, ...), custom_call_target="tpu_custom_call" | custom-call | tf_op jit(solution)/shard_map/pallas_call | solution.py:713
  81.9 15.0 %all-to-all-start.1 = ((bf16[64,48,128]{2,1,0:T(8,128)(2,1)}), bf16[64,48,128]{2,1,0:T(8,128)(2,1)S(1)}, u32[]{:S(2)}, u32[]{:S(2)}) async-start(bf16[64,48,128]{2,1,0:T(8,128)(2,1)} %shard_map.96), calls=%async_computation.1 | async-start | bytes 1572864 | tf_op jit(solution)/shard_map/all_to_all | solution.py:737
  96.9 1.1 copy-done.3
  98.9 3.5 %shard_map.97 = (bf16[192,768]{1,0:T(8,128)(2,1)S(1)}, bf16[192,192]{1,0:T(8,128)(2,1)S(1)}) custom-call(bf16[1,147456]{1,0:T(2,128)(2,1)S(1)} %copy-done.3, bf16[1,36864]{1,0:T(2,128)(2,1)S(1)} %copy-done.11), custom_call_target="tpu_custom_call" | custom-call | tf_op jit(solution)/shard_map/pallas_call | solution.py:731
  102.3 18.9 %all-to-all-done.1.got_ref = bf16[64,48,128]{2,1,0:T(8,128)(2,1)S(1)} async-done(((bf16[64,48,128]{2,1,0:T(8,128)(2,1)}), bf16[64,48,128]{2,1,0:T(8,128)(2,1)S(1)}, u32[]{:S(2)}, u32[]{:S(2)}) %all-to-all-start.1) | async-done | bytes 786464 | tf_op jit(solution)/shard_map/all_to_all | solution.py:737
  121.2 4.8 %shard_map.98 = (bf16[192,2048]{1,0:T(8,128)(2,1)S(1)}, bf16[192,1024]{1,0:T(8,128)(2,1)S(1)}, bf16[56,1024]{1,0:T(8,128)(2,1)S(1)}, bf16[56,1024]{1,0:T(8,128)(...) custom-call(s32[4]{0:T(128)S(1)} %pad_add_fusion.flags, ...), custom_call_target="tpu_custom_call" | custom-call | tf_op jit(solution)/shard_map/pallas_call | solution.py:747
  126.0 2.6 %collective-permute-start.12 = (bf16[56,1024]{1,0:T(8,128)(2,1)S(1)}, bf16[56,1024]{1,0:T(8,128)(2,1)S(1)}, u32[]{:S(2)}, u32[]{:S(2)}) collective-permute-start(bf16[56,1024]{1,0:T(8,128)(2,1)S(1)} %get-tuple-element.79), channel_id=1, source_target_pairs={{0,1},{1,0},{2,3},{3,2},{4,5},{5,4},{6,7},{7,6},{8,9},{9,8},{10,11... | collective-permute-start | bytes 344072 | tf_op jit(solution)/shard_map/ppermute | solution.py:632
  128.7 1.7 %collective-permute-start.14 = (bf16[56,1024]{1,0:T(8,128)(2,1)S(1)}, bf16[56,1024]{1,0:T(8,128)(2,1)S(1)}, u32[]{:S(2)}, u32[]{:S(2)}) collective-permute-start(bf16[56,1024]{1,0:T(8,128)(2,1)S(1)} %get-tuple-element.81), channel_id=1, source_target_pairs={{0,3},{1,2},{2,1},{3,0},{4,7},{5,6},{6,5},{7,4},{8,11},{9,10},{10,... | collective-permute-start | bytes 344072 | tf_op jit(solution)/shard_map/ppermute | solution.py:632
  130.4 3.5 %shard_map.99 = (bf16[192,1024]{1,0:T(8,128)(2,1)S(1)}, bf16[56,1024]{1,0:T(8,128)(2,1)S(1)}, bf16[56,1024]{1,0:T(8,128)(2,1)S(1)}, bf16[56,1024]{1,0:T(8,128)(2,1)S(1)}, bf16[56,1024]{1,0:T(8,128)(2,1)S(1)}) custom-call(s32[4]{0:T(128)S(1)} %pad_add_fusion.flags, bf16[192,2048]{1,0:T(8,128)(2,1)S(1)} %get-tuple-element.65.values_ref, ...), custom_call_target="tpu_custom_call" | custom-call | tf_op jit(solution)/shard_map/pallas_call | solution.py:752
  134.1 2.0 %collective-permute-start.8 = (bf16[56,1024]{1,0:T(8,128)(2,1)S(1)}, bf16[56,1024]{1,0:T(8,128)(2,1)S(1)}, u32[]{:S(2)}, u32[]{:S(2)}) collective-permute-start(bf16[56,1024]{1,0:T(8,128)(2,1)S(1)} %get-tuple-element.69), channel_id=1, source_target_pairs={{0,3},{1,2},{2,1},{3,0},{4,7},{5,6},{6,5},{7,4},{8,11},{9,10},{10,... | collective-permute-start | bytes 344072 | tf_op jit(solution)/shard_map/ppermute | solution.py:632
  136.1 2.2 %shard_map.101 = (bf16[48,1024]{1,0:T(8,128)(2,1)S(1)}, bf16[48,1024]{1,0:T(8,128)(2,1)S(1)}, bf16[48,1024]{1,0:T(8,128)(2,1)S(1)}, bf16[48,1024]{1,0:T(8,128)(2,1)S(1)}) custom-call(s32[4]{0:T(128)S(1)} %pad_add_fusion.flags, bf16[56,1024]{1,0:T(8,128)(2,1)S(1)} %get-tuple-element.78.p0, bf16[56,1024]{1,0:T(8,128)(2,1)S(1)} %collective-permute-done.12.p1, ...), custom_call_target="tpu_custom_call" | custom-call | tf_op jit(solution)/shard_map/pallas_call | solution.py:758
  138.7 1.9 %collective-permute-start.17 = (bf16[48,1024]{1,0:T(8,128)(2,1)S(1)}, bf16[48,1024]{1,0:T(8,128)(2,1)S(1)}, u32[]{:S(2)}, u32[]{:S(2)}) collective-permute-start(bf16[48,1024]{1,0:T(8,128)(2,1)S(1)} %get-tuple-element.85), channel_id=1, source_target_pairs={{0,3},{1,2},{2,1},{3,0},{4,7},{5,6},{6,5},{7,4},{8,11},{9,10},{10,... | collective-permute-start | bytes 294920 | tf_op jit(solution)/shard_map/ppermute | solution.py:632
  140.6 1.4 collective-permute-done.8.p3
  142.0 2.2 %shard_map.100 = (bf16[48,1024]{1,0:T(8,128)(2,1)S(1)}, bf16[48,1024]{1,0:T(8,128)(2,1)S(1)}, bf16[48,1024]{1,0:T(8,128)(2,1)S(1)}, bf16[48,1024]{1,0:T(8,128)(2,1)S(1)}) custom-call(s32[4]{0:T(128)S(1)} %pad_add_fusion.flags, bf16[56,1024]{1,0:T(8,128)(2,1)S(1)} %get-tuple-element.66.p0, bf16[56,1024]{1,0:T(8,128)(2,1)S(1)} %collective-permute-done.6.p1, ...), custom_call_target="tpu_custom_call" | custom-call | tf_op jit(solution)/shard_map/pallas_call | solution.py:758
  144.3 0.9 collective-permute-start.11
  147.0 1.8 %collective-permute-done.10.p2 = bf16[48,1024]{1,0:T(8,128)(2,1)S(1)} collective-permute-done((bf16[48,1024]{1,0:T(8,128)(2,1)S(1)}, bf16[48,1024]{1,0:T(8,128)(2,1)S(1)}, u32[]{:S(2)}, u32[]{:S(2)}) %collective-permute-start.10) | collective-permute-done | bytes 98336 | tf_op jit(solution)/shard_map/ppermute | solution.py:632
  148.8 2.0 %collective-permute-done.11.p3 = bf16[48,1024]{1,0:T(8,128)(2,1)S(1)} collective-permute-done((bf16[48,1024]{1,0:T(8,128)(2,1)S(1)}, bf16[48,1024]{1,0:T(8,128)(2,1)S(1)}, u32[]{:S(2)}, u32[]{:S(2)}) %collective-permute-start.11) | collective-permute-done | bytes 98336 | tf_op jit(solution)/shard_map/ppermute | solution.py:632
  150.7 1.7 %shard_map.103 = bf16[192,2048]{1,0:T(8,128)(2,1)} custom-call(s32[4]{0:T(128)S(1)} %pad_add_fusion.flags, bf16[48,1024]{1,0:T(8,128)(2,1)S(1)} %get-tuple-element.72.p0, bf16[48,1024]{1,0:T(8,128)(2,1)S(1)} %collective-permute-done.9.p1, bf16[48,1024]{1,0:T(8,128)(2,1)S(1)} %collective-permute-done.10.p2, bf16[48,1024]{1,0:T(8,128)(2,1)S(1)} %collective-permute-done.11.p3, ...), custom_call_target="tpu_custom_call" | custom-call | tf_op jit(solution)/shard_map/pallas_call | solution.py:771
  (73 shorter events, 10.3 us)
Async XLA Ops:
  0.0 1.1 copy-start
  1.1 7.7 %copy-start.1 = (bf16[192,2048]{1,0:T(8,128)(2,1)S(1)}, bf16[192,2048]{1,0:T(8,128)(2,1)}, u32[]{:S(2)}) copy-start(bf16[192,2048]{1,0:T(8,128)(2,1)} %x_ref.7) | copy-start | bytes 2359300
  1.1 7.7 %copy-start.16 = (f32[192]{0:T(256)S(1)}, f32[192]{0:T(256)}, u32[]{:S(2)}) copy-start(f32[192]{0:T(256)} %param.12) | copy-start | bytes 2308
  1.3 7.5 %collective-permute-start = (f32[2,2048]{1,0:T(2,128)S(1)}, f32[2,2048]{1,0:T(2,128)S(1)}, u32[]{:S(2)}, u32[]{:S(2)}) collective-permute-start(f32[2,2048]{1,0:T(2,128)S(1)} %shard_map.91.s0), channel_id=1, source_target_pairs={{0,1},{1,0},{2,3},{3,2},{4,5},{5,4},{6,7},{7,6},{8,9},{9,8},{10,11... | collective-permute-start | bytes 49160 | tf_op jit(solution)/shard_map/ppermute | solution.py:632
  4.6 4.2 %collective-permute-start.1 = (f32[2,2048]{1,0:T(2,128)S(1)}, f32[2,2048]{1,0:T(2,128)S(1)}, u32[]{:S(2)}, u32[]{:S(2)}) collective-permute-start(f32[2,2048]{1,0:T(2,128)S(1)} %shard_map.91.s0), channel_id=1, source_target_pairs={{0,2},{1,3},{2,0},{3,1},{4,6},{5,7},{6,4},{7,5},{8,10},{9,11},{10,... | collective-permute-start | bytes 49160 | tf_op jit(solution)/shard_map/ppermute | solution.py:632
  4.6 4.2 %collective-permute-start.2 = (f32[2,2048]{1,0:T(2,128)S(1)}, f32[2,2048]{1,0:T(2,128)S(1)}, u32[]{:S(2)}, u32[]{:S(2)}) collective-permute-start(f32[2,2048]{1,0:T(2,128)S(1)} %shard_map.91.s0), channel_id=1, source_target_pairs={{0,3},{1,2},{2,1},{3,0},{4,7},{5,6},{6,5},{7,4},{8,11},{9,10},{10,... | collective-permute-start | bytes 49160 | tf_op jit(solution)/shard_map/ppermute | solution.py:632
  11.7 37.0 %all-to-all-start = ((bf16[64,48,128]{2,1,0:T(8,128)(2,1)}), bf16[64,48,128]{2,1,0:T(8,128)(2,1)}, u32[]{:S(2)}, u32[]{:S(2)}) async-start(bf16[64,48,128]{2,1,0:T(8,128)(2,1)} %get-tuple-element.46), calls=%async_computation | async-start | bytes 1572864 | tf_op jit(solution)/shard_map/all_to_all | solution.py:698
  24.5 10.1 %copy-start.17 = (f32[2,192,2048]{2,1,0:T(8,128)S(1)}, f32[2,192,2048]{2,1,0:T(8,128)}, u32[]{:S(2)}) copy-start(f32[2,192,2048]{2,1,0:T(8,128)} %filter_ref.1) | copy-start | bytes 9437188
  26.9 13.2 %copy-start.14 = (f32[192]{0:T(256)S(1)}, f32[192]{0:T(256)}, u32[]{:S(2)}) copy-start(f32[192]{0:T(256)} %param.11) | copy-start | bytes 2308
  26.9 13.2 %copy-start.15 = (f32[192]{0:T(256)S(1)}, f32[192]{0:T(256)}, u32[]{:S(2)}) copy-start(f32[192]{0:T(256)} %param.13) | copy-start | bytes 2308
  26.9 47.6 %collective-permute-start.3 = (bf16[2,96,2048]{2,1,0:T(8,128)(2,1)S(1)}, bf16[2,96,2048]{2,1,0:T(8,128)(2,1)}, u32[]{:S(2)}, u32[]{:S(2)}) collective-permute-start(bf16[2,96,2048]{2,1,0:T(8,128)(2,1)S(1)} %shard_map.95), channel_id=1, source_target_pairs={{0,252},{4,248},{8,244},{12,240},{16,236},{20,232},{24,228},{28,22... | collective-permute-start | bytes 2359304 | tf_op jit(solution)/shard_map/ppermute | solution.py:657
  36.0 12.7 %collective-permute-start.4 = (bf16[2,96,64]{2,1,0:T(8,128)(2,1)}, bf16[2,96,64]{2,1,0:T(8,128)(2,1)}, u32[]{:S(2)}, u32[]{:S(2)}) collective-permute-start(bf16[2,96,64]{2,1,0:T(8,128)(2,1)} %get-tuple-element.88), channel_id=1, source_target_pairs={{128,0},{252,4},{248,8},{244,12},{240,16},{236,20},{232,24},{228,2... | collective-permute-start | bytes 73736 | tf_op jit(solution)/shard_map/ppermute | solution.py:669
  37.3 11.4 %collective-permute-start.5 = (bf16[2,96,64]{2,1,0:T(8,128)(2,1)}, bf16[2,96,64]{2,1,0:T(8,128)(2,1)}, u32[]{:S(2)}, u32[]{:S(2)}) collective-permute-start(bf16[2,96,64]{2,1,0:T(8,128)(2,1)} %get-tuple-element.87), channel_id=1, source_target_pairs={{128,252},{132,128},{136,132},{140,136},{144,140},{148,144},{152,1... | collective-permute-start | bytes 73736 | tf_op jit(solution)/shard_map/ppermute | solution.py:670
  40.1 1.1 copy-start.2
  74.5 46.7 %copy-start.5 = (f32[192,1]{1,0:T(8,128)S(1)}, f32[192,1]{1,0:T(8,128)}, u32[]{:S(2)}) copy-start(f32[192,1]{1,0:T(8,128)} %copy-done.4) | copy-start | bytes 2308
  74.5 46.7 %copy-start.7 = (f32[192,1]{1,0:T(8,128)S(1)}, f32[192,1]{1,0:T(8,128)}, u32[]{:S(2)}) copy-start(f32[192,1]{1,0:T(8,128)} %copy-done.6) | copy-start | bytes 2308
  74.5 46.7 %copy-start.9 = (bf16[192,192]{1,0:T(8,128)(2,1)S(1)}, bf16[192,192]{1,0:T(8,128)(2,1)}, u32[]{:S(2)}) copy-start(bf16[192,192]{1,0:T(8,128)(2,1)} %copy-done.8) | copy-start | bytes 221188
  74.5 46.7 %copy-start.13 = (f32[8,1024]{1,0:T(8,128)S(1)}, f32[8,1024]{1,0:T(8,128)}, u32[]{:S(2)}) copy-start(f32[8,1024]{1,0:T(8,128)} %copy-done.12) | copy-start | bytes 98308
  81.9 39.3 %all-to-all-start.1 = ((bf16[64,48,128]{2,1,0:T(8,128)(2,1)}), bf16[64,48,128]{2,1,0:T(8,128)(2,1)S(1)}, u32[]{:S(2)}, u32[]{:S(2)}) async-start(bf16[64,48,128]{2,1,0:T(8,128)(2,1)} %shard_map.96), calls=%async_computation.1 | async-start | bytes 1572864 | tf_op jit(solution)/shard_map/all_to_all | solution.py:737
  96.9 1.1 copy-start.3
  126.0 8.1 %collective-permute-start.12 = (bf16[56,1024]{1,0:T(8,128)(2,1)S(1)}, bf16[56,1024]{1,0:T(8,128)(2,1)S(1)}, u32[]{:S(2)}, u32[]{:S(2)}) collective-permute-start(bf16[56,1024]{1,0:T(8,128)(2,1)S(1)} %get-tuple-element.79), channel_id=1, source_target_pairs={{0,1},{1,0},{2,3},{3,2},{4,5},{5,4},{6,7},{7,6},{8,9},{9,8},{10,11... | collective-permute-start | bytes 344072 | tf_op jit(solution)/shard_map/ppermute | solution.py:632
  128.7 7.5 %collective-permute-start.13 = (bf16[56,1024]{1,0:T(8,128)(2,1)S(1)}, bf16[56,1024]{1,0:T(8,128)(2,1)S(1)}, u32[]{:S(2)}, u32[]{:S(2)}) collective-permute-start(bf16[56,1024]{1,0:T(8,128)(2,1)S(1)} %get-tuple-element.80), channel_id=1, source_target_pairs={{0,2},{1,3},{2,0},{3,1},{4,6},{5,7},{6,4},{7,5},{8,10},{9,11},{10,... | collective-permute-start | bytes 344072 | tf_op jit(solution)/shard_map/ppermute | solution.py:632
  128.7 7.5 %collective-permute-start.14 = (bf16[56,1024]{1,0:T(8,128)(2,1)S(1)}, bf16[56,1024]{1,0:T(8,128)(2,1)S(1)}, u32[]{:S(2)}, u32[]{:S(2)}) collective-permute-start(bf16[56,1024]{1,0:T(8,128)(2,1)S(1)} %get-tuple-element.81), channel_id=1, source_target_pairs={{0,3},{1,2},{2,1},{3,0},{4,7},{5,6},{6,5},{7,4},{8,11},{9,10},{10,... | collective-permute-start | bytes 344072 | tf_op jit(solution)/shard_map/ppermute | solution.py:632
  133.9 4.8 %collective-permute-start.6 = (bf16[56,1024]{1,0:T(8,128)(2,1)S(1)}, bf16[56,1024]{1,0:T(8,128)(2,1)S(1)}, u32[]{:S(2)}, u32[]{:S(2)}) collective-permute-start(bf16[56,1024]{1,0:T(8,128)(2,1)S(1)} %get-tuple-element.67), channel_id=1, source_target_pairs={{0,1},{1,0},{2,3},{3,2},{4,5},{5,4},{6,7},{7,6},{8,9},{9,8},{10,11... | collective-permute-start | bytes 344072 | tf_op jit(solution)/shard_map/ppermute | solution.py:632
  134.1 6.4 %collective-permute-start.7 = (bf16[56,1024]{1,0:T(8,128)(2,1)S(1)}, bf16[56,1024]{1,0:T(8,128)(2,1)S(1)}, u32[]{:S(2)}, u32[]{:S(2)}) collective-permute-start(bf16[56,1024]{1,0:T(8,128)(2,1)S(1)} %get-tuple-element.68), channel_id=1, source_target_pairs={{0,2},{1,3},{2,0},{3,1},{4,6},{5,7},{6,4},{7,5},{8,10},{9,11},{10,... | collective-permute-start | bytes 344072 | tf_op jit(solution)/shard_map/ppermute | solution.py:632
  134.1 7.8 %collective-permute-start.8 = (bf16[56,1024]{1,0:T(8,128)(2,1)S(1)}, bf16[56,1024]{1,0:T(8,128)(2,1)S(1)}, u32[]{:S(2)}, u32[]{:S(2)}) collective-permute-start(bf16[56,1024]{1,0:T(8,128)(2,1)S(1)} %get-tuple-element.69), channel_id=1, source_target_pairs={{0,3},{1,2},{2,1},{3,0},{4,7},{5,6},{6,5},{7,4},{8,11},{9,10},{10,... | collective-permute-start | bytes 344072 | tf_op jit(solution)/shard_map/ppermute | solution.py:632
  138.3 6.9 %collective-permute-start.15 = (bf16[48,1024]{1,0:T(8,128)(2,1)S(1)}, bf16[48,1024]{1,0:T(8,128)(2,1)S(1)}, u32[]{:S(2)}, u32[]{:S(2)}) collective-permute-start(bf16[48,1024]{1,0:T(8,128)(2,1)S(1)} %get-tuple-element.83), channel_id=1, source_target_pairs={{0,1},{1,0},{2,3},{3,2},{4,5},{5,4},{6,7},{7,6},{8,9},{9,8},{10,11... | collective-permute-start | bytes 294920 | tf_op jit(solution)/shard_map/ppermute | solution.py:632
  138.4 7.7 %collective-permute-start.16 = (bf16[48,1024]{1,0:T(8,128)(2,1)S(1)}, bf16[48,1024]{1,0:T(8,128)(2,1)S(1)}, u32[]{:S(2)}, u32[]{:S(2)}) collective-permute-start(bf16[48,1024]{1,0:T(8,128)(2,1)S(1)} %get-tuple-element.84), channel_id=1, source_target_pairs={{0,2},{1,3},{2,0},{3,1},{4,6},{5,7},{6,4},{7,5},{8,10},{9,11},{10,... | collective-permute-start | bytes 294920 | tf_op jit(solution)/shard_map/ppermute | solution.py:632
  138.7 7.4 %collective-permute-start.17 = (bf16[48,1024]{1,0:T(8,128)(2,1)S(1)}, bf16[48,1024]{1,0:T(8,128)(2,1)S(1)}, u32[]{:S(2)}, u32[]{:S(2)}) collective-permute-start(bf16[48,1024]{1,0:T(8,128)(2,1)S(1)} %get-tuple-element.85), channel_id=1, source_target_pairs={{0,3},{1,2},{2,1},{3,0},{4,7},{5,6},{6,5},{7,4},{8,11},{9,10},{10,... | collective-permute-start | bytes 294920 | tf_op jit(solution)/shard_map/ppermute | solution.py:632
  144.2 4.6 %collective-permute-start.10 = (bf16[48,1024]{1,0:T(8,128)(2,1)S(1)}, bf16[48,1024]{1,0:T(8,128)(2,1)S(1)}, u32[]{:S(2)}, u32[]{:S(2)}) collective-permute-start(bf16[48,1024]{1,0:T(8,128)(2,1)S(1)} %get-tuple-element.74), channel_id=1, source_target_pairs={{0,2},{1,3},{2,0},{3,1},{4,6},{5,7},{6,4},{7,5},{8,10},{9,11},{10,... | collective-permute-start | bytes 294920 | tf_op jit(solution)/shard_map/ppermute | solution.py:632
  144.3 6.5 %collective-permute-start.11 = (bf16[48,1024]{1,0:T(8,128)(2,1)S(1)}, bf16[48,1024]{1,0:T(8,128)(2,1)S(1)}, u32[]{:S(2)}, u32[]{:S(2)}) collective-permute-start(bf16[48,1024]{1,0:T(8,128)(2,1)S(1)} %get-tuple-element.75), channel_id=1, source_target_pairs={{0,3},{1,2},{2,1},{3,0},{4,7},{5,6},{6,5},{7,4},{8,11},{9,10},{10,... | collective-permute-start | bytes 294920 | tf_op jit(solution)/shard_map/ppermute | solution.py:632
  145.2 5.5 %collective-permute-start.9 = (bf16[48,1024]{1,0:T(8,128)(2,1)S(1)}, bf16[48,1024]{1,0:T(8,128)(2,1)S(1)}, u32[]{:S(2)}, u32[]{:S(2)}) collective-permute-start(bf16[48,1024]{1,0:T(8,128)(2,1)S(1)} %get-tuple-element.73), channel_id=1, source_target_pairs={{0,1},{1,0},{2,3},{3,2},{4,5},{5,4},{6,7},{7,6},{8,9},{9,8},{10,11... | collective-permute-start | bytes 294920 | tf_op jit(solution)/shard_map/ppermute | solution.py:632
  (6 other events, 4.3 us)
